TPU v7x, 256 devices: a whole 4x4x8 slice. The times are simulated.
256 devices in a mesh: seq: 64 (over x, z, core), head: 4 (over y).
Axes of the slice: x: 4, y: 4, z: 8, core: 2. Of those that a mesh axis runs over, the one named last changes fastest.
Arguments:
- queries: bfloat16 [32768, 4096], P('seq', 'head'), may hold values from -120 to 120
- keys: bfloat16 [32768, 1024], P('seq', 'head'), may hold values from -4 to 4
- values: bfloat16 [32768, 1024], P('seq', 'head'), may hold values from -6 to 6
- doc_start: int32 [32768], P('seq'), may hold values from 0 to 32767, as said below
- hop_counts: int32 [64], P('seq'), may hold values from 0 to 4, as said below
- loss_mask: int32 [32768], P('seq'), may hold values from 0 to 1, as said below
Outputs:
- attention: bfloat16 [32768, 4096], P('seq', 'head')
- objective: float32 [], replicated
Inputs may be any that keep to these rules, and one draw needn't show every extreme that they name: doc_start is nondecreasing; doc_start[doc_start[i]] = doc_start[i] <= i; a document holds at most 2048 tokens, and some document holds exactly that many in every draw. hop_counts[b] = b - floor(doc_start[b * 512] / 512); the most, 4, is reached in every draw. loss_mask[0] = 1.
All inputs are finite; a program needn't handle non-finite values.
Results may differ from a plain program's by a relative error of at most 0.0035.
Values may be sent and summed in bfloat16 or wider, within the bound.
No kernel may reach another device: no remote copies, remote signals or barrier semaphores. Data moves between devices by JAX's collectives and lax.ppermute only.
A program may use at most 128 MiB of HBM per device.

v0:
```python
import functools
import math

import jax
import jax.numpy as jnp
from jax import lax
from jax.sharding import Mesh
from jax.sharding import PartitionSpec as P

QUERY_HEADS = 32
KEY_VALUE_HEADS = 8
HEAD_WIDTH = 128
HOPS = 4
SEQ = ("seq_0", "seq_1", "seq_2")
SEQ_HEAD = ("seq_0", "seq_1", "seq_2", "head")


def passed_along(shard, axis, by):
    devices = lax.axis_size(axis)
    pairs = [(i, i + by) for i in range(devices) if 0 <= i + by < devices]
    return lax.ppermute(shard, axis, pairs)


def over_axes(shard, axes):
    return functools.reduce(lax.psum, axes, shard)


def attend_block(
    carry, key_block, value_block, distance, grouped_queries, doc_start, block_index, hop_limit
):
    top_old, total_old, weighted = carry
    rows = grouped_queries.shape[0]
    scores = jnp.einsum(
        "tgqd,sgd->tgqs", grouped_queries, key_block, preferred_element_type=jnp.float32
    ) * (1.0 / math.sqrt(HEAD_WIDTH))
    key_place = (block_index - distance) * rows + jnp.arange(rows, dtype=jnp.int32)
    query_place = block_index * rows + jnp.arange(rows, dtype=jnp.int32)
    seen = (
        (key_place[None, :] >= doc_start[:, None])
        & (key_place[None, :] <= query_place[:, None])
        & (distance <= hop_limit)
    )
    seen = seen[:, None, None, :]
    masked = jnp.where(seen, scores, jnp.float32(-1e30))
    top_new = jnp.maximum(top_old, jnp.max(masked, axis=-1))
    ratio_old = jnp.exp(top_old - top_new)
    weights = jnp.where(seen, jnp.exp(masked - top_new[..., None]), jnp.float32(0.0))
    total_new = total_old * ratio_old + jnp.sum(weights, axis=-1)
    rounded = weights.astype(jnp.bfloat16)
    update = jnp.einsum("tgqs,sgd->tgqd", rounded, value_block, preferred_element_type=jnp.float32)
    return (top_new, total_new, weighted * ratio_old[..., None] + update)


def on_device(queries, keys, values, doc_start, hop_counts, loss_mask):
    rows = queries.shape[0]
    kv_heads = keys.shape[1] // HEAD_WIDTH
    group_size = QUERY_HEADS // KEY_VALUE_HEADS
    block_index = lax.axis_index(SEQ)
    hop_limit = hop_counts[0]
    grouped_queries = queries.reshape(rows, kv_heads, group_size, HEAD_WIDTH)
    carry = (
        jnp.full((rows, kv_heads, group_size), -1e30, jnp.float32),
        jnp.zeros((rows, kv_heads, group_size), jnp.float32),
        jnp.zeros((rows, kv_heads, group_size, HEAD_WIDTH), jnp.float32),
    )

    def absorb(state, key_part, value_part, distance):
        key_block = key_part.reshape(rows, kv_heads, HEAD_WIDTH)
        value_block = value_part.reshape(rows, kv_heads, HEAD_WIDTH)
        return attend_block(
            state,
            key_block,
            value_block,
            distance,
            grouped_queries,
            doc_start,
            block_index,
            hop_limit,
        )

    carry = absorb(carry, keys, values, 0)
    moving_keys, moving_values = (keys, values)
    for distance in range(1, HOPS + 1):
        moving_keys, moving_values = passed_along((moving_keys, moving_values), SEQ, 1)
        carry = absorb(carry, moving_keys, moving_values, distance)
    top_final, total_final, weighted = carry
    attended = (weighted / total_final[..., None]).reshape(rows, kv_heads * group_size * HEAD_WIDTH)
    attention = attended.astype(jnp.bfloat16)
    marks = loss_mask.astype(jnp.float32)
    local_squares = jnp.sum(marks[:, None] * attended * attended)
    local_count = jnp.sum(marks)
    head_index = lax.axis_index("head")
    share = jnp.where(head_index == 0, local_count, jnp.float32(0.0))
    squares_total, count_total = (over_axes(local_squares, SEQ_HEAD), over_axes(share, SEQ_HEAD))
    objective = squares_total / (QUERY_HEADS * count_total)
    return (attention, objective)


def solution(mesh):
    torus = Mesh(
        mesh.devices.reshape(4, 8, 2, mesh.shape["head"]), ("seq_0", "seq_1", "seq_2", "head")
    )
    placed = (P(SEQ, "head"), P(SEQ, "head"), P(SEQ, "head"), P(SEQ), P(SEQ), P(SEQ))
    return jax.shard_map(
        on_device, mesh=torus, in_specs=placed, out_specs=(P(SEQ, "head"), P()), check_vma=False
    )
```

profile of v0, /device:TPU:1, one launch (start us, length us, event | category | flops | bytes accessed | tf_op | source)
XLA Modules:
  0.0 148.4 jit_solution(18145175230012953295)
XLA Ops:
  1.7 4.9 %collective-permute-start = (bf16[512,256]{0,1:T(8,128)(2,1)S(1)}, bf16[512,256]{0,1:T(8,128)(2,1)S(1)}, u32[]{:S(2)}, u32[]{:S(2)}) collective-permute-start(bf16[512,256]{0,1:T(8,128)(2,1)S(1)} %copy.29), channel_id=1, source_target_pairs={{0,4},{4,8},{8,12},{12,16},{16,20},{20,24},{24,28},{28,32},{32,36}... | collective-permute-start | bytes 786440 | tf_op jit(solution)/shard_map/ppermute | solution.py:21
  6.7 1.9 %collective-permute-start.1 = (bf16[512,256]{1,0:T(8,128)(2,1)}, bf16[512,256]{1,0:T(8,128)(2,1)S(1)}, u32[]{:S(2)}, u32[]{:S(2)}) collective-permute-start(bf16[512,256]{1,0:T(8,128)(2,1)} %param.8), channel_id=1, source_target_pairs={{0,4},{4,8},{8,12},{12,16},{16,20},{20,24},{24,28},{28,32},{32,36}... | collective-permute-start | bytes 786440 | tf_op jit(solution)/shard_map/ppermute | solution.py:21
  16.6 2.1 %and_and_fusion.4 = (pred[512,512]{0,1:T(8,128)(4,1)S(1)}, pred[512,512]{0,1:T(8,128)(4,1)S(1)}, pred[512,512]{0,1:T(8,128)(4,1)S(1)}, pred[512,512]{0,1:T(8,128)(4,1)S(1)}, pred[512,512]{0,1:T(8,128)(4,1)S(1)}) fusion(s32[512]{0:T(512)S(1)} %iota_add_fusion.4, s32[512]{0:T(512)} %param.9, pred[]{:T(512)} %bitcast, pred[]{:T(512)} %bitcast.15, ...), kind=kLoop, calls=%fused_computation.51 | loop fusion | flops 5242880 | bytes 1323013 | tf_op jit(solution)/shard_map/and | solution.py:39
  18.6 5.8 %fusion = (f32[512,2,4]{0,2,1:T(4,128)S(1)}, f32[2,512,512,4]{2,1,3,0:T(8,128)}) fusion(pred[512,512]{0,1:T(8,128)(4,1)S(1)} %get-tuple-element.27, bf16[512,2,4,128]{3,2,1,0:T(4,128)(2,1)S(1)} %reshape.417, bf16[512,2,128,1]{2,1,0,3:T(2,128)(2,1)} %bitcast.160), kind=kOutput, calls=%fused_computation.10 | convolution fusion | flops 543158272 | bytes 9977856 | tf_op jit(solution)/shard_map/tgqd,sgd->tgqs/dot_general | solution.py:33
  24.5 3.9 %collective-permute-start.3 = (bf16[512,256]{1,0:T(8,128)(2,1)S(1)}, bf16[512,256]{1,0:T(8,128)(2,1)}, u32[]{:S(2)}, u32[]{:S(2)}) collective-permute-start(bf16[512,256]{1,0:T(8,128)(2,1)S(1)} %collective-permute-done.1), channel_id=1, source_target_pairs={{0,4},{4,8},{8,12},{12,16},{16,20},{20,24},{24,28},{28,32},{32,36}... | collective-permute-start | bytes 786440 | tf_op jit(solution)/shard_map/ppermute | solution.py:21
  31.2 5.0 %fusion.1 = (f32[512,2,4]{0,2,1:T(4,128)S(1)}, f32[2,512,512,4]{2,1,3,0:T(8,128)}) fusion(pred[512,512]{0,1:T(8,128)(4,1)S(1)} %get-tuple-element.31, bf16[512,2,128,1]{0,2,3,1:T(8,128)(2,1)S(1)} %bitcast.155, bf16[512,2,4,128]{3,2,1,0:T(4,128)(2,1)S(1)} %reshape.417), kind=kOutput, calls=%fused_computation.11 | convolution fusion | flops 543158272 | bytes 9977856 | tf_op jit(solution)/shard_map/tgqd,sgd->tgqs/dot_general | solution.py:33
  36.1 3.9 %collective-permute-start.5 = (bf16[512,256]{1,0:T(8,128)(2,1)}, bf16[512,256]{1,0:T(8,128)(2,1)}, u32[]{:S(2)}, u32[]{:S(2)}) collective-permute-start(bf16[512,256]{1,0:T(8,128)(2,1)} %collective-permute-done.3), channel_id=1, source_target_pairs={{0,4},{4,8},{8,12},{12,16},{16,20},{20,24},{24,28},{28,32},{32,36}... | collective-permute-start | bytes 786440 | tf_op jit(solution)/shard_map/ppermute | solution.py:21
  43.8 5.0 %fusion.2 = (f32[512,2,4]{0,2,1:T(4,128)S(1)}, f32[2,512,512,4]{2,1,3,0:T(8,128)}) fusion(pred[512,512]{0,1:T(8,128)(4,1)S(1)} %get-tuple-element.28, bf16[512,2,128,1]{0,2,3,1:T(8,128)(2,1)S(1)} %bitcast.156, bf16[512,2,4,128]{3,2,1,0:T(4,128)(2,1)S(1)} %reshape.417), kind=kOutput, calls=%fused_computation.12 | convolution fusion | flops 543158272 | bytes 9977856 | tf_op jit(solution)/shard_map/tgqd,sgd->tgqs/dot_general | solution.py:33
  48.7 5.1 %collective-permute-start.7 = (bf16[512,256]{1,0:T(8,128)(2,1)}, bf16[512,256]{1,0:T(8,128)(2,1)}, u32[]{:S(2)}, u32[]{:S(2)}) collective-permute-start(bf16[512,256]{1,0:T(8,128)(2,1)} %collective-permute-done.5), channel_id=1, source_target_pairs={{0,4},{4,8},{8,12},{12,16},{16,20},{20,24},{24,28},{28,32},{32,36}... | collective-permute-start | bytes 786440 | tf_op jit(solution)/shard_map/ppermute | solution.py:21
  55.7 2.1 %collective-permute-start.6 = (bf16[512,256]{0,1:T(8,128)(2,1)S(1)}, bf16[512,256]{0,1:T(8,128)(2,1)S(1)}, u32[]{:S(2)}, u32[]{:S(2)}) collective-permute-start(bf16[512,256]{0,1:T(8,128)(2,1)S(1)} %collective-permute-done.4), channel_id=1, source_target_pairs={{0,4},{4,8},{8,12},{12,16},{16,20},{20,24},{24,28},{28,32},{32,36}... | collective-permute-start | bytes 786440 | tf_op jit(solution)/shard_map/ppermute | solution.py:21
  57.8 2.2 %fusion.3 = (f32[512,2,4]{0,2,1:T(4,128)S(1)}, f32[2,512,512,4]{2,1,3,0:T(8,128)S(1)}) fusion(pred[512,512]{0,1:T(8,128)(4,1)S(1)} %get-tuple-element.29, bf16[512,2,128,1]{0,2,3,1:T(8,128)(2,1)S(1)} %bitcast.157, bf16[512,2,4,128]{3,2,1,0:T(4,128)(2,1)S(1)} %reshape.417), kind=kOutput, calls=%fused_computation.13 | convolution fusion | flops 543158272 | bytes 9977856 | tf_op jit(solution)/shard_map/tgqd,sgd->tgqs/dot_general | solution.py:33
  60.9 2.2 %fusion.4 = (f32[512,2,4]{0,2,1:T(4,128)S(1)}, f32[2,512,512,4]{2,1,3,0:T(8,128)S(1)}) fusion(pred[512,512]{0,1:T(8,128)(4,1)S(1)} %get-tuple-element.30, bf16[512,2,128,1]{0,2,3,1:T(8,128)(2,1)S(1)} %bitcast.158, bf16[512,2,4,128]{3,2,1,0:T(4,128)(2,1)S(1)} %reshape.417), kind=kOutput, calls=%fused_computation.14 | convolution fusion | flops 543158272 | bytes 9977856 | tf_op jit(solution)/shard_map/tgqd,sgd->tgqs/dot_general | solution.py:33
  63.1 4.0 %fusion.17 = f32[2,512,4,128]{1,3,2,0:T(8,128)} fusion(bf16[512,2,128,1]{0,2,3,1:T(8,128)(2,1)S(1)} %bitcast.163, f32[2,512,512,4]{2,1,3,0:T(8,128)S(1)} %get-tuple-element.35, f32[512,2,4]{0,2,1:T(4,128)S(1)} %get-tuple-element.20, pred[512,512]{0,1:T(8,128)(4,1)S(1)} %get-tuple-element.29), kind=kOutput, calls=%fused_computation.26 | convolution fusion | flops 547356672 | bytes 11026432 | tf_op jit(solution)/shard_map/tgqs,sgd->tgqd/dot_general | solution.py:50
  70.2 4.0 %fusion.9 = (f32[512,2,4]{0,2,1:T(4,128)S(1)}, f32[512,2,4]{0,2,1:T(4,128)S(1)}) fusion(f32[2,512,512,4]{2,1,3,0:T(8,128)S(1)} %bitcast.151, f32[512,2,4]{0,2,1:T(4,128)S(1)} %get-tuple-element.21, pred[512,512]{0,1:T(8,128)(4,1)S(1)} %get-tuple-element.28, f32[512,2,4]{0,2,1:T(4,128)S(1)} %get-tuple-element.20, ...), kind=kLoop, calls=%fused_computation.19 | loop fusion | flops 20963328 | bytes 17367040 | tf_op jit(solution)/shard_map/reduce_sum | solution.py:48
  74.3 4.1 %fusion.19 = f32[2,512,4,128]{1,3,2,0:T(8,128)} fusion(bf16[512,2,128,1]{0,2,3,1:T(8,128)(2,1)S(1)} %bitcast.162, f32[2,512,512,4]{2,1,3,0:T(8,128)S(1)} %bitcast.151, f32[512,2,4]{0,2,1:T(4,128)S(1)} %get-tuple-element.21, pred[512,512]{0,1:T(8,128)(4,1)S(1)} %get-tuple-element.28), kind=kOutput, calls=%fused_computation.27 | convolution fusion | flops 547356672 | bytes 11026432 | tf_op jit(solution)/shard_map/tgqs,sgd->tgqd/dot_general | solution.py:50
  78.5 4.0 %fusion.21 = f32[2,512,4,128]{1,3,2,0:T(8,128)} fusion(bf16[512,2,128,1]{0,2,3,1:T(8,128)(2,1)S(1)} %bitcast.161, f32[2,512,512,4]{2,1,3,0:T(8,128)S(1)} %bitcast.149, f32[512,2,4]{0,2,1:T(4,128)S(1)} %get-tuple-element.22, pred[512,512]{0,1:T(8,128)(4,1)S(1)} %get-tuple-element.31), kind=kOutput, calls=%fused_computation.28 | convolution fusion | flops 547356672 | bytes 11026432 | tf_op jit(solution)/shard_map/tgqs,sgd->tgqd/dot_general | solution.py:50
  82.4 4.3 %fusion.5 = (f32[512,2,4]{0,2,1:T(4,128)S(1)}, f32[512,2,4]{0,2,1:T(4,128)S(1)}) fusion(f32[2,512,512,4]{2,1,3,0:T(8,128)S(1)} %bitcast.153, f32[512,2,4]{0,2,1:T(4,128)S(1)} %get-tuple-element.26, pred[512,512]{0,1:T(8,128)(4,1)S(1)} %get-tuple-element.27, f32[512,2,4]{0,2,1:T(4,128)S(1)} %get-tuple-element.22, f32[2,512,512,4]{2,1,3,0:T(8,128)S(1)} %bitcast.149, ...), kind=kLoop, calls=%fused_computation.15 | loop fusion | flops 20963328 | bytes 17367040 | tf_op jit(solution)/shard_map/reduce_sum | solution.py:48
  86.7 4.1 %fusion.23 = f32[2,512,4,128]{1,3,2,0:T(8,128)} fusion(bf16[512,2,128,1]{0,2,3,1:T(8,128)(2,1)S(1)} %bitcast.159, f32[2,512,512,4]{2,1,3,0:T(8,128)S(1)} %bitcast.153, f32[512,2,4]{0,2,1:T(4,128)S(1)} %get-tuple-element.26, pred[512,512]{0,1:T(8,128)(4,1)S(1)} %get-tuple-element.27), kind=kOutput, calls=%fused_computation.29 | convolution fusion | flops 547356672 | bytes 11026432 | tf_op jit(solution)/shard_map/tgqs,sgd->tgqd/dot_general | solution.py:50
  90.8 2.0 %fusion.13 = f32[512,2,4]{0,2,1:T(4,128)S(1)} fusion(f32[2,512,512,4]{2,1,3,0:T(8,128)S(1)} %get-tuple-element.33, f32[512,2,4]{0,2,1:T(4,128)S(1)} %get-tuple-element.19, pred[512,512]{0,1:T(8,128)(4,1)S(1)} %get-tuple-element.30), kind=kLoop, calls=%fused_computation.23 | loop fusion | flops 10481664 | bytes 8683520 | tf_op jit(solution)/shard_map/reduce_sum | solution.py:48
  94.0 9.7 %fusion.30 = (f32[]{:T(128)}, bf16[512,2,4,128]{0,3,2,1:T(8,128)(2,1)S(1)}) fusion(f32[512]{0:T(512)S(1)} %convert_element_type.31, f32[512,2,4]{0,2,1:T(4,128)S(1)} %get-tuple-element.14, bf16[512,2,128,1]{0,2,3,1:T(8,128)(2,1)S(1)} %bitcast.164, f32[2,512,512,4]{2,1,3,0:T(8,128)} %copy-done, f32[512,2,4]{0,2,1:T(4,128)S(1)} %get-tuple-element.19, ...), kind=kOutput, calls=%fused_computation.36 | convolution fusion | flops 554696704 | bytes 18466820 | tf_op jit(solution)/shard_map/tgqs,sgd->tgqd/dot_general | solution.py:50
  105.0 9.1 %all-reduce.2 = (f32[]{:T(128)}, f32[]{:T(128)}) all-reduce(f32[]{:T(128)} %get-tuple-element.23, f32[]{:T(128)S(6)} %select_n.45), channel_id=1, replica_groups=mesh['seq_0'=4,'seq_1'=8,'seq_2'=2,'head'=4] {'seq_0'}, use_global_device_ids=true, to_apply=%region_11.12 | all-reduce | flops 2 | bytes 16 | tf_op jit(solution)/shard_map/psum | solution.py:25
  114.1 12.1 %all-reduce = (f32[]{:T(128)}, f32[]{:T(128)}) all-reduce(f32[]{:T(128)} %get-tuple-element.10, f32[]{:T(128)} %get-tuple-element.11), channel_id=1, replica_groups=mesh['seq_0'=4,'seq_1'=8,'seq_2'=2,'head'=4] {'seq_1'}, use_global_device_ids=true, to_apply=%region_12.13 | all-reduce | flops 2 | bytes 16 | tf_op jit(solution)/shard_map/psum | solution.py:25
  126.2 10.4 %all-reduce.3 = (f32[]{:T(128)}, f32[]{:T(128)}) all-reduce(f32[]{:T(128)} %get-tuple-element.6, f32[]{:T(128)} %get-tuple-element.7), channel_id=1, replica_groups=mesh['seq_0'=4,'seq_1'=8,'seq_2'=2,'head'=4] {'seq_2'}, use_global_device_ids=true, to_apply=%region_13.14 | all-reduce | flops 2 | bytes 16 | tf_op jit(solution)/shard_map/psum | solution.py:25
  136.6 9.4 %all-reduce.1 = (f32[]{:T(128)}, f32[]{:T(128)}) all-reduce(f32[]{:T(128)} %get-tuple-element.12, f32[]{:T(128)} %get-tuple-element.13), channel_id=1, replica_groups=mesh['seq_0'=4,'seq_1'=8,'seq_2'=2,'head'=4] {'head'}, use_global_device_ids=true, to_apply=%region_14.15 | all-reduce | flops 2 | bytes 16 | tf_op jit(solution)/shard_map/psum | solution.py:25
  (51 shorter events, 22.6 us)
Async XLA Ops:
  1.7 27.5 %collective-permute-start = (bf16[512,256]{0,1:T(8,128)(2,1)S(1)}, bf16[512,256]{0,1:T(8,128)(2,1)S(1)}, u32[]{:S(2)}, u32[]{:S(2)}) collective-permute-start(bf16[512,256]{0,1:T(8,128)(2,1)S(1)} %copy.29), channel_id=1, source_target_pairs={{0,4},{4,8},{8,12},{12,16},{16,20},{20,24},{24,28},{28,32},{32,36}... | collective-permute-start | bytes 786440 | tf_op jit(solution)/shard_map/ppermute | solution.py:21
  6.7 17.8 %collective-permute-start.1 = (bf16[512,256]{1,0:T(8,128)(2,1)}, bf16[512,256]{1,0:T(8,128)(2,1)S(1)}, u32[]{:S(2)}, u32[]{:S(2)}) collective-permute-start(bf16[512,256]{1,0:T(8,128)(2,1)} %param.8), channel_id=1, source_target_pairs={{0,4},{4,8},{8,12},{12,16},{16,20},{20,24},{24,28},{28,32},{32,36}... | collective-permute-start | bytes 786440 | tf_op jit(solution)/shard_map/ppermute | solution.py:21
  24.5 11.6 %collective-permute-start.3 = (bf16[512,256]{1,0:T(8,128)(2,1)S(1)}, bf16[512,256]{1,0:T(8,128)(2,1)}, u32[]{:S(2)}, u32[]{:S(2)}) collective-permute-start(bf16[512,256]{1,0:T(8,128)(2,1)S(1)} %collective-permute-done.1), channel_id=1, source_target_pairs={{0,4},{4,8},{8,12},{12,16},{16,20},{20,24},{24,28},{28,32},{32,36}... | collective-permute-start | bytes 786440 | tf_op jit(solution)/shard_map/ppermute | solution.py:21
  29.2 12.6 %collective-permute-start.2 = (bf16[512,256]{0,1:T(8,128)(2,1)S(1)}, bf16[512,256]{0,1:T(8,128)(2,1)S(1)}, u32[]{:S(2)}, u32[]{:S(2)}) collective-permute-start(bf16[512,256]{0,1:T(8,128)(2,1)S(1)} %collective-permute-done), channel_id=1, source_target_pairs={{0,4},{4,8},{8,12},{12,16},{16,20},{20,24},{24,28},{28,32},{32,36}... | collective-permute-start | bytes 786440 | tf_op jit(solution)/shard_map/ppermute | solution.py:21
  36.1 12.6 %collective-permute-start.5 = (bf16[512,256]{1,0:T(8,128)(2,1)}, bf16[512,256]{1,0:T(8,128)(2,1)}, u32[]{:S(2)}, u32[]{:S(2)}) collective-permute-start(bf16[512,256]{1,0:T(8,128)(2,1)} %collective-permute-done.3), channel_id=1, source_target_pairs={{0,4},{4,8},{8,12},{12,16},{16,20},{20,24},{24,28},{28,32},{32,36}... | collective-permute-start | bytes 786440 | tf_op jit(solution)/shard_map/ppermute | solution.py:21
  41.9 13.8 %collective-permute-start.4 = (bf16[512,256]{0,1:T(8,128)(2,1)S(1)}, bf16[512,256]{0,1:T(8,128)(2,1)S(1)}, u32[]{:S(2)}, u32[]{:S(2)}) collective-permute-start(bf16[512,256]{0,1:T(8,128)(2,1)S(1)} %collective-permute-done.2), channel_id=1, source_target_pairs={{0,4},{4,8},{8,12},{12,16},{16,20},{20,24},{24,28},{28,32},{32,36}... | collective-permute-start | bytes 786440 | tf_op jit(solution)/shard_map/ppermute | solution.py:21
  48.7 44.2 %collective-permute-start.7 = (bf16[512,256]{1,0:T(8,128)(2,1)}, bf16[512,256]{1,0:T(8,128)(2,1)}, u32[]{:S(2)}, u32[]{:S(2)}) collective-permute-start(bf16[512,256]{1,0:T(8,128)(2,1)} %collective-permute-done.5), channel_id=1, source_target_pairs={{0,4},{4,8},{8,12},{12,16},{16,20},{20,24},{24,28},{28,32},{32,36}... | collective-permute-start | bytes 786440 | tf_op jit(solution)/shard_map/ppermute | solution.py:21
  55.7 5.2 %collective-permute-start.6 = (bf16[512,256]{0,1:T(8,128)(2,1)S(1)}, bf16[512,256]{0,1:T(8,128)(2,1)S(1)}, u32[]{:S(2)}, u32[]{:S(2)}) collective-permute-start(bf16[512,256]{0,1:T(8,128)(2,1)S(1)} %collective-permute-done.4), channel_id=1, source_target_pairs={{0,4},{4,8},{8,12},{12,16},{16,20},{20,24},{24,28},{28,32},{32,36}... | collective-permute-start | bytes 786440 | tf_op jit(solution)/shard_map/ppermute | solution.py:21
  57.8 5.3 %copy-start.3 = (bf16[512,256]{0,1:T(8,128)(2,1)S(1)}, bf16[512,256]{0,1:T(8,128)(2,1)}, u32[]{:S(2)}) copy-start(bf16[512,256]{0,1:T(8,128)(2,1)} %copy.40) | copy-start | bytes 786436
  63.1 27.7 %copy-start = (f32[2,512,512,4]{2,1,3,0:T(8,128)}, f32[2,512,512,4]{2,1,3,0:T(8,128)S(1)}, u32[]{:S(2)}) copy-start(f32[2,512,512,4]{2,1,3,0:T(8,128)S(1)} %get-tuple-element.33) | copy-start | bytes 25165828
  63.1 5.3 %slice-start.2 = ((s8[8388608]{0:T(1024)(128)(4,1)}), s8[4194304]{0:T(1024)(128)(4,1)S(1)}, s32[]{:S(2)}) async-start(s8[8388608]{0:T(1024)(128)(4,1)} %bitcast.150), calls=%async_computation.2 | async-start | bytes 8388608
  63.1 7.1 %slice-start.3 = ((s8[8388608]{0:T(1024)(128)(4,1)}), s8[4194304]{0:T(1024)(128)(4,1)S(1)}, s32[]{:S(2)}) async-start(s8[8388608]{0:T(1024)(128)(4,1)} %bitcast.150), calls=%async_computation.3 | async-start | bytes 8388608
  70.2 4.1 %copy-start.2 = (bf16[512,256]{0,1:T(8,128)(2,1)S(1)}, bf16[512,256]{0,1:T(8,128)(2,1)}, u32[]{:S(2)}) copy-start(bf16[512,256]{0,1:T(8,128)(2,1)} %copy.36) | copy-start | bytes 786436
  74.3 4.1 %slice-start = ((s8[8388608]{0:T(1024)(128)(4,1)}), s8[4194304]{0:T(1024)(128)(4,1)S(1)}, s32[]{:S(2)}) async-start(s8[8388608]{0:T(1024)(128)(4,1)} %bitcast.148), calls=%async_computation | async-start | bytes 8388608
  74.3 4.1 %copy-start.1 = (bf16[512,256]{0,1:T(8,128)(2,1)S(1)}, bf16[512,256]{0,1:T(8,128)(2,1)}, u32[]{:S(2)}) copy-start(bf16[512,256]{0,1:T(8,128)(2,1)} %copy.32) | copy-start | bytes 786436
  74.3 4.1 %slice-start.1 = ((s8[8388608]{0:T(1024)(128)(4,1)}), s8[4194304]{0:T(1024)(128)(4,1)S(1)}, s32[]{:S(2)}) async-start(s8[8388608]{0:T(1024)(128)(4,1)} %bitcast.148), calls=%async_computation.1 | async-start | bytes 8388608
  78.4 4.0 %slice-start.4 = ((s8[8388608]{0:T(1024)(128)(4,1)}), s8[4194304]{0:T(1024)(128)(4,1)S(1)}, s32[]{:S(2)}) async-start(s8[8388608]{0:T(1024)(128)(4,1)} %bitcast.152), calls=%async_computation.4 | async-start | bytes 8388608
  78.4 4.0 %slice-start.5 = ((s8[8388608]{0:T(1024)(128)(4,1)}), s8[4194304]{0:T(1024)(128)(4,1)S(1)}, s32[]{:S(2)}) async-start(s8[8388608]{0:T(1024)(128)(4,1)} %bitcast.152), calls=%async_computation.5 | async-start | bytes 8388608
where the time goes:
time: 149 us; the launch traced here: 148 us
  matrix products  45.9 us (31%)
  blocking collectives  41 us (28%)
  starting transfers between devices  25.7 us (17%)
  local copies, waits for them, and re-layouts  15.7 us (11%)
  other arithmetic  14.5 us (10%)
  between operations  4.69 us (3%)
    psum x4, blocking collectives, over_axes(): return functools.reduce(lax.psum, axes, shard)  41 us
    dot_general x5, matrix products, attend_block(): jnp.einsum('tgqs,sgd->tgqd', rounded, value_block, preferred_element_type...  25.8 us
    ppermute x8, starting transfers between devices, passed_along(): return lax.ppermute(shard, axis, pairs)  25.7 us
    dot_general x5, matrix products, attend_block(): jnp.einsum('tgqd,sgd->tgqs', grouped_queries, key_block, preferred_elemen...  20.1 us
    reduce_sum x3, other arithmetic, attend_block(): total_new = total_old * ratio_old + jnp.sum(weights, axis=-1)  10.4 us
    ppermute x4, local copies, waits for them, and re-layouts, passed_along(): return lax.ppermute(shard, axis, pairs)  5.55 us
    unnamed x22, local copies, waits for them, and re-layouts  5.54 us
  transfers between devices with their start and end apart: 8, of which 1 were waited for; matrix products, arithmetic and copies ran while one was open for 40% of the time, Pallas kernels for 0%

commit v1 on v0

v1 whole, which is shorter than its diff:
```python
import math

import jax
import jax.numpy as jnp
from jax import lax
from jax.experimental import pallas as pl
from jax.experimental.pallas import tpu as pltpu
from jax.sharding import Mesh
from jax.sharding import PartitionSpec as P

QUERY_HEADS = 32
KEY_VALUE_HEADS = 8
HEAD_WIDTH = 128
GROUP = QUERY_HEADS // KEY_VALUE_HEADS
SEQ = ("seq_0", "seq_1", "seq_2")
SEQ_HEAD = ("seq_0", "seq_1", "seq_2", "head")
ROWS = 512
TILE = 128
TILES = ROWS // TILE
LOCAL_KV = 2
WIDE = GROUP * HEAD_WIDTH
LOWEST = -1e30
EXP2_SCALE = math.log2(math.e) / math.sqrt(HEAD_WIDTH)
TOP, TOTAL, FIRST, MARK = 0, GROUP, 2 * GROUP, 2 * GROUP + 1


def ds(start, size):
    return pl.ds(start if isinstance(start, int) else pl.multiple_of(start, size), size)


def dot(a, b, contract_b):
    return lax.dot_general(
        a, b, (((1,), (contract_b,)), ((), ())), preferred_element_type=jnp.float32
    )


def grouped_queries(q_ref, kv, tile):
    parts = [
        q_ref[ds(tile * TILE, TILE), ds(kv * WIDE + g * HEAD_WIDTH, HEAD_WIDTH)]
        for g in range(GROUP)
    ]
    return jnp.concatenate(parts, axis=0)


def with_lanes(base, columns):
    lane = lax.broadcasted_iota(jnp.int32, base.shape, 1)
    for at, column in columns:
        base = jnp.where(lane == at, column, base)
    return base


def absorb_own(q_ref, block_ref, acc_ref, stat_ref, kv, tile, first, mark):
    seen_keys = (tile + 1) * TILE
    k = block_ref[0:seen_keys, ds(kv * HEAD_WIDTH, HEAD_WIDTH)]
    v = block_ref[0:seen_keys, ds((LOCAL_KV + kv) * HEAD_WIDTH, HEAD_WIDTH)]
    scores = dot(grouped_queries(q_ref, kv, tile), k, 1)
    place = lax.broadcasted_iota(jnp.int32, (TILE, seen_keys), 1).astype(jnp.float32)
    row = lax.broadcasted_iota(jnp.int32, (TILE, seen_keys), 0).astype(jnp.float32) + tile * TILE
    seen = (place >= first[:, 0:1]) & (place <= row)
    rounded, columns = [], [(FIRST, first), (MARK, mark)]
    for g in range(GROUP):
        part = jnp.where(seen, scores[g * TILE : (g + 1) * TILE], LOWEST)
        top = jnp.max(part, axis=1, keepdims=True)
        weights = jnp.exp2((part - top) * EXP2_SCALE)
        columns += [(TOP + g, top), (TOTAL + g, jnp.sum(weights, axis=1, keepdims=True))]
        rounded.append(weights.astype(jnp.bfloat16))
    update = dot(jnp.concatenate(rounded, axis=0), v, 0)
    for g in range(GROUP):
        acc_ref[tile * TILE : (tile + 1) * TILE, ds(kv * WIDE + g * HEAD_WIDTH, HEAD_WIDTH)] = (
            update[g * TILE : (g + 1) * TILE]
        )
    stat_ref[kv, tile * TILE : (tile + 1) * TILE, :] = with_lanes(
        jnp.zeros((TILE, 128), jnp.float32), columns
    )


def absorb_earlier(q_ref, block_ref, acc_ref, stat_ref, kv, tile, offset):
    rows = ds(tile * TILE, TILE)
    stats = stat_ref[kv, rows, :]
    k = block_ref[:, ds(kv * HEAD_WIDTH, HEAD_WIDTH)]
    v = block_ref[:, ds((LOCAL_KV + kv) * HEAD_WIDTH, HEAD_WIDTH)]
    scores = dot(grouped_queries(q_ref, kv, tile), k, 1)
    place = (lax.broadcasted_iota(jnp.int32, (TILE, ROWS), 1) + offset).astype(jnp.float32)
    seen = place >= stats[:, FIRST : FIRST + 1]
    rounded, columns, ratios = [], [], []
    for g in range(GROUP):
        part = jnp.where(seen, scores[g * TILE : (g + 1) * TILE], LOWEST)
        top_old = stats[:, TOP + g : TOP + g + 1]
        top = jnp.maximum(top_old, jnp.max(part, axis=1, keepdims=True))
        ratio = jnp.exp2((top_old - top) * EXP2_SCALE)
        weights = jnp.exp2((part - top) * EXP2_SCALE)
        total = stats[:, TOTAL + g : TOTAL + g + 1] * ratio
        columns += [
            (TOP + g, top),
            (TOTAL + g, total + jnp.sum(weights, axis=1, keepdims=True)),
        ]
        ratios.append(ratio)
        rounded.append(weights.astype(jnp.bfloat16))
    update = dot(jnp.concatenate(rounded, axis=0), v, 0)
    for g in range(GROUP):
        cols = ds(kv * WIDE + g * HEAD_WIDTH, HEAD_WIDTH)
        acc_ref[rows, cols] = acc_ref[rows, cols] * ratios[g] + update[g * TILE : (g + 1) * TILE]
    stat_ref[kv, rows, :] = with_lanes(stats, columns)


def reaches(doc_ref, spot_ref, tile, offset):
    earliest = jnp.maximum(doc_ref[tile * TILE], spot_ref[1]) - spot_ref[0]
    return (offset < 0) & (offset + ROWS > earliest)


def first_kernel(
    spot_ref, doc_ref, rows_ref, q_ref, own_ref, side_ref, acc_ref, stat_ref
):
    def turned(at):
        row = jnp.broadcast_to(rows_ref[at : at + 1, :], (TILE, 128))
        return row.T

    def head(kv, carry):
        for tile in range(TILES):
            absorb_own(
                q_ref, own_ref, acc_ref, stat_ref, kv, tile, turned(tile), turned(TILES + tile)
            )
        return carry

    lax.fori_loop(0, LOCAL_KV, head, 0)
    sweep(spot_ref, doc_ref, q_ref, (side_ref,), acc_ref, stat_ref, lambda kv, tile: None)


def sweep(spot_ref, doc_ref, q_ref, block_refs, acc_ref, stat_ref, before):
    def step(index, carry):
        kv, tile = index // TILES, index % TILES
        before(kv, tile)
        for slot, block_ref in enumerate(block_refs):
            offset = spot_ref[2 + slot]

            @pl.when(reaches(doc_ref, spot_ref, tile, offset))
            def _():
                absorb_earlier(q_ref, block_ref, acc_ref, stat_ref, kv, tile, offset)

        return carry

    lax.fori_loop(0, LOCAL_KV * TILES, step, 0)


def middle_kernel(
    spot_ref, doc_ref, q_ref, far_ref, side_ref, acc_in, stat_in, acc_ref, stat_ref
):
    def before(kv, tile):
        rows, cols = ds(tile * TILE, TILE), ds(kv * WIDE, WIDE)
        acc_ref[rows, cols] = acc_in[rows, cols]
        stat_ref[kv, rows, :] = stat_in[kv, rows, :]

    sweep(spot_ref, doc_ref, q_ref, (far_ref, side_ref), acc_ref, stat_ref, before)


def last_kernel(
    spot_ref, doc_ref, q_ref, far_ref, side_ref, acc_in, stat_in, out_ref, share_ref,
    acc_ref, stat_ref, squares_ref, count_ref
):
    squares_ref[...] = jnp.zeros_like(squares_ref)
    count_ref[...] = jnp.zeros_like(count_ref)

    def finish(acc, stat, kv, tile):
        rows = ds(tile * TILE, TILE)
        stats = stat[kv, rows, :]
        marks = stats[:, MARK : MARK + 1]
        squares = jnp.zeros((TILE, HEAD_WIDTH), jnp.float32)
        for g in range(GROUP):
            cols = ds(kv * WIDE + g * HEAD_WIDTH, HEAD_WIDTH)
            attended = acc[rows, cols] / stats[:, TOTAL + g : TOTAL + g + 1]
            out_ref[rows, cols] = attended.astype(jnp.bfloat16)
            squares += attended * attended
        squares *= marks
        squares_ref[...] += jnp.sum(squares.reshape(TILE // 8, 8, HEAD_WIDTH), axis=0)
        count_ref[...] += jnp.sum(stats.reshape(TILE // 8, 8, 128), axis=0)

    def step(index, carry):
        kv, tile = index // TILES, index % TILES
        rows, cols = ds(tile * TILE, TILE), ds(kv * WIDE, WIDE)
        needs = [
            reaches(doc_ref, spot_ref, tile, spot_ref[2]),
            reaches(doc_ref, spot_ref, tile, spot_ref[3]),
        ]

        @pl.when(needs[0] | needs[1])
        def _():
            acc_ref[rows, cols] = acc_in[rows, cols]
            stat_ref[kv, rows, :] = stat_in[kv, rows, :]
            for slot, block_ref in enumerate((far_ref, side_ref)):

                @pl.when(needs[slot])
                def _():
                    absorb_earlier(
                        q_ref, block_ref, acc_ref, stat_ref, kv, tile, spot_ref[2 + slot]
                    )

            finish(acc_ref, stat_ref, kv, tile)

        @pl.when(jnp.logical_not(needs[0] | needs[1]))
        def _():
            finish(acc_in, stat_in, kv, tile)

        return carry

    lax.fori_loop(0, LOCAL_KV * TILES, step, 0)
    lane = lax.broadcasted_iota(jnp.int32, (8, 128), 1)
    squares = jnp.sum(squares_ref[...])
    count = jnp.sum(jnp.where(lane == MARK, count_ref[...], 0.0)) * (1.0 / LOCAL_KV)
    full = lax.broadcasted_iota(jnp.int32, share_ref.shape, 1)
    share_ref[...] = jnp.where(full == 0, squares, jnp.where(full == 1, count, 0.0))


def call(kernel, out_shapes, operands, flops, scratch=()):
    smem = pl.BlockSpec(memory_space=pltpu.SMEM)
    vmem = pl.BlockSpec(memory_space=pltpu.VMEM)
    return pl.pallas_call(
        kernel,
        out_shape=out_shapes,
        in_specs=[smem, smem] + [vmem] * (len(operands) - 2),
        out_specs=[vmem] * len(out_shapes),
        scratch_shapes=list(scratch),
        compiler_params=pltpu.CompilerParams(vmem_limit_bytes=24 * 1024 * 1024),
        cost_estimate=pl.CostEstimate(flops=flops, bytes_accessed=2**20, transcendentals=2**21),
    )(*operands)


def on_device(queries, keys, values, doc_start, hop_counts, loss_mask):
    core = lax.axis_index("seq_2")
    block = lax.axis_index(SEQ)
    here = block * ROWS
    floor = (block - hop_counts[0]) * ROWS
    nowhere = jnp.int32(ROWS)

    def spot(*offsets):
        return jnp.stack([here, floor] + [jnp.int32(o) for o in offsets])

    own = jnp.concatenate([keys, values], axis=1)

    def onward(shard):
        devices = lax.axis_size(SEQ)
        return lax.ppermute(shard, SEQ, [(i, i + 2) for i in range(devices - 2)])

    def across(shard, pairs):
        return lax.ppermute(shard, "seq_2", pairs)

    far_2 = onward(own)
    side_a = across(own, [(0, 1)])

    first_key = (jnp.maximum(doc_start, floor) - here).astype(jnp.float32)
    rows = jnp.concatenate(
        [first_key.reshape(TILES, TILE), loss_mask.astype(jnp.float32).reshape(TILES, TILE)]
    )
    acc_shape = jax.ShapeDtypeStruct((ROWS, LOCAL_KV * WIDE), jnp.float32)
    stat_shape = jax.ShapeDtypeStruct((LOCAL_KV, ROWS, 128), jnp.float32)
    acc, stat = call(
        first_kernel,
        [acc_shape, stat_shape],
        [spot(jnp.where(core == 1, -ROWS, nowhere)), doc_start, rows, queries, own, side_a],
        2 * 10**9,
    )
    far_4 = onward(far_2)
    side_b = across(far_2, [(0, 1), (1, 0)])
    acc, stat = call(
        middle_kernel,
        [acc_shape, stat_shape],
        [
            spot(-2 * ROWS, jnp.where(core == 1, -3 * ROWS, -ROWS)),
            doc_start, queries, far_2, side_b, acc, stat,
        ],
        2 * 10**9,
    )
    side_c = across(far_4, [(1, 0)])
    devices = lax.axis_size(SEQ_HEAD)
    attention, share = call(
        last_kernel,
        [
            jax.ShapeDtypeStruct((ROWS, LOCAL_KV * WIDE), jnp.bfloat16),
            jax.ShapeDtypeStruct((devices, 128), jnp.float32),
        ],
        [
            spot(-4 * ROWS, jnp.where(core == 1, nowhere, -3 * ROWS)),
            doc_start, queries, far_4, side_c, acc, stat,
        ],
        10**9,
        scratch=[
            pltpu.VMEM(acc_shape.shape, jnp.float32),
            pltpu.VMEM(stat_shape.shape, jnp.float32),
            pltpu.VMEM((8, 128), jnp.float32),
            pltpu.VMEM((8, 128), jnp.float32),
        ],
    )
    shares = lax.all_to_all(share, SEQ_HEAD, 0, 0, tiled=True)
    sums = jnp.sum(shares, axis=0)
    objective = sums[0] / (QUERY_HEADS * (sums[1] / lax.axis_size("head")))
    return (attention, objective)


def solution(mesh):
    torus = Mesh(
        mesh.devices.reshape(4, 8, 2, mesh.shape["head"]), ("seq_0", "seq_1", "seq_2", "head")
    )
    placed = (P(SEQ, "head"), P(SEQ, "head"), P(SEQ, "head"), P(SEQ), P(SEQ), P(SEQ))

    return jax.shard_map(
        on_device, mesh=torus, in_specs=placed, out_specs=(P(SEQ, "head"), P()), check_vma=False
    )
```

time: 149 us -> 112 us (0.75)
  matrix products: 45.9 us -> 0 us
  blocking collectives: 41 us -> 56.7 us
  waiting for transfers between devices: 0.94 us -> 15.6 us
  Pallas kernels: 0 us -> 14.2 us
  other arithmetic: 14.5 us -> 1.23 us
  local copies, waits for them, and re-layouts: 15.7 us -> 4.43 us
  starting transfers between devices: 25.7 us -> 16 us
    all_to_all x0 -> x1, blocking collectives: none -> 56.7 us  [on_device(): shares = lax.all_to_all(share, SEQ_HEAD, 0, 0, tiled=True)]
    dot_general x10 -> x0, matrix products: 45.9 us -> none  [the longest x5 25.8 us: attend_block(): jnp.einsum('tgqs,sgd->tgqd', rounded, value_block, preferred_element_type...]
    psum x4 -> x0, blocking collectives: 41 us -> none  [over_axes(): return functools.reduce(lax.psum, axes, shard)]
    ppermute x8 -> x5, waiting for transfers between devices: 0.94 us -> 15.6 us  [the longest x2 15.6 us: onward(): return lax.ppermute(shard, SEQ, [(i, i + 2) for i in range(devices - 2)])]
    pallas_call x0 -> x3, Pallas kernels: none -> 14.2 us  [call(): pl.pallas_call(kernel, out_shape=out_shapes, in_specs=[smem, smem] + [vme...]
    reduce_sum x4 -> x1, other arithmetic: 11.7 us -> 0.29 us  [on_device(): sums = jnp.sum(shares, axis=0)]
    ppermute x8 -> x5, starting transfers between devices: 25.7 us -> 16 us  [the longest x2 8.52 us: onward(): return lax.ppermute(shard, SEQ, [(i, i + 2) for i in range(devices - 2)])]
    ppermute x4 -> x0, local copies, waits for them, and re-layouts: 5.55 us -> none  [passed_along(): return lax.ppermute(shard, axis, pairs)]
  transfers between devices with their start and end apart: 8 -> 5, of which waited for: 1 -> 2; matrix products, arithmetic and copies ran while one was open for 40% -> 1% of each run, Pallas kernels for 0% -> 10%
where the time goes in v1:
time: 112 us
  blocking collectives  56.7 us (51%)
  starting transfers between devices  16 us (14%)
  waiting for transfers between devices  15.6 us (14%)
  Pallas kernels  14.2 us (13%)
  local copies, waits for them, and re-layouts  4.43 us (4%)
  between operations  3.81 us (3%)
  other arithmetic  1.23 us (1%)
    all_to_all x1, blocking collectives, on_device(): shares = lax.all_to_all(share, SEQ_HEAD, 0, 0, tiled=True)  56.7 us
    ppermute x2, waiting for transfers between devices, onward(): return lax.ppermute(shard, SEQ, [(i, i + 2) for i in range(devices - 2)])  15.6 us
    pallas_call x3, Pallas kernels, call(): pl.pallas_call(kernel, out_shape=out_shapes, in_specs=[smem, smem] + [vme...  14.2 us
    ppermute x2, starting transfers between devices, onward(): return lax.ppermute(shard, SEQ, [(i, i + 2) for i in range(devices - 2)])  8.52 us
    ppermute x3, starting transfers between devices, across(): return lax.ppermute(shard, 'seq_2', pairs)  7.44 us
    unnamed x7, local copies, waits for them, and re-layouts  2.87 us
  transfers between devices with their start and end apart: 5, of which 2 were waited for; matrix products, arithmetic and copies ran while one was open for 1% of the time, Pallas kernels for 10%

profile of v1, /device:TPU:1, one launch (start us, length us, event | category | flops | bytes accessed | tf_op | source)
XLA Modules:
  0.0 111.9 jit_solution(11797634349016886573)
XLA Ops:
  0.6 1.0 constant_dynamic-update-slice_fusion.1
  1.6 1.0 constant_dynamic-update-slice_fusion.own_ref
  2.6 4.4 %collective-permute-start = (bf16[512,512]{1,0:T(8,128)(2,1)S(1)}, bf16[512,512]{1,0:T(8,128)(2,1)S(1)}, u32[]{:S(2)}, u32[]{:S(2)}) collective-permute-start(bf16[512,512]{1,0:T(8,128)(2,1)S(1)} %constant_dynamic-update-slice_fusion.own_ref), channel_id=1, source_target_pairs={{0,8},{4,12},{8,16},{12,20},{16,24},{20,28},{24,32},{28,36},{32,40... | collective-permute-start | bytes 1572872 | tf_op jit(solution)/shard_map/ppermute | solution.py:241
  7.0 10.6 %collective-permute-done.far_ref = bf16[512,512]{1,0:T(8,128)(2,1)S(1)} collective-permute-done((bf16[512,512]{1,0:T(8,128)(2,1)S(1)}, bf16[512,512]{1,0:T(8,128)(2,1)S(1)}, u32[]{:S(2)}, u32[]{:S(2)}) %collective-permute-start) | collective-permute-done | bytes 524320 | tf_op jit(solution)/shard_map/ppermute | solution.py:241
  17.5 4.1 %collective-permute-start.1 = (bf16[512,512]{1,0:T(8,128)(2,1)S(1)}, bf16[512,512]{1,0:T(8,128)(2,1)S(1)}, u32[]{:S(2)}, u32[]{:S(2)}) collective-permute-start(bf16[512,512]{1,0:T(8,128)(2,1)S(1)} %collective-permute-done.far_ref), channel_id=1, source_target_pairs={{0,8},{4,12},{8,16},{12,20},{16,24},{20,28},{24,32},{28,36},{32,40... | collective-permute-start | bytes 1572872 | tf_op jit(solution)/shard_map/ppermute | solution.py:241
  21.7 1.3 %collective-permute-start.4 = (bf16[512,512]{1,0:T(8,128)(2,1)S(1)}, bf16[512,512]{1,0:T(8,128)(2,1)S(1)}, u32[]{:S(2)}, u32[]{:S(2)}) collective-permute-start(bf16[512,512]{1,0:T(8,128)(2,1)S(1)} %constant_dynamic-update-slice_fusion.own_ref), channel_id=1, source_target_pairs={{0,4},{1,5},{2,6},{3,7},{8,12},{9,13},{10,14},{11,15},{16,20},{17,... | collective-permute-start | bytes 1572872 | tf_op jit(solution)/shard_map/ppermute | solution.py:244
  23.6 0.1 pad_add_fusion.3.spot_ref
  23.7 0.7 convert_bitcast_fusion
  24.4 1.8 %collective-permute-start.3 = (bf16[512,512]{1,0:T(8,128)(2,1)S(1)}, bf16[512,512]{1,0:T(8,128)(2,1)S(1)}, u32[]{:S(2)}, u32[]{:S(2)}) collective-permute-start(bf16[512,512]{1,0:T(8,128)(2,1)S(1)} %collective-permute-done.far_ref), channel_id=1, source_target_pairs={{0,4},{4,0},{1,5},{5,1},{2,6},{6,2},{3,7},{7,3},{8,12},{12,8},{9,1... | collective-permute-start | bytes 1572872 | tf_op jit(solution)/shard_map/ppermute | solution.py:244
  26.2 0.1 pad_add_fusion.2.spot_ref
  26.3 5.0 %collective-permute-done.1.far_ref = bf16[512,512]{1,0:T(8,128)(2,1)S(1)} collective-permute-done((bf16[512,512]{1,0:T(8,128)(2,1)S(1)}, bf16[512,512]{1,0:T(8,128)(2,1)S(1)}, u32[]{:S(2)}, u32[]{:S(2)}) %collective-permute-start.1) | collective-permute-done | bytes 524320 | tf_op jit(solution)/shard_map/ppermute | solution.py:241
  31.4 4.3 %collective-permute-start.2 = (bf16[512,512]{1,0:T(8,128)(2,1)S(1)}, bf16[512,512]{1,0:T(8,128)(2,1)S(1)}, u32[]{:S(2)}, u32[]{:S(2)}) collective-permute-start(bf16[512,512]{1,0:T(8,128)(2,1)S(1)} %collective-permute-done.1.far_ref), channel_id=1, source_target_pairs={{4,0},{5,1},{6,2},{7,3},{12,8},{13,9},{14,10},{15,11},{20,16},{21,... | collective-permute-start | bytes 1572872 | tf_op jit(solution)/shard_map/ppermute | solution.py:244
  35.7 0.1 pad_add_fusion.spot_ref
  35.8 0.0 copy-start
  35.8 1.2 %copy-done = bf16[512,1024]{1,0:T(8,128)(2,1)S(1)} copy-done((bf16[512,1024]{1,0:T(8,128)(2,1)S(1)}, bf16[512,1024]{1,0:T(8,128)(2,1)}, u32[]{:S(2)}) %copy-start) | copy-done | bytes 1048600
  37.0 0.7 copy-done.2
  37.7 10.2 %shard_map.77 = (f32[512,1024]{1,0:T(8,128)S(1)}, f32[2,512,128]{2,1,0:T(8,128)S(1)}) custom-call(s32[3]{0:T(128)S(1)} %pad_add_fusion.3.spot_ref, s32[512]{0:T(512)S(1)} %copy-done.2, f32[8,128]{1,0:T(8,128)S(1)} %pad_maximum_fusion.rows_ref, bf16[512,1024]{1,0:T(8,128)(2,1)S(1)} %copy-done, bf16[512,512]{1,0:T(8,128)(2,1)S(1)} %constant_dynamic-update-slice_fusion.own_ref, ...), custom_call_target="tpu_custom_call" | custom-call | flops 2000000000 | bytes 1048576 | tf_op jit(solution)/shard_map/pallas_call | solution.py:216
  48.0 0.0 collective-permute-done.3.side_ref
  48.0 0.9 shard_map.78
  48.9 0.0 collective-permute-done.2.side_ref
  48.9 3.0 %shard_map.79 = (bf16[512,1024]{1,0:T(8,128)(2,1)}, f32[256,128]{1,0:T(8,128)S(1)}) custom-call(s32[4]{0:T(128)S(1)} %pad_add_fusion.spot_ref, s32[512]{0:T(512)S(1)} %copy-done.2, bf16[512,1024]{1,0:T(8,128)(2,1)S(1)} %copy-done.1, bf16[512,512]{1,0:T(8,128)(2,1)S(1)} %collective-permute-done.1.far_ref, ...), custom_call_target="tpu_custom_call" | custom-call | flops 1000000000 | bytes 1048576 | tf_op jit(solution)/shard_map/pallas_call | solution.py:216
  51.9 56.7 %all_to_all.9 = f32[256,1,128]{2,1,0:T(1,128)S(1)} all-to-all(f32[256,1,128]{2,1,0:T(1,128)S(1)} %bitcast.15), channel_id=1, replica_groups=mesh['seq_0'=4,'seq_1'=8,'seq_2'=2,'head'=4] {'seq_0','seq_1','seq_2','h..., dimensions={0} | all-to-all | bytes 262144 | tf_op jit(solution)/shard_map/all_to_all | solution.py:292
  108.6 0.3 reduce_sum.9
  108.9 0.6 fusion
  (5 shorter events, 0.0 us)
Async XLA Ops:
  2.6 15.0 %collective-permute-start = (bf16[512,512]{1,0:T(8,128)(2,1)S(1)}, bf16[512,512]{1,0:T(8,128)(2,1)S(1)}, u32[]{:S(2)}, u32[]{:S(2)}) collective-permute-start(bf16[512,512]{1,0:T(8,128)(2,1)S(1)} %constant_dynamic-update-slice_fusion.own_ref), channel_id=1, source_target_pairs={{0,8},{4,12},{8,16},{12,20},{16,24},{20,28},{24,32},{28,36},{32,40... | collective-permute-start | bytes 1572872 | tf_op jit(solution)/shard_map/ppermute | solution.py:241
  17.5 13.8 %collective-permute-start.1 = (bf16[512,512]{1,0:T(8,128)(2,1)S(1)}, bf16[512,512]{1,0:T(8,128)(2,1)S(1)}, u32[]{:S(2)}, u32[]{:S(2)}) collective-permute-start(bf16[512,512]{1,0:T(8,128)(2,1)S(1)} %collective-permute-done.far_ref), channel_id=1, source_target_pairs={{0,8},{4,12},{8,16},{12,20},{16,24},{20,28},{24,32},{28,36},{32,40... | collective-permute-start | bytes 1572872 | tf_op jit(solution)/shard_map/ppermute | solution.py:241
  21.7 14.1 %collective-permute-start.4 = (bf16[512,512]{1,0:T(8,128)(2,1)S(1)}, bf16[512,512]{1,0:T(8,128)(2,1)S(1)}, u32[]{:S(2)}, u32[]{:S(2)}) collective-permute-start(bf16[512,512]{1,0:T(8,128)(2,1)S(1)} %constant_dynamic-update-slice_fusion.own_ref), channel_id=1, source_target_pairs={{0,4},{1,5},{2,6},{3,7},{8,12},{9,13},{10,14},{11,15},{16,20},{17,... | collective-permute-start | bytes 1572872 | tf_op jit(solution)/shard_map/ppermute | solution.py:244
  24.4 23.5 %collective-permute-start.3 = (bf16[512,512]{1,0:T(8,128)(2,1)S(1)}, bf16[512,512]{1,0:T(8,128)(2,1)S(1)}, u32[]{:S(2)}, u32[]{:S(2)}) collective-permute-start(bf16[512,512]{1,0:T(8,128)(2,1)S(1)} %collective-permute-done.far_ref), channel_id=1, source_target_pairs={{0,4},{4,0},{1,5},{5,1},{2,6},{6,2},{3,7},{7,3},{8,12},{12,8},{9,1... | collective-permute-start | bytes 1572872 | tf_op jit(solution)/shard_map/ppermute | solution.py:244
  31.4 17.6 %collective-permute-start.2 = (bf16[512,512]{1,0:T(8,128)(2,1)S(1)}, bf16[512,512]{1,0:T(8,128)(2,1)S(1)}, u32[]{:S(2)}, u32[]{:S(2)}) collective-permute-start(bf16[512,512]{1,0:T(8,128)(2,1)S(1)} %collective-permute-done.1.far_ref), channel_id=1, source_target_pairs={{4,0},{5,1},{6,2},{7,3},{12,8},{13,9},{14,10},{15,11},{20,16},{21,... | collective-permute-start | bytes 1572872 | tf_op jit(solution)/shard_map/ppermute | solution.py:244
  35.8 1.2 %copy-start = (bf16[512,1024]{1,0:T(8,128)(2,1)S(1)}, bf16[512,1024]{1,0:T(8,128)(2,1)}, u32[]{:S(2)}) copy-start(bf16[512,1024]{1,0:T(8,128)(2,1)} %q_ref.5) | copy-start | bytes 3145732
  37.0 0.7 copy-start.2
  37.7 10.3 %copy-start.1 = (bf16[512,1024]{1,0:T(8,128)(2,1)S(1)}, bf16[512,1024]{1,0:T(8,128)(2,1)}, u32[]{:S(2)}) copy-start(bf16[512,1024]{1,0:T(8,128)(2,1)} %q_ref.5) | copy-start | bytes 3145732

commit v2 on v0

v2 whole, which is shorter than its diff:
```python
import math

import jax
import jax.numpy as jnp
from jax import lax
from jax.experimental import pallas as pl
from jax.experimental.pallas import tpu as pltpu
from jax.sharding import Mesh
from jax.sharding import PartitionSpec as P

QUERY_HEADS = 32
KEY_VALUE_HEADS = 8
HEAD_WIDTH = 128
GROUP = QUERY_HEADS // KEY_VALUE_HEADS
SEQ = ("seq_0", "seq_1", "seq_2")
SEQ_HEAD = ("seq_0", "seq_1", "seq_2", "head")
ROWS = 512
TILE = 128
TILES = ROWS // TILE
LOCAL_KV = 2
HEADS = LOCAL_KV * GROUP
LOWEST = -1e30
EXP2_SCALE = math.log2(math.e) / math.sqrt(HEAD_WIDTH)
NOWHERE = ROWS


def aligned(start, size):
    return pl.ds(start if isinstance(start, int) else pl.multiple_of(start, size), size)


def tile_rows(tile):
    return aligned(tile * TILE, TILE)


def columns(head):
    return slice(head * HEAD_WIDTH, (head + 1) * HEAD_WIDTH)


def dot(a, b, contract_b):
    return lax.dot_general(
        a, b, (((1,), (contract_b,)), ((), ())), preferred_element_type=jnp.float32
    )


def lane_groups(x):
    return [x[:, i : i + 128] for i in range(0, x.shape[1], 128)]


def folded(op, parts):
    while len(parts) > 1:
        parts = [op(*parts[i : i + 2]) if i + 1 < len(parts) else parts[i] for i in range(0, len(parts), 2)]
    return parts[0]


def widened(x, width):
    return jnp.concatenate([x] * (width // 128), axis=1)


def attend(q_ref, block_ref, tile, width, seen, old, new):
    rows = tile_rows(tile)
    for kv in range(LOCAL_KV):
        k = block_ref[0, 0:width, columns(kv)]
        v = block_ref[1, 0:width, columns(kv)]
        heads = [kv * GROUP + g for g in range(GROUP)]
        q = jnp.concatenate([q_ref[rows, columns(h)] for h in heads], axis=0)
        scores = dot(q, k, 1)
        rounded, states = [], []
        for g, head in enumerate(heads):
            part = jnp.where(seen, scores[g * TILE : (g + 1) * TILE], LOWEST)
            top = jnp.max(folded(jnp.maximum, lane_groups(part)), axis=1, keepdims=True)
            top = jnp.broadcast_to(top, (TILE, 128))
            before = old(head)
            ratio = None
            if before is not None:
                top = jnp.maximum(before[0], top)
                ratio = jnp.exp2((before[0] - top) * EXP2_SCALE)
            weights = jnp.exp2((part - widened(top, width)) * EXP2_SCALE)
            total = folded(jnp.add, lane_groups(weights))
            if before is not None:
                total = before[1] * ratio + total
            states.append((top, total, ratio))
            rounded.append(weights.astype(jnp.bfloat16))
        update = dot(jnp.concatenate(rounded, axis=0), v, 0)
        for g, head in enumerate(heads):
            top, total, ratio = states[g]
            sums = update[g * TILE : (g + 1) * TILE]
            if ratio is not None:
                sums = old(head)[2]() * ratio + sums
            new(head, top, total, sums)


def reader(state, rows):
    acc_ref, top_ref, tot_ref = state
    return lambda head: (
        top_ref[head, rows, :],
        tot_ref[head, rows, :],
        lambda: acc_ref[rows, columns(head)],
    )


def writer(state, rows):
    acc_ref, top_ref, tot_ref = state

    def store(head, top, total, sums):
        top_ref[head, rows, :] = top
        tot_ref[head, rows, :] = total
        acc_ref[rows, columns(head)] = sums

    return store


def attend_earlier(q_ref, block_ref, first_ref, tile, offset, old, new):
    place = (lax.broadcasted_iota(jnp.int32, (TILE, ROWS), 1) + offset).astype(jnp.float32)
    seen = place >= widened(first_ref[tile_rows(tile), :], ROWS)
    attend(q_ref, block_ref, tile, ROWS, seen, old, new)


def reaches(spot_ref, hop_ref, doc_ref, tile, offset):
    floor = spot_ref[0] - hop_ref[0] * ROWS
    earliest = jnp.maximum(doc_ref[tile * TILE], floor) - spot_ref[0]
    return (offset < 0) & (offset + ROWS > earliest)


def pack_kernel(keys_ref, values_ref, out_ref, sems):
    copies = [
        pltpu.make_async_copy(ref, out_ref.at[i], sems.at[i])
        for i, ref in enumerate((keys_ref, values_ref))
    ]
    for copy in copies:
        copy.start()
    for copy in copies:
        copy.wait()


def first_kernel(
    spot_ref, hop_ref, doc_ref, starts_ref, marks_ref, q_ref, own_ref, side_ref,
    acc_ref, top_ref, tot_ref, first_ref, mark_ref,
):
    floor = spot_ref[0] - hop_ref[0] * ROWS
    state = (acc_ref, top_ref, tot_ref)
    for tile in range(TILES):
        width = (tile + 1) * TILE
        rows = tile_rows(tile)
        starts = jnp.maximum(starts_ref[tile : tile + 1, :], floor) - spot_ref[0]
        first = jnp.broadcast_to(starts.astype(jnp.float32), (TILE, 128)).T
        first_ref[rows, :] = first
        marks = marks_ref[tile : tile + 1, :].astype(jnp.float32)
        mark_ref[rows, :] = jnp.broadcast_to(marks, (TILE, 128)).T
        place = lax.broadcasted_iota(jnp.int32, (TILE, width), 1)
        row = lax.broadcasted_iota(jnp.int32, (TILE, width), 0) + tile * TILE
        seen = (place.astype(jnp.float32) >= widened(first, width)) & (place <= row)
        attend(q_ref, own_ref, tile, width, seen, lambda head: None, writer(state, rows))
    offset = jnp.where(spot_ref[1] == 1, -ROWS, NOWHERE)

    def step(tile, carry):
        @pl.when(reaches(spot_ref, hop_ref, doc_ref, tile, offset))
        def _():
            rows = tile_rows(tile)
            attend_earlier(
                q_ref, side_ref, first_ref, tile, offset, reader(state, rows), writer(state, rows)
            )

        return carry

    lax.fori_loop(0, TILES, step, 0)


def copy_tile(source, target, rows, target_rows):
    for head in range(HEADS):
        top, total, sums = reader(source, rows)(head)
        writer(target, target_rows)(head, top, total, sums())


def middle_kernel(
    spot_ref, hop_ref, doc_ref, q_ref, far_ref, side_ref, first_ref, acc_in, top_in, tot_in,
    acc_ref, top_ref, tot_ref,
):
    source, state = (acc_in, top_in, tot_in), (acc_ref, top_ref, tot_ref)
    offsets = (-2 * ROWS, jnp.where(spot_ref[1] == 1, -3 * ROWS, -ROWS))

    def step(tile, carry):
        rows = tile_rows(tile)
        far = reaches(spot_ref, hop_ref, doc_ref, tile, offsets[0])
        side = reaches(spot_ref, hop_ref, doc_ref, tile, offsets[1])

        @pl.when(far)
        def _():
            attend_earlier(
                q_ref, far_ref, first_ref, tile, offsets[0],
                reader(source, rows), writer(state, rows),
            )

        @pl.when(jnp.logical_not(far))
        def _():
            copy_tile(source, state, rows, rows)

        @pl.when(side)
        def _():
            attend_earlier(
                q_ref, side_ref, first_ref, tile, offsets[1],
                reader(state, rows), writer(state, rows),
            )

        return carry

    lax.fori_loop(0, TILES, step, 0)


def last_kernel(
    spot_ref, hop_ref, doc_ref, q_ref, far_ref, side_ref, first_ref, mark_ref, acc_in, top_in,
    tot_in, out_ref, share_ref, acc_ref, top_ref, tot_ref, squares_ref, count_ref,
):
    source, state = (acc_in, top_in, tot_in), (acc_ref, top_ref, tot_ref)
    offsets = (-4 * ROWS, jnp.where(spot_ref[1] == 1, NOWHERE, -3 * ROWS))
    squares_ref[...] = jnp.zeros_like(squares_ref)
    count_ref[...] = jnp.zeros_like(count_ref)
    here = slice(0, TILE)

    def finish(final, rows, tile):
        marks = mark_ref[tile_rows(tile), :]
        squares = jnp.zeros((TILE, HEAD_WIDTH), jnp.float32)
        for head in range(HEADS):
            _, total, sums = reader(final, rows)(head)
            attended = sums() * (1.0 / jnp.sum(total, axis=1, keepdims=True))
            out_ref[tile_rows(tile), columns(head)] = attended.astype(jnp.bfloat16)
            squares += attended * attended
        squares *= marks
        squares_ref[...] += jnp.sum(squares.reshape(TILE // 8, 8, HEAD_WIDTH), axis=0)
        count_ref[...] += jnp.sum(marks.reshape(TILE // 8, 8, 128), axis=0)

    def step(tile, carry):
        rows = tile_rows(tile)
        far = reaches(spot_ref, hop_ref, doc_ref, tile, offsets[0])
        side = reaches(spot_ref, hop_ref, doc_ref, tile, offsets[1])

        @pl.when(far | side)
        def _():
            copy_tile(source, state, rows, here)
            for needed, block_ref, offset in (
                (far, far_ref, offsets[0]),
                (side, side_ref, offsets[1]),
            ):

                @pl.when(needed)
                def _():
                    attend_earlier(
                        q_ref, block_ref, first_ref, tile, offset,
                        reader(state, here), writer(state, here),
                    )

            finish(state, here, tile)

        @pl.when(jnp.logical_not(far | side))
        def _():
            finish(source, rows, tile)

        return carry

    lax.fori_loop(0, TILES, step, 0)
    squares = jnp.sum(squares_ref[...])
    count = jnp.sum(count_ref[...]) * (1.0 / 128)
    lane = lax.broadcasted_iota(jnp.int32, share_ref.shape, 1)
    share_ref[...] = jnp.where(lane == 0, squares, jnp.where(lane == 1, count, 0.0))


def call(kernel, scalars, arrays, out_shapes, flops, scratch=()):
    smem = pl.BlockSpec(memory_space=pltpu.SMEM)
    vmem = pl.BlockSpec(memory_space=pltpu.VMEM)
    return pl.pallas_call(
        kernel,
        out_shape=out_shapes,
        in_specs=[smem] * len(scalars) + [vmem] * len(arrays),
        out_specs=[vmem] * len(out_shapes),
        scratch_shapes=list(scratch),
        compiler_params=pltpu.CompilerParams(vmem_limit_bytes=8 * 1024 * 1024),
        cost_estimate=pl.CostEstimate(flops=flops, bytes_accessed=2**20, transcendentals=2**21),
    )(*scalars, *arrays)


def packed(keys, values):
    return pl.pallas_call(
        pack_kernel,
        out_shape=jax.ShapeDtypeStruct((2, *keys.shape), keys.dtype),
        in_specs=[pl.BlockSpec(memory_space=pltpu.HBM)] * 2,
        out_specs=pl.BlockSpec(memory_space=pltpu.VMEM),
        scratch_shapes=[pltpu.SemaphoreType.DMA((2,))],
        compiler_params=pltpu.CompilerParams(vmem_limit_bytes=4 * 1024 * 1024),
    )(keys, values)


def onward(shard):
    devices = lax.axis_size(SEQ)
    return lax.ppermute(shard, SEQ, [(i, i + 2) for i in range(devices - 2)])


def across(shard, pairs):
    return lax.ppermute(shard, "seq_2", pairs)


def f32(*shape):
    return jax.ShapeDtypeStruct(shape, jnp.float32)


def on_device(queries, keys, values, doc_start, hop_counts, loss_mask):
    spot = jnp.stack([lax.axis_index(SEQ) * ROWS, lax.axis_index("seq_2")])
    scalars = [spot, hop_counts, doc_start]
    own = packed(keys, values)
    far_2 = onward(own)
    side_1 = across(own, [(0, 1)])
    state_shapes = [f32(ROWS, HEADS * HEAD_WIDTH), f32(HEADS, ROWS, 128), f32(HEADS, ROWS, 128)]
    *state, first, mark = call(
        first_kernel,
        scalars,
        [doc_start.reshape(TILES, TILE), loss_mask.reshape(TILES, TILE), queries, own, side_1],
        state_shapes + [f32(ROWS, 128)] * 2,
        2 * 10**9,
    )
    far_4 = onward(far_2)
    side_2 = across(far_2, [(0, 1), (1, 0)])
    state = call(
        middle_kernel, scalars, [queries, far_2, side_2, first, *state], state_shapes, 2 * 10**9
    )
    side_3 = across(far_4, [(1, 0)])
    devices = lax.axis_size(SEQ_HEAD)
    attention, share = call(
        last_kernel,
        scalars,
        [queries, far_4, side_3, first, mark, *state],
        [jax.ShapeDtypeStruct((ROWS, HEADS * HEAD_WIDTH), jnp.bfloat16), f32(devices, 128)],
        10**9,
        scratch=[
            pltpu.VMEM((TILE, HEADS * HEAD_WIDTH), jnp.float32),
            pltpu.VMEM((HEADS, TILE, 128), jnp.float32),
            pltpu.VMEM((HEADS, TILE, 128), jnp.float32),
            pltpu.VMEM((8, 128), jnp.float32),
            pltpu.VMEM((8, 128), jnp.float32),
        ],
    )
    shares = lax.all_to_all(share, SEQ_HEAD, 0, 0, tiled=True)
    sums = jnp.sum(shares, axis=0)
    objective = sums[0] / (QUERY_HEADS * (sums[1] / lax.axis_size("head")))
    return (attention, objective)


def solution(mesh):
    torus = Mesh(
        mesh.devices.reshape(4, 8, 2, mesh.shape["head"]), ("seq_0", "seq_1", "seq_2", "head")
    )
    placed = (P(SEQ, "head"), P(SEQ, "head"), P(SEQ, "head"), P(SEQ), P(SEQ), P(SEQ))

    return jax.shard_map(
        on_device, mesh=torus, in_specs=placed, out_specs=(P(SEQ, "head"), P()), check_vma=False
    )
```

time: 149 us -> 88.6 us (0.59)
  matrix products: 45.9 us -> 0 us
  waiting for transfers between devices: 0.94 us -> 17 us
  other arithmetic: 14.5 us -> 0.36 us
  local copies, waits for them, and re-layouts: 15.7 us -> 5.07 us
  starting transfers between devices: 25.7 us -> 16 us
  Pallas kernels: 0 us -> 9.16 us
  blocking collectives: 41 us -> 36.7 us
    dot_general x10 -> x0, matrix products: 45.9 us -> none  [the longest x5 25.8 us: attend_block(): jnp.einsum('tgqs,sgd->tgqd', rounded, value_block, preferred_element_type...]
    psum x4 -> x0, blocking collectives: 41 us -> none  [over_axes(): return functools.reduce(lax.psum, axes, shard)]
    all_to_all x0 -> x1, blocking collectives: none -> 36.7 us  [on_device(): shares = lax.all_to_all(share, SEQ_HEAD, 0, 0, tiled=True)]
    ppermute x8 -> x5, waiting for transfers between devices: 0.94 us -> 17 us  [the longest x2 17 us: onward(): return lax.ppermute(shard, SEQ, [(i, i + 2) for i in range(devices - 2)])]
    reduce_sum x4 -> x1, other arithmetic: 11.7 us -> 0.29 us  [on_device(): sums = jnp.sum(shares, axis=0)]
    ppermute x8 -> x5, starting transfers between devices: 25.7 us -> 16 us  [the longest x2 8.52 us: onward(): return lax.ppermute(shard, SEQ, [(i, i + 2) for i in range(devices - 2)])]
    pallas_call x0 -> x4, Pallas kernels: none -> 9.16 us  [the longest x3 9.1 us: call(): pl.pallas_call(kernel, out_shape=out_shapes, in_specs=[smem] * len(scalar...]
    ppermute x4 -> x0, local copies, waits for them, and re-layouts: 5.55 us -> none  [passed_along(): return lax.ppermute(shard, axis, pairs)]
  transfers between devices with their start and end apart: 8 -> 5, of which waited for: 1 -> 2; matrix products, arithmetic and copies ran while one was open for 40% -> 0% of each run, Pallas kernels for 0% -> 7%
where the time goes in v2:
time: 88.6 us; the launch traced here: 88.2 us
  blocking collectives  36.7 us (41%)
  waiting for transfers between devices  17 us (19%)
  starting transfers between devices  16 us (18%)
  Pallas kernels  9.16 us (10%)
  local copies, waits for them, and re-layouts  5.07 us (6%)
  between operations  3.8 us (4%)
    all_to_all x1, blocking collectives, on_device(): shares = lax.all_to_all(share, SEQ_HEAD, 0, 0, tiled=True)  36.7 us
    ppermute x2, waiting for transfers between devices, onward(): return lax.ppermute(shard, SEQ, [(i, i + 2) for i in range(devices - 2)])  17 us
    pallas_call x3, Pallas kernels, call(): pl.pallas_call(kernel, out_shape=out_shapes, in_specs=[smem] * len(scalar...  9.1 us
    ppermute x2, starting transfers between devices, onward(): return lax.ppermute(shard, SEQ, [(i, i + 2) for i in range(devices - 2)])  8.52 us
    ppermute x3, starting transfers between devices, across(): return lax.ppermute(shard, 'seq_2', pairs)  7.53 us
    unnamed x12, local copies, waits for them, and re-layouts  4.48 us
  transfers between devices with their start and end apart: 5, of which 2 were waited for; matrix products, arithmetic and copies ran while one was open for 0% of the time, Pallas kernels for 7%

profile of v2, /device:TPU:1, one launch (start us, length us, event | category | flops | bytes accessed | tf_op | source)
XLA Modules:
  0.0 88.2 jit_solution(1869196576314533470)
XLA Ops:
  0.6 0.0 copy-start.2
  0.6 0.9 %copy-done.2 = bf16[512,256]{1,0:T(8,128)(2,1)S(1)} copy-done((bf16[512,256]{1,0:T(8,128)(2,1)S(1)}, bf16[512,256]{1,0:T(8,128)(2,1)}, u32[]{:S(2)}) %copy-start.2) | copy-done | bytes 262168
  1.6 0.9 %copy-done.3 = bf16[512,256]{1,0:T(8,128)(2,1)S(1)} copy-done((bf16[512,256]{1,0:T(8,128)(2,1)S(1)}, bf16[512,256]{1,0:T(8,128)(2,1)}, u32[]{:S(2)}) %copy-start.3) | copy-done | bytes 262168
  2.5 0.1 shard_map.77.own_ref
  2.6 4.4 %collective-permute-start = (bf16[2,512,256]{2,1,0:T(8,128)(2,1)S(1)}, bf16[2,512,256]{2,1,0:T(8,128)(2,1)S(1)}, u32[]{:S(2)}, u32[]{:S(2)}) collective-permute-start(bf16[2,512,256]{2,1,0:T(8,128)(2,1)S(1)} %shard_map.77.own_ref), channel_id=1, source_target_pairs={{0,8},{4,12},{8,16},{12,20},{16,24},{20,28},{24,32},{28,36},{32,40... | collective-permute-start | bytes 1572872 | tf_op jit(solution)/shard_map/ppermute | solution.py:293
  7.0 10.6 %collective-permute-done.far_ref = bf16[2,512,256]{2,1,0:T(8,128)(2,1)S(1)} collective-permute-done((bf16[2,512,256]{2,1,0:T(8,128)(2,1)S(1)}, bf16[2,512,256]{2,1,0:T(8,128)(2,1)S(1)}, u32[]{:S(2)}, u32[]{:S(2)}) %collective-permute-start) | collective-permute-done | bytes 524320 | tf_op jit(solution)/shard_map/ppermute | solution.py:293
  17.6 4.1 %collective-permute-start.1 = (bf16[2,512,256]{2,1,0:T(8,128)(2,1)S(1)}, bf16[2,512,256]{2,1,0:T(8,128)(2,1)S(1)}, u32[]{:S(2)}, u32[]{:S(2)}) collective-permute-start(bf16[2,512,256]{2,1,0:T(8,128)(2,1)S(1)} %collective-permute-done.far_ref), channel_id=1, source_target_pairs={{0,8},{4,12},{8,16},{12,20},{16,24},{20,28},{24,32},{28,36},{32,40... | collective-permute-start | bytes 1572872 | tf_op jit(solution)/shard_map/ppermute | solution.py:293
  21.7 1.3 %collective-permute-start.3 = (bf16[2,512,256]{2,1,0:T(8,128)(2,1)S(1)}, bf16[2,512,256]{2,1,0:T(8,128)(2,1)S(1)}, u32[]{:S(2)}, u32[]{:S(2)}) collective-permute-start(bf16[2,512,256]{2,1,0:T(8,128)(2,1)S(1)} %shard_map.77.own_ref), channel_id=1, source_target_pairs={{0,4},{1,5},{2,6},{3,7},{8,12},{9,13},{10,14},{11,15},{16,20},{17,... | collective-permute-start | bytes 1572872 | tf_op jit(solution)/shard_map/ppermute | solution.py:297
  23.0 1.9 %collective-permute-start.4 = (bf16[2,512,256]{2,1,0:T(8,128)(2,1)S(1)}, bf16[2,512,256]{2,1,0:T(8,128)(2,1)S(1)}, u32[]{:S(2)}, u32[]{:S(2)}) collective-permute-start(bf16[2,512,256]{2,1,0:T(8,128)(2,1)S(1)} %collective-permute-done.far_ref), channel_id=1, source_target_pairs={{0,4},{4,0},{1,5},{5,1},{2,6},{6,2},{3,7},{7,3},{8,12},{12,8},{9,1... | collective-permute-start | bytes 1572872 | tf_op jit(solution)/shard_map/ppermute | solution.py:297
  24.9 6.5 %collective-permute-done.1.far_ref = bf16[2,512,256]{2,1,0:T(8,128)(2,1)S(1)} collective-permute-done((bf16[2,512,256]{2,1,0:T(8,128)(2,1)S(1)}, bf16[2,512,256]{2,1,0:T(8,128)(2,1)S(1)}, u32[]{:S(2)}, u32[]{:S(2)}) %collective-permute-start.1) | collective-permute-done | bytes 524320 | tf_op jit(solution)/shard_map/ppermute | solution.py:293
  31.4 4.3 %collective-permute-start.2 = (bf16[2,512,256]{2,1,0:T(8,128)(2,1)S(1)}, bf16[2,512,256]{2,1,0:T(8,128)(2,1)S(1)}, u32[]{:S(2)}, u32[]{:S(2)}) collective-permute-start(bf16[2,512,256]{2,1,0:T(8,128)(2,1)S(1)} %collective-permute-done.1.far_ref), channel_id=1, source_target_pairs={{4,0},{5,1},{6,2},{7,3},{12,8},{13,9},{14,10},{15,11},{20,16},{21,... | collective-permute-start | bytes 1572872 | tf_op jit(solution)/shard_map/ppermute | solution.py:297
  36.4 0.1 pad_add_fusion.spot_ref
  36.4 0.0 collective-permute-done.3.side_ref
  36.4 1.2 %copy-done = bf16[512,1024]{1,0:T(8,128)(2,1)S(1)} copy-done((bf16[512,1024]{1,0:T(8,128)(2,1)S(1)}, bf16[512,1024]{1,0:T(8,128)(2,1)}, u32[]{:S(2)}) %copy-start) | copy-done | bytes 1048600
  37.7 0.7 copy-done.4
  38.4 0.7 copy-done.5
  39.0 5.4 %shard_map.78 = (f32[512,1024]{1,0:T(8,128)S(1)}, f32[8,512,128]{2,1,0:T(8,128)S(1)}, f32[8,512,128]{2,1,0:T(8,128)S(1)}, f32[512,128]{1,0:T(8,128)S(1)}, f32[512,128]{1,0:T(8,128)S(1)}) custom-call(s32[2]{0:T(128)S(1)} %pad_add_fusion.spot_ref, s32[1]{0:T(128)S(6)} %copy.9.hop_ref, s32[512]{0:T(512)S(1)} %copy-done.4, s32[4,128]{1,0:T(4,128)S(1)} %bitcast.9, ...), custom_call_target="tpu_custom_call" | custom-call | flops 2000000000 | bytes 1048576 | tf_op jit(solution)/shard_map/pallas_call | solution.py:269
  44.4 0.0 collective-permute-done.4.side_ref
  44.4 1.2 %shard_map.79 = (f32[512,1024]{1,0:T(8,128)S(1)}, f32[8,512,128]{2,1,0:T(8,128)S(1)}, f32[8,512,128]{2,1,0:T(8,128)S(1)}) custom-call(s32[2]{0:T(128)S(1)} %pad_add_fusion.spot_ref, s32[1]{0:T(128)S(6)} %copy.9.hop_ref, s32[512]{0:T(512)S(1)} %copy-done.4, bf16[512,1024]{1,0:T(8,128)(2,1)S(1)} %copy-done.1, ...), custom_call_target="tpu_custom_call" | custom-call | flops 2000000000 | bytes 1048576 | tf_op jit(solution)/shard_map/pallas_call | solution.py:269
  45.7 0.0 collective-permute-done.2.side_ref
  45.7 2.5 %shard_map.80 = (bf16[512,1024]{1,0:T(8,128)(2,1)}, f32[256,128]{1,0:T(8,128)S(1)}) custom-call(s32[2]{0:T(128)S(1)} %pad_add_fusion.spot_ref, s32[1]{0:T(128)S(6)} %copy.9.hop_ref, s32[512]{0:T(512)S(1)} %copy-done.4, bf16[512,1024]{1,0:T(8,128)(2,1)S(1)} %copy-done.1, bf16[2,512,256]{2,1,0:T(8,128)(2,1)S(1)} %collective-permute-done.1.far_ref, ...), custom_call_target="tpu_custom_call" | custom-call | flops 1000000000 | bytes 1048576 | tf_op jit(solution)/shard_map/pallas_call | solution.py:269
  48.2 36.7 %all_to_all.9 = f32[256,1,128]{2,1,0:T(1,128)S(1)} all-to-all(f32[256,1,128]{2,1,0:T(1,128)S(1)} %bitcast.8), channel_id=1, replica_groups=mesh['seq_0'=4,'seq_1'=8,'seq_2'=2,'head'=4] {'seq_0','seq_1','seq_2','h..., dimensions={0} | all-to-all | bytes 262144 | tf_op jit(solution)/shard_map/all_to_all | solution.py:339
  84.9 0.3 reduce_sum.9
  85.2 0.6 fusion
  (6 shorter events, 0.0 us)
Async XLA Ops:
  0.6 1.0 %copy-start.2 = (bf16[512,256]{1,0:T(8,128)(2,1)S(1)}, bf16[512,256]{1,0:T(8,128)(2,1)}, u32[]{:S(2)}) copy-start(bf16[512,256]{1,0:T(8,128)(2,1)} %keys_ref.1) | copy-start | bytes 786436
  1.6 0.9 %copy-start.3 = (bf16[512,256]{1,0:T(8,128)(2,1)S(1)}, bf16[512,256]{1,0:T(8,128)(2,1)}, u32[]{:S(2)}) copy-start(bf16[512,256]{1,0:T(8,128)(2,1)} %values_ref.1) | copy-start | bytes 786436
  2.6 15.0 %collective-permute-start = (bf16[2,512,256]{2,1,0:T(8,128)(2,1)S(1)}, bf16[2,512,256]{2,1,0:T(8,128)(2,1)S(1)}, u32[]{:S(2)}, u32[]{:S(2)}) collective-permute-start(bf16[2,512,256]{2,1,0:T(8,128)(2,1)S(1)} %shard_map.77.own_ref), channel_id=1, source_target_pairs={{0,8},{4,12},{8,16},{12,20},{16,24},{20,28},{24,32},{28,36},{32,40... | collective-permute-start | bytes 1572872 | tf_op jit(solution)/shard_map/ppermute | solution.py:293
  17.6 13.8 %collective-permute-start.1 = (bf16[2,512,256]{2,1,0:T(8,128)(2,1)S(1)}, bf16[2,512,256]{2,1,0:T(8,128)(2,1)S(1)}, u32[]{:S(2)}, u32[]{:S(2)}) collective-permute-start(bf16[2,512,256]{2,1,0:T(8,128)(2,1)S(1)} %collective-permute-done.far_ref), channel_id=1, source_target_pairs={{0,8},{4,12},{8,16},{12,20},{16,24},{20,28},{24,32},{28,36},{32,40... | collective-permute-start | bytes 1572872 | tf_op jit(solution)/shard_map/ppermute | solution.py:293
  21.7 14.8 %collective-permute-start.3 = (bf16[2,512,256]{2,1,0:T(8,128)(2,1)S(1)}, bf16[2,512,256]{2,1,0:T(8,128)(2,1)S(1)}, u32[]{:S(2)}, u32[]{:S(2)}) collective-permute-start(bf16[2,512,256]{2,1,0:T(8,128)(2,1)S(1)} %shard_map.77.own_ref), channel_id=1, source_target_pairs={{0,4},{1,5},{2,6},{3,7},{8,12},{9,13},{10,14},{11,15},{16,20},{17,... | collective-permute-start | bytes 1572872 | tf_op jit(solution)/shard_map/ppermute | solution.py:297
  23.0 21.4 %collective-permute-start.4 = (bf16[2,512,256]{2,1,0:T(8,128)(2,1)S(1)}, bf16[2,512,256]{2,1,0:T(8,128)(2,1)S(1)}, u32[]{:S(2)}, u32[]{:S(2)}) collective-permute-start(bf16[2,512,256]{2,1,0:T(8,128)(2,1)S(1)} %collective-permute-done.far_ref), channel_id=1, source_target_pairs={{0,4},{4,0},{1,5},{5,1},{2,6},{6,2},{3,7},{7,3},{8,12},{12,8},{9,1... | collective-permute-start | bytes 1572872 | tf_op jit(solution)/shard_map/ppermute | solution.py:297
  31.4 14.3 %collective-permute-start.2 = (bf16[2,512,256]{2,1,0:T(8,128)(2,1)S(1)}, bf16[2,512,256]{2,1,0:T(8,128)(2,1)S(1)}, u32[]{:S(2)}, u32[]{:S(2)}) collective-permute-start(bf16[2,512,256]{2,1,0:T(8,128)(2,1)S(1)} %collective-permute-done.1.far_ref), channel_id=1, source_target_pairs={{4,0},{5,1},{6,2},{7,3},{12,8},{13,9},{14,10},{15,11},{20,16},{21,... | collective-permute-start | bytes 1572872 | tf_op jit(solution)/shard_map/ppermute | solution.py:297
  36.4 1.2 %copy-start = (bf16[512,1024]{1,0:T(8,128)(2,1)S(1)}, bf16[512,1024]{1,0:T(8,128)(2,1)}, u32[]{:S(2)}) copy-start(bf16[512,1024]{1,0:T(8,128)(2,1)} %q_ref.5) | copy-start | bytes 3145732
  37.7 0.7 copy-start.4
  38.4 0.7 copy-start.5
  39.0 5.4 %copy-start.1 = (bf16[512,1024]{1,0:T(8,128)(2,1)S(1)}, bf16[512,1024]{1,0:T(8,128)(2,1)}, u32[]{:S(2)}) copy-start(bf16[512,1024]{1,0:T(8,128)(2,1)} %q_ref.5) | copy-start | bytes 3145732

commit v3 on v2

--- a/solution.py
+++ b/solution.py
@@ -1,3 +1,4 @@
+import functools
 import math
 
 import jax
@@ -133,7 +134,7 @@
 
 
 def first_kernel(
-    spot_ref, hop_ref, doc_ref, starts_ref, marks_ref, q_ref, own_ref, side_ref,
+    spot_ref, hop_ref, doc_ref, starts_ref, marks_ref, q_ref, own_ref,
     acc_ref, top_ref, tot_ref, first_ref, mark_ref,
 ):
     floor = spot_ref[0] - hop_ref[0] * ROWS
@@ -150,19 +151,6 @@
         row = lax.broadcasted_iota(jnp.int32, (TILE, width), 0) + tile * TILE
         seen = (place.astype(jnp.float32) >= widened(first, width)) & (place <= row)
         attend(q_ref, own_ref, tile, width, seen, lambda head: None, writer(state, rows))
-    offset = jnp.where(spot_ref[1] == 1, -ROWS, NOWHERE)
-
-    def step(tile, carry):
-        @pl.when(reaches(spot_ref, hop_ref, doc_ref, tile, offset))
-        def _():
-            rows = tile_rows(tile)
-            attend_earlier(
-                q_ref, side_ref, first_ref, tile, offset, reader(state, rows), writer(state, rows)
-            )
-
-        return carry
-
-    lax.fori_loop(0, TILES, step, 0)
 
 
 def copy_tile(source, target, rows, target_rows):
@@ -171,35 +159,52 @@
         writer(target, target_rows)(head, top, total, sums())
 
 
+def finish(state, rows, mark_ref, out_ref, squares_ref, tile):
+    marks = mark_ref[tile_rows(tile), :]
+    squares = jnp.zeros((TILE, HEAD_WIDTH), jnp.float32)
+    for head in range(HEADS):
+        _, total, sums = reader(state, rows)(head)
+        attended = sums() * (1.0 / jnp.sum(total, axis=1, keepdims=True))
+        out_ref[tile_rows(tile), columns(head)] = attended.astype(jnp.bfloat16)
+        squares += attended * attended
+    squares *= marks
+    squares_ref[...] += jnp.sum(squares.reshape(TILE // 8, 8, HEAD_WIDTH), axis=0)
+
+
+def last_offsets(spot_ref):
+    return (-4 * ROWS, jnp.where(spot_ref[1] == 1, NOWHERE, -3 * ROWS))
+
+
 def middle_kernel(
-    spot_ref, hop_ref, doc_ref, q_ref, far_ref, side_ref, first_ref, acc_in, top_in, tot_in,
-    acc_ref, top_ref, tot_ref,
+    spot_ref, hop_ref, doc_ref, q_ref, near_ref, far_ref, side_ref, first_ref, mark_ref,
+    acc_in, top_in, tot_in, acc_ref, top_ref, tot_ref, out_ref, squares_ref,
 ):
     source, state = (acc_in, top_in, tot_in), (acc_ref, top_ref, tot_ref)
-    offsets = (-2 * ROWS, jnp.where(spot_ref[1] == 1, -3 * ROWS, -ROWS))
+    odd = spot_ref[1] == 1
+    slots = (
+        (near_ref, jnp.where(odd, -ROWS, NOWHERE)),
+        (far_ref, -2 * ROWS),
+        (side_ref, jnp.where(odd, -3 * ROWS, -ROWS)),
+    )
+    squares_ref[...] = jnp.zeros_like(squares_ref)
 
     def step(tile, carry):
         rows = tile_rows(tile)
-        far = reaches(spot_ref, hop_ref, doc_ref, tile, offsets[0])
-        side = reaches(spot_ref, hop_ref, doc_ref, tile, offsets[1])
-
-        @pl.when(far)
+        copy_tile(source, state, rows, rows)
+        for block_ref, offset in slots:
+
+            @pl.when(reaches(spot_ref, hop_ref, doc_ref, tile, offset))
+            def _():
+                attend_earlier(
+                    q_ref, block_ref, first_ref, tile, offset,
+                    reader(state, rows), writer(state, rows),
+                )
+
+        late = [reaches(spot_ref, hop_ref, doc_ref, tile, o) for o in last_offsets(spot_ref)]
+
+        @pl.when(jnp.logical_not(late[0] | late[1]))
         def _():
-            attend_earlier(
-                q_ref, far_ref, first_ref, tile, offsets[0],
-                reader(source, rows), writer(state, rows),
-            )
-
-        @pl.when(jnp.logical_not(far))
-        def _():
-            copy_tile(source, state, rows, rows)
-
-        @pl.when(side)
-        def _():
-            attend_earlier(
-                q_ref, side_ref, first_ref, tile, offsets[1],
-                reader(state, rows), writer(state, rows),
-            )
+            finish(state, rows, mark_ref, out_ref, squares_ref, tile)
 
         return carry
 
@@ -208,38 +213,21 @@
 
 def last_kernel(
     spot_ref, hop_ref, doc_ref, q_ref, far_ref, side_ref, first_ref, mark_ref, acc_in, top_in,
-    tot_in, out_ref, share_ref, acc_ref, top_ref, tot_ref, squares_ref, count_ref,
+    tot_in, done_ref, squares_in, out_ref, share_ref, acc_ref, top_ref, tot_ref, squares_ref,
 ):
     source, state = (acc_in, top_in, tot_in), (acc_ref, top_ref, tot_ref)
-    offsets = (-4 * ROWS, jnp.where(spot_ref[1] == 1, NOWHERE, -3 * ROWS))
-    squares_ref[...] = jnp.zeros_like(squares_ref)
-    count_ref[...] = jnp.zeros_like(count_ref)
+    offsets = last_offsets(spot_ref)
+    squares_ref[...] = squares_in[...]
     here = slice(0, TILE)
-
-    def finish(final, rows, tile):
-        marks = mark_ref[tile_rows(tile), :]
-        squares = jnp.zeros((TILE, HEAD_WIDTH), jnp.float32)
-        for head in range(HEADS):
-            _, total, sums = reader(final, rows)(head)
-            attended = sums() * (1.0 / jnp.sum(total, axis=1, keepdims=True))
-            out_ref[tile_rows(tile), columns(head)] = attended.astype(jnp.bfloat16)
-            squares += attended * attended
-        squares *= marks
-        squares_ref[...] += jnp.sum(squares.reshape(TILE // 8, 8, HEAD_WIDTH), axis=0)
-        count_ref[...] += jnp.sum(marks.reshape(TILE // 8, 8, 128), axis=0)
 
     def step(tile, carry):
         rows = tile_rows(tile)
-        far = reaches(spot_ref, hop_ref, doc_ref, tile, offsets[0])
-        side = reaches(spot_ref, hop_ref, doc_ref, tile, offsets[1])
-
-        @pl.when(far | side)
+        late = [reaches(spot_ref, hop_ref, doc_ref, tile, offset) for offset in offsets]
+
+        @pl.when(late[0] | late[1])
         def _():
             copy_tile(source, state, rows, here)
-            for needed, block_ref, offset in (
-                (far, far_ref, offsets[0]),
-                (side, side_ref, offsets[1]),
-            ):
+            for needed, block_ref, offset in zip(late, (far_ref, side_ref), offsets):
 
                 @pl.when(needed)
                 def _():
@@ -248,17 +236,17 @@
                         reader(state, here), writer(state, here),
                     )
 
-            finish(state, here, tile)
-
-        @pl.when(jnp.logical_not(far | side))
+            finish(state, here, mark_ref, out_ref, squares_ref, tile)
+
+        @pl.when(jnp.logical_not(late[0] | late[1]))
         def _():
-            finish(source, rows, tile)
+            out_ref[rows, :] = done_ref[rows, :]
 
         return carry
 
     lax.fori_loop(0, TILES, step, 0)
     squares = jnp.sum(squares_ref[...])
-    count = jnp.sum(count_ref[...]) * (1.0 / 128)
+    count = jnp.sum(jnp.sum(mark_ref[...].reshape(ROWS // 8, 8, 128), axis=0)) * (1.0 / 128)
     lane = lax.broadcasted_iota(jnp.int32, share_ref.shape, 1)
     share_ref[...] = jnp.where(lane == 0, squares, jnp.where(lane == 1, count, 0.0))
 
@@ -288,6 +276,24 @@
     )(keys, values)
 
 
+def objective_kernel(copies, shares_ref, out_ref):
+    sums = jnp.sum(shares_ref[...], axis=0, keepdims=True)
+    lane = lax.broadcasted_iota(jnp.int32, sums.shape, 1)
+    squares = jnp.sum(jnp.where(lane == 0, sums, 0.0))
+    count = jnp.sum(jnp.where(lane == 1, sums, 0.0)) * (1.0 / copies)
+    out_ref[0] = squares / (QUERY_HEADS * count)
+
+
+def objective_of(shares, copies):
+    return pl.pallas_call(
+        functools.partial(objective_kernel, copies),
+        out_shape=f32(1),
+        in_specs=[pl.BlockSpec(memory_space=pltpu.VMEM)],
+        out_specs=pl.BlockSpec(memory_space=pltpu.SMEM),
+        compiler_params=pltpu.CompilerParams(vmem_limit_bytes=4 * 1024 * 1024),
+    )(shares).reshape(())
+
+
 def onward(shard):
     devices = lax.axis_size(SEQ)
     return lax.ppermute(shard, SEQ, [(i, i + 2) for i in range(devices - 2)])
@@ -311,35 +317,37 @@
     *state, first, mark = call(
         first_kernel,
         scalars,
-        [doc_start.reshape(TILES, TILE), loss_mask.reshape(TILES, TILE), queries, own, side_1],
+        [doc_start.reshape(TILES, TILE), loss_mask.reshape(TILES, TILE), queries, own],
         state_shapes + [f32(ROWS, 128)] * 2,
         2 * 10**9,
     )
     far_4 = onward(far_2)
     side_2 = across(far_2, [(0, 1), (1, 0)])
-    state = call(
-        middle_kernel, scalars, [queries, far_2, side_2, first, *state], state_shapes, 2 * 10**9
+    out_shape = jax.ShapeDtypeStruct((ROWS, HEADS * HEAD_WIDTH), jnp.bfloat16)
+    *state, done, squares = call(
+        middle_kernel,
+        scalars,
+        [queries, side_1, far_2, side_2, first, mark, *state],
+        state_shapes + [out_shape, f32(8, 128)],
+        2 * 10**9,
     )
     side_3 = across(far_4, [(1, 0)])
     devices = lax.axis_size(SEQ_HEAD)
     attention, share = call(
         last_kernel,
         scalars,
-        [queries, far_4, side_3, first, mark, *state],
-        [jax.ShapeDtypeStruct((ROWS, HEADS * HEAD_WIDTH), jnp.bfloat16), f32(devices, 128)],
+        [queries, far_4, side_3, first, mark, *state, done, squares],
+        [out_shape, f32(devices, 128)],
         10**9,
         scratch=[
             pltpu.VMEM((TILE, HEADS * HEAD_WIDTH), jnp.float32),
             pltpu.VMEM((HEADS, TILE, 128), jnp.float32),
             pltpu.VMEM((HEADS, TILE, 128), jnp.float32),
             pltpu.VMEM((8, 128), jnp.float32),
-            pltpu.VMEM((8, 128), jnp.float32),
         ],
     )
     shares = lax.all_to_all(share, SEQ_HEAD, 0, 0, tiled=True)
-    sums = jnp.sum(shares, axis=0)
-    objective = sums[0] / (QUERY_HEADS * (sums[1] / lax.axis_size("head")))
-    return (attention, objective)
+    return (attention, objective_of(shares, lax.axis_size("head")))
 
 
 def solution(mesh):

time: 88.6 us -> 86.7 us (0.979)
  between operations: 3.8 us -> 1.4 us
    unnamed x12 -> x14, local copies, waits for them, and re-layouts: 4.48 us -> 4.49 us
  transfers between devices with their start and end apart: 5 -> 5, of which waited for: 2 -> 2; matrix products, arithmetic and copies ran while one was open for 0% -> 0% of each run, Pallas kernels for 7% -> 9%
where the time goes in v3:
time: 86.7 us; the launch traced here: 86.4 us
  blocking collectives  37.3 us (43%)
  waiting for transfers between devices  17 us (20%)
  starting transfers between devices  16 us (18%)
  Pallas kernels  9.99 us (12%)
  local copies, waits for them, and re-layouts  4.49 us (5%)
  between operations  1.4 us (2%)
    all_to_all x1, blocking collectives, on_device(): shares = lax.all_to_all(share, SEQ_HEAD, 0, 0, tiled=True)  37.3 us
    ppermute x2, waiting for transfers between devices, onward(): return lax.ppermute(shard, SEQ, [(i, i + 2) for i in range(devices - 2)])  17 us
    pallas_call x3, Pallas kernels, call(): pl.pallas_call(kernel, out_shape=out_shapes, in_specs=[smem] * len(scalar...  9.21 us
    ppermute x2, starting transfers between devices, onward(): return lax.ppermute(shard, SEQ, [(i, i + 2) for i in range(devices - 2)])  8.52 us
    ppermute x3, starting transfers between devices, across(): return lax.ppermute(shard, 'seq_2', pairs)  7.53 us
    unnamed x14, local copies, waits for them, and re-layouts  4.49 us
  transfers between devices with their start and end apart: 5, of which 2 were waited for; matrix products, arithmetic and copies ran while one was open for 0% of the time, Pallas kernels for 9%

profile of v3, /device:TPU:1, one launch (start us, length us, event | category | flops | bytes accessed | tf_op | source)
XLA Modules:
  0.0 86.4 jit_solution(12183620484177582758)
XLA Ops:
  0.6 0.9 %copy-done.2 = bf16[512,256]{1,0:T(8,128)(2,1)S(1)} copy-done((bf16[512,256]{1,0:T(8,128)(2,1)S(1)}, bf16[512,256]{1,0:T(8,128)(2,1)}, u32[]{:S(2)}) %copy-start.2) | copy-done | bytes 262168
  1.6 0.9 %copy-done.3 = bf16[512,256]{1,0:T(8,128)(2,1)S(1)} copy-done((bf16[512,256]{1,0:T(8,128)(2,1)S(1)}, bf16[512,256]{1,0:T(8,128)(2,1)}, u32[]{:S(2)}) %copy-start.3) | copy-done | bytes 262168
  2.5 0.1 shard_map.77.own_ref
  2.6 4.4 %collective-permute-start = (bf16[2,512,256]{2,1,0:T(8,128)(2,1)S(1)}, bf16[2,512,256]{2,1,0:T(8,128)(2,1)S(1)}, u32[]{:S(2)}, u32[]{:S(2)}) collective-permute-start(bf16[2,512,256]{2,1,0:T(8,128)(2,1)S(1)} %shard_map.77.own_ref), channel_id=1, source_target_pairs={{0,8},{4,12},{8,16},{12,20},{16,24},{20,28},{24,32},{28,36},{32,40... | collective-permute-start | bytes 1572872 | tf_op jit(solution)/shard_map/ppermute | solution.py:299
  7.0 10.6 %collective-permute-done.far_ref = bf16[2,512,256]{2,1,0:T(8,128)(2,1)S(1)} collective-permute-done((bf16[2,512,256]{2,1,0:T(8,128)(2,1)S(1)}, bf16[2,512,256]{2,1,0:T(8,128)(2,1)S(1)}, u32[]{:S(2)}, u32[]{:S(2)}) %collective-permute-start) | collective-permute-done | bytes 524320 | tf_op jit(solution)/shard_map/ppermute | solution.py:299
  17.6 4.1 %collective-permute-start.1 = (bf16[2,512,256]{2,1,0:T(8,128)(2,1)S(1)}, bf16[2,512,256]{2,1,0:T(8,128)(2,1)S(1)}, u32[]{:S(2)}, u32[]{:S(2)}) collective-permute-start(bf16[2,512,256]{2,1,0:T(8,128)(2,1)S(1)} %collective-permute-done.far_ref), channel_id=1, source_target_pairs={{0,8},{4,12},{8,16},{12,20},{16,24},{20,28},{24,32},{28,36},{32,40... | collective-permute-start | bytes 1572872 | tf_op jit(solution)/shard_map/ppermute | solution.py:299
  21.7 1.3 %collective-permute-start.3 = (bf16[2,512,256]{2,1,0:T(8,128)(2,1)S(1)}, bf16[2,512,256]{2,1,0:T(8,128)(2,1)S(1)}, u32[]{:S(2)}, u32[]{:S(2)}) collective-permute-start(bf16[2,512,256]{2,1,0:T(8,128)(2,1)S(1)} %shard_map.77.own_ref), channel_id=1, source_target_pairs={{0,4},{1,5},{2,6},{3,7},{8,12},{9,13},{10,14},{11,15},{16,20},{17,... | collective-permute-start | bytes 1572872 | tf_op jit(solution)/shard_map/ppermute | solution.py:303
  23.0 1.9 %collective-permute-start.4 = (bf16[2,512,256]{2,1,0:T(8,128)(2,1)S(1)}, bf16[2,512,256]{2,1,0:T(8,128)(2,1)S(1)}, u32[]{:S(2)}, u32[]{:S(2)}) collective-permute-start(bf16[2,512,256]{2,1,0:T(8,128)(2,1)S(1)} %collective-permute-done.far_ref), channel_id=1, source_target_pairs={{0,4},{4,0},{1,5},{5,1},{2,6},{6,2},{3,7},{7,3},{8,12},{12,8},{9,1... | collective-permute-start | bytes 1572872 | tf_op jit(solution)/shard_map/ppermute | solution.py:303
  24.9 6.5 %collective-permute-done.1.far_ref = bf16[2,512,256]{2,1,0:T(8,128)(2,1)S(1)} collective-permute-done((bf16[2,512,256]{2,1,0:T(8,128)(2,1)S(1)}, bf16[2,512,256]{2,1,0:T(8,128)(2,1)S(1)}, u32[]{:S(2)}, u32[]{:S(2)}) %collective-permute-start.1) | collective-permute-done | bytes 524320 | tf_op jit(solution)/shard_map/ppermute | solution.py:299
  31.4 4.3 %collective-permute-start.2 = (bf16[2,512,256]{2,1,0:T(8,128)(2,1)S(1)}, bf16[2,512,256]{2,1,0:T(8,128)(2,1)S(1)}, u32[]{:S(2)}, u32[]{:S(2)}) collective-permute-start(bf16[2,512,256]{2,1,0:T(8,128)(2,1)S(1)} %collective-permute-done.1.far_ref), channel_id=1, source_target_pairs={{4,0},{5,1},{6,2},{7,3},{12,8},{13,9},{14,10},{15,11},{20,16},{21,... | collective-permute-start | bytes 1572872 | tf_op jit(solution)/shard_map/ppermute | solution.py:303
  36.4 0.1 pad_add_fusion.spot_ref
  36.4 1.2 %copy-done = bf16[512,1024]{1,0:T(8,128)(2,1)S(1)} copy-done((bf16[512,1024]{1,0:T(8,128)(2,1)S(1)}, bf16[512,1024]{1,0:T(8,128)(2,1)}, u32[]{:S(2)}) %copy-start) | copy-done | bytes 1048600
  37.7 0.7 copy-done.4
  38.3 0.7 copy-done.6
  39.0 3.1 %shard_map.78 = (f32[512,1024]{1,0:T(8,128)S(1)}, f32[8,512,128]{2,1,0:T(8,128)S(1)}, f32[8,512,128]{2,1,0:T(8,128)S(1)}, f32[512,128]{1,0:T(8,128)S(1)}, f32[512,128]{1,0:T(8,128)S(1)}) custom-call(s32[2]{0:T(128)S(1)} %pad_add_fusion.spot_ref, s32[1]{0:T(128)S(6)} %copy.9.hop_ref, s32[512]{0:T(512)S(1)} %copy-done.4, s32[4,128]{1,0:T(4,128)S(1)} %bitcast.11, ...), custom_call_target="tpu_custom_call" | custom-call | flops 2000000000 | bytes 1048576 | tf_op jit(solution)/shard_map/pallas_call | solution.py:257
  42.2 0.0 collective-permute-done.3.near_ref
  42.2 0.0 collective-permute-done.4.side_ref
  42.2 0.0 copy-done.1
  42.2 0.0 copy-done.5
  42.2 4.4 %shard_map.79 = (f32[512,1024]{1,0:T(8,128)S(1)}, f32[8,512,128]{2,1,0:T(8,128)S(1)}, f32[8,512,128]{2,1,0:T(8,128)S(1)}, bf16[512,1024]{1,0:T(8,128)(2,1)S(1)}, f32[8,128]{1,0:T(8,128)S(1)}) custom-call(s32[2]{0:T(128)S(1)} %pad_add_fusion.spot_ref, s32[1]{0:T(128)S(6)} %copy.9.hop_ref, s32[512]{0:T(512)S(1)} %copy-done.5, bf16[512,1024]{1,0:T(8,128)(2,1)S(1)} %copy-done.1, ...), custom_call_target="tpu_custom_call" | custom-call | flops 2000000000 | bytes 1048576 | tf_op jit(solution)/shard_map/pallas_call | solution.py:257
  46.6 0.0 collective-permute-done.2.side_ref
  46.6 1.7 %shard_map.80 = (bf16[512,1024]{1,0:T(8,128)(2,1)}, f32[256,128]{1,0:T(8,128)S(1)}) custom-call(s32[2]{0:T(128)S(1)} %pad_add_fusion.spot_ref, s32[1]{0:T(128)S(6)} %copy.9.hop_ref, s32[512]{0:T(512)S(1)} %copy-done.5, bf16[512,1024]{1,0:T(8,128)(2,1)S(1)} %copy-done.1, bf16[2,512,256]{2,1,0:T(8,128)(2,1)S(1)} %collective-permute-done.1.far_ref, ...), custom_call_target="tpu_custom_call" | custom-call | flops 1000000000 | bytes 1048576 | tf_op jit(solution)/shard_map/pallas_call | solution.py:257
  48.3 37.3 %all_to_all.11 = f32[256,1,128]{2,1,0:T(1,128)S(1)} all-to-all(f32[256,1,128]{2,1,0:T(1,128)S(1)} %bitcast.10), channel_id=1, replica_groups=mesh['seq_0'=4,'seq_1'=8,'seq_2'=2,'head'=4] {'seq_0','seq_1','seq_2','h..., dimensions={0} | all-to-all | bytes 262144 | tf_op jit(solution)/shard_map/all_to_all | solution.py:349
  85.6 0.7 shard_map.81
  (7 shorter events, 0.0 us)
Async XLA Ops:
  0.6 1.0 %copy-start.2 = (bf16[512,256]{1,0:T(8,128)(2,1)S(1)}, bf16[512,256]{1,0:T(8,128)(2,1)}, u32[]{:S(2)}) copy-start(bf16[512,256]{1,0:T(8,128)(2,1)} %keys_ref.1) | copy-start | bytes 786436
  1.6 0.9 %copy-start.3 = (bf16[512,256]{1,0:T(8,128)(2,1)S(1)}, bf16[512,256]{1,0:T(8,128)(2,1)}, u32[]{:S(2)}) copy-start(bf16[512,256]{1,0:T(8,128)(2,1)} %values_ref.1) | copy-start | bytes 786436
  2.6 15.0 %collective-permute-start = (bf16[2,512,256]{2,1,0:T(8,128)(2,1)S(1)}, bf16[2,512,256]{2,1,0:T(8,128)(2,1)S(1)}, u32[]{:S(2)}, u32[]{:S(2)}) collective-permute-start(bf16[2,512,256]{2,1,0:T(8,128)(2,1)S(1)} %shard_map.77.own_ref), channel_id=1, source_target_pairs={{0,8},{4,12},{8,16},{12,20},{16,24},{20,28},{24,32},{28,36},{32,40... | collective-permute-start | bytes 1572872 | tf_op jit(solution)/shard_map/ppermute | solution.py:299
  17.6 13.8 %collective-permute-start.1 = (bf16[2,512,256]{2,1,0:T(8,128)(2,1)S(1)}, bf16[2,512,256]{2,1,0:T(8,128)(2,1)S(1)}, u32[]{:S(2)}, u32[]{:S(2)}) collective-permute-start(bf16[2,512,256]{2,1,0:T(8,128)(2,1)S(1)} %collective-permute-done.far_ref), channel_id=1, source_target_pairs={{0,8},{4,12},{8,16},{12,20},{16,24},{20,28},{24,32},{28,36},{32,40... | collective-permute-start | bytes 1572872 | tf_op jit(solution)/shard_map/ppermute | solution.py:299
  21.7 20.5 %collective-permute-start.3 = (bf16[2,512,256]{2,1,0:T(8,128)(2,1)S(1)}, bf16[2,512,256]{2,1,0:T(8,128)(2,1)S(1)}, u32[]{:S(2)}, u32[]{:S(2)}) collective-permute-start(bf16[2,512,256]{2,1,0:T(8,128)(2,1)S(1)} %shard_map.77.own_ref), channel_id=1, source_target_pairs={{0,4},{1,5},{2,6},{3,7},{8,12},{9,13},{10,14},{11,15},{16,20},{17,... | collective-permute-start | bytes 1572872 | tf_op jit(solution)/shard_map/ppermute | solution.py:303
  23.0 19.2 %collective-permute-start.4 = (bf16[2,512,256]{2,1,0:T(8,128)(2,1)S(1)}, bf16[2,512,256]{2,1,0:T(8,128)(2,1)S(1)}, u32[]{:S(2)}, u32[]{:S(2)}) collective-permute-start(bf16[2,512,256]{2,1,0:T(8,128)(2,1)S(1)} %collective-permute-done.far_ref), channel_id=1, source_target_pairs={{0,4},{4,0},{1,5},{5,1},{2,6},{6,2},{3,7},{7,3},{8,12},{12,8},{9,1... | collective-permute-start | bytes 1572872 | tf_op jit(solution)/shard_map/ppermute | solution.py:303
  31.4 15.2 %collective-permute-start.2 = (bf16[2,512,256]{2,1,0:T(8,128)(2,1)S(1)}, bf16[2,512,256]{2,1,0:T(8,128)(2,1)S(1)}, u32[]{:S(2)}, u32[]{:S(2)}) collective-permute-start(bf16[2,512,256]{2,1,0:T(8,128)(2,1)S(1)} %collective-permute-done.1.far_ref), channel_id=1, source_target_pairs={{4,0},{5,1},{6,2},{7,3},{12,8},{13,9},{14,10},{15,11},{20,16},{21,... | collective-permute-start | bytes 1572872 | tf_op jit(solution)/shard_map/ppermute | solution.py:303
  36.4 1.2 %copy-start = (bf16[512,1024]{1,0:T(8,128)(2,1)S(1)}, bf16[512,1024]{1,0:T(8,128)(2,1)}, u32[]{:S(2)}) copy-start(bf16[512,1024]{1,0:T(8,128)(2,1)} %q_ref.5) | copy-start | bytes 3145732
  37.7 0.7 copy-start.4
  38.3 0.7 copy-start.6
  39.0 3.2 %copy-start.1 = (bf16[512,1024]{1,0:T(8,128)(2,1)S(1)}, bf16[512,1024]{1,0:T(8,128)(2,1)}, u32[]{:S(2)}) copy-start(bf16[512,1024]{1,0:T(8,128)(2,1)} %q_ref.5) | copy-start | bytes 3145732
  39.0 3.2 %copy-start.5 = (s32[512]{0:T(512)S(1)}, s32[512]{0:T(512)}, u32[]{:S(2)}) copy-start(s32[512]{0:T(512)} %doc_ref.5) | copy-start | bytes 6148

commit v4 on v3

--- a/solution.py
+++ b/solution.py
@@ -43,6 +43,10 @@
     )
 
 
+def heads_of(kv):
+    return range(kv * GROUP, (kv + 1) * GROUP)
+
+
 def lane_groups(x):
     return [x[:, i : i + 128] for i in range(0, x.shape[1], 128)]
 
@@ -59,14 +63,14 @@
 
 def attend(q_ref, block_ref, tile, width, seen, old, new):
     rows = tile_rows(tile)
-    for kv in range(LOCAL_KV):
-        k = block_ref[0, 0:width, columns(kv)]
-        v = block_ref[1, 0:width, columns(kv)]
-        heads = [kv * GROUP + g for g in range(GROUP)]
-        q = jnp.concatenate([q_ref[rows, columns(h)] for h in heads], axis=0)
-        scores = dot(q, k, 1)
+
+    def score(kv):
+        q = jnp.concatenate([q_ref[rows, columns(h)] for h in heads_of(kv)], axis=0)
+        return dot(q, block_ref[0, 0:width, columns(kv)], 1)
+
+    def weigh(kv, scores):
         rounded, states = [], []
-        for g, head in enumerate(heads):
+        for g, head in enumerate(heads_of(kv)):
             part = jnp.where(seen, scores[g * TILE : (g + 1) * TILE], LOWEST)
             top = jnp.max(folded(jnp.maximum, lane_groups(part)), axis=1, keepdims=True)
             top = jnp.broadcast_to(top, (TILE, 128))
@@ -76,18 +80,31 @@
                 top = jnp.maximum(before[0], top)
                 ratio = jnp.exp2((before[0] - top) * EXP2_SCALE)
             weights = jnp.exp2((part - widened(top, width)) * EXP2_SCALE)
-            total = folded(jnp.add, lane_groups(weights))
-            if before is not None:
-                total = before[1] * ratio + total
-            states.append((top, total, ratio))
+            states.append((top, ratio))
             rounded.append(weights.astype(jnp.bfloat16))
-        update = dot(jnp.concatenate(rounded, axis=0), v, 0)
-        for g, head in enumerate(heads):
-            top, total, ratio = states[g]
-            sums = update[g * TILE : (g + 1) * TILE]
+        return jnp.concatenate(rounded, axis=0), states
+
+    def add(kv, rounded, states):
+        v = block_ref[1, 0:width, columns(kv)]
+        update = dot(rounded, jnp.concatenate([v, jnp.ones_like(v)], axis=1), 0)
+        for g, head in enumerate(heads_of(kv)):
+            top, ratio = states[g]
+            part = update[g * TILE : (g + 1) * TILE]
+            sums, total = part[:, 0:HEAD_WIDTH], part[:, HEAD_WIDTH:]
             if ratio is not None:
-                sums = old(head)[2]() * ratio + sums
+                _, total_old, sums_old = old(head)
+                sums, total = sums_old() * ratio + sums, total_old * ratio + total
             new(head, top, total, sums)
+
+    scores = score(0)
+    pending = None
+    for kv in range(LOCAL_KV):
+        ahead = score(kv + 1) if kv + 1 < LOCAL_KV else None
+        weighed = weigh(kv, scores)
+        if pending is not None:
+            add(*pending)
+        scores, pending = ahead, (kv, *weighed)
+    add(*pending)
 
 
 def reader(state, rows):
@@ -164,7 +181,7 @@
     squares = jnp.zeros((TILE, HEAD_WIDTH), jnp.float32)
     for head in range(HEADS):
         _, total, sums = reader(state, rows)(head)
-        attended = sums() * (1.0 / jnp.sum(total, axis=1, keepdims=True))
+        attended = sums() * (1.0 / total)
         out_ref[tile_rows(tile), columns(head)] = attended.astype(jnp.bfloat16)
         squares += attended * attended
     squares *= marks
@@ -175,14 +192,40 @@
     return (-4 * ROWS, jnp.where(spot_ref[1] == 1, NOWHERE, -3 * ROWS))
 
 
+def near_kernel(
+    spot_ref, hop_ref, doc_ref, q_ref, near_ref, first_ref, acc_in, top_in, tot_in,
+    acc_ref, top_ref, tot_ref,
+):
+    source, state = (acc_in, top_in, tot_in), (acc_ref, top_ref, tot_ref)
+    offset = jnp.where(spot_ref[1] == 1, -ROWS, NOWHERE)
+
+    def step(tile, carry):
+        rows = tile_rows(tile)
+        needed = reaches(spot_ref, hop_ref, doc_ref, tile, offset)
+
+        @pl.when(needed)
+        def _():
+            attend_earlier(
+                q_ref, near_ref, first_ref, tile, offset,
+                reader(source, rows), writer(state, rows),
+            )
+
+        @pl.when(jnp.logical_not(needed))
+        def _():
+            copy_tile(source, state, rows, rows)
+
+        return carry
+
+    lax.fori_loop(0, TILES, step, 0)
+
+
 def middle_kernel(
-    spot_ref, hop_ref, doc_ref, q_ref, near_ref, far_ref, side_ref, first_ref, mark_ref,
+    spot_ref, hop_ref, doc_ref, q_ref, far_ref, side_ref, first_ref, mark_ref,
     acc_in, top_in, tot_in, acc_ref, top_ref, tot_ref, out_ref, squares_ref,
 ):
     source, state = (acc_in, top_in, tot_in), (acc_ref, top_ref, tot_ref)
     odd = spot_ref[1] == 1
     slots = (
-        (near_ref, jnp.where(odd, -ROWS, NOWHERE)),
         (far_ref, -2 * ROWS),
         (side_ref, jnp.where(odd, -3 * ROWS, -ROWS)),
     )
@@ -321,13 +364,14 @@
         state_shapes + [f32(ROWS, 128)] * 2,
         2 * 10**9,
     )
+    state = call(near_kernel, scalars, [queries, side_1, first, *state], state_shapes, 10**9)
     far_4 = onward(far_2)
     side_2 = across(far_2, [(0, 1), (1, 0)])
     out_shape = jax.ShapeDtypeStruct((ROWS, HEADS * HEAD_WIDTH), jnp.bfloat16)
     *state, done, squares = call(
         middle_kernel,
         scalars,
-        [queries, side_1, far_2, side_2, first, mark, *state],
+        [queries, far_2, side_2, first, mark, *state],
         state_shapes + [out_shape, f32(8, 128)],
         2 * 10**9,
     )

time: 86.7 us -> 85.3 us (0.984)
  blocking collectives: 37.3 us -> 36 us
    all_to_all x1, blocking collectives: 37.3 us -> 36 us  [on_device(): shares = lax.all_to_all(share, SEQ_HEAD, 0, 0, tiled=True)]
    pallas_call x3 -> x4, Pallas kernels: 9.21 us -> 9.19 us  [call(): pl.pallas_call(kernel, out_shape=out_shapes, in_specs=[smem] * len(scalar...]
where the time goes in v4:
time: 85.3 us; the launch traced here: 85 us
  blocking collectives  36 us (42%)
  waiting for transfers between devices  17 us (20%)
  starting transfers between devices  16 us (19%)
  Pallas kernels  9.96 us (12%)
  local copies, waits for them, and re-layouts  4.48 us (5%)
  between operations  1.41 us (2%)
    all_to_all x1, blocking collectives, on_device(): shares = lax.all_to_all(share, SEQ_HEAD, 0, 0, tiled=True)  36 us
    ppermute x2, waiting for transfers between devices, onward(): return lax.ppermute(shard, SEQ, [(i, i + 2) for i in range(devices - 2)])  17 us
    pallas_call x4, Pallas kernels, call(): pl.pallas_call(kernel, out_shape=out_shapes, in_specs=[smem] * len(scalar...  9.19 us
    ppermute x2, starting transfers between devices, onward(): return lax.ppermute(shard, SEQ, [(i, i + 2) for i in range(devices - 2)])  8.52 us
    ppermute x3, starting transfers between devices, across(): return lax.ppermute(shard, 'seq_2', pairs)  7.53 us
    unnamed x14, local copies, waits for them, and re-layouts  4.48 us
  transfers between devices with their start and end apart: 5, of which 2 were waited for; matrix products, arithmetic and copies ran while one was open for 0% of the time, Pallas kernels for 9%

profile of v4, /device:TPU:1, one launch (start us, length us, event | category | flops | bytes accessed | tf_op | source)
XLA Modules:
  0.0 85.0 jit_solution(901566061956308687)
XLA Ops:
  0.6 0.9 %copy-done.2 = bf16[512,256]{1,0:T(8,128)(2,1)S(1)} copy-done((bf16[512,256]{1,0:T(8,128)(2,1)S(1)}, bf16[512,256]{1,0:T(8,128)(2,1)}, u32[]{:S(2)}) %copy-start.2) | copy-done | bytes 262168
  1.6 0.9 %copy-done.3 = bf16[512,256]{1,0:T(8,128)(2,1)S(1)} copy-done((bf16[512,256]{1,0:T(8,128)(2,1)S(1)}, bf16[512,256]{1,0:T(8,128)(2,1)}, u32[]{:S(2)}) %copy-start.3) | copy-done | bytes 262168
  2.5 0.1 shard_map.77.own_ref
  2.6 4.4 %collective-permute-start = (bf16[2,512,256]{2,1,0:T(8,128)(2,1)S(1)}, bf16[2,512,256]{2,1,0:T(8,128)(2,1)S(1)}, u32[]{:S(2)}, u32[]{:S(2)}) collective-permute-start(bf16[2,512,256]{2,1,0:T(8,128)(2,1)S(1)} %shard_map.77.own_ref), channel_id=1, source_target_pairs={{0,8},{4,12},{8,16},{12,20},{16,24},{20,28},{24,32},{28,36},{32,40... | collective-permute-start | bytes 1572872 | tf_op jit(solution)/shard_map/ppermute | solution.py:342
  7.0 10.6 %collective-permute-done.far_ref = bf16[2,512,256]{2,1,0:T(8,128)(2,1)S(1)} collective-permute-done((bf16[2,512,256]{2,1,0:T(8,128)(2,1)S(1)}, bf16[2,512,256]{2,1,0:T(8,128)(2,1)S(1)}, u32[]{:S(2)}, u32[]{:S(2)}) %collective-permute-start) | collective-permute-done | bytes 524320 | tf_op jit(solution)/shard_map/ppermute | solution.py:342
  17.6 4.1 %collective-permute-start.1 = (bf16[2,512,256]{2,1,0:T(8,128)(2,1)S(1)}, bf16[2,512,256]{2,1,0:T(8,128)(2,1)S(1)}, u32[]{:S(2)}, u32[]{:S(2)}) collective-permute-start(bf16[2,512,256]{2,1,0:T(8,128)(2,1)S(1)} %collective-permute-done.far_ref), channel_id=1, source_target_pairs={{0,8},{4,12},{8,16},{12,20},{16,24},{20,28},{24,32},{28,36},{32,40... | collective-permute-start | bytes 1572872 | tf_op jit(solution)/shard_map/ppermute | solution.py:342
  21.7 1.3 %collective-permute-start.4 = (bf16[2,512,256]{2,1,0:T(8,128)(2,1)S(1)}, bf16[2,512,256]{2,1,0:T(8,128)(2,1)S(1)}, u32[]{:S(2)}, u32[]{:S(2)}) collective-permute-start(bf16[2,512,256]{2,1,0:T(8,128)(2,1)S(1)} %shard_map.77.own_ref), channel_id=1, source_target_pairs={{0,4},{1,5},{2,6},{3,7},{8,12},{9,13},{10,14},{11,15},{16,20},{17,... | collective-permute-start | bytes 1572872 | tf_op jit(solution)/shard_map/ppermute | solution.py:346
  23.0 1.9 %collective-permute-start.3 = (bf16[2,512,256]{2,1,0:T(8,128)(2,1)S(1)}, bf16[2,512,256]{2,1,0:T(8,128)(2,1)S(1)}, u32[]{:S(2)}, u32[]{:S(2)}) collective-permute-start(bf16[2,512,256]{2,1,0:T(8,128)(2,1)S(1)} %collective-permute-done.far_ref), channel_id=1, source_target_pairs={{0,4},{4,0},{1,5},{5,1},{2,6},{6,2},{3,7},{7,3},{8,12},{12,8},{9,1... | collective-permute-start | bytes 1572872 | tf_op jit(solution)/shard_map/ppermute | solution.py:346
  24.9 6.5 %collective-permute-done.1.far_ref = bf16[2,512,256]{2,1,0:T(8,128)(2,1)S(1)} collective-permute-done((bf16[2,512,256]{2,1,0:T(8,128)(2,1)S(1)}, bf16[2,512,256]{2,1,0:T(8,128)(2,1)S(1)}, u32[]{:S(2)}, u32[]{:S(2)}) %collective-permute-start.1) | collective-permute-done | bytes 524320 | tf_op jit(solution)/shard_map/ppermute | solution.py:342
  31.4 4.3 %collective-permute-start.2 = (bf16[2,512,256]{2,1,0:T(8,128)(2,1)S(1)}, bf16[2,512,256]{2,1,0:T(8,128)(2,1)S(1)}, u32[]{:S(2)}, u32[]{:S(2)}) collective-permute-start(bf16[2,512,256]{2,1,0:T(8,128)(2,1)S(1)} %collective-permute-done.1.far_ref), channel_id=1, source_target_pairs={{4,0},{5,1},{6,2},{7,3},{12,8},{13,9},{14,10},{15,11},{20,16},{21,... | collective-permute-start | bytes 1572872 | tf_op jit(solution)/shard_map/ppermute | solution.py:346
  35.7 0.1 pad_add_fusion.spot_ref
  36.4 0.0 copy-start
  36.4 1.2 %copy-done = bf16[512,1024]{1,0:T(8,128)(2,1)S(1)} copy-done((bf16[512,1024]{1,0:T(8,128)(2,1)S(1)}, bf16[512,1024]{1,0:T(8,128)(2,1)}, u32[]{:S(2)}) %copy-start) | copy-done | bytes 1048600
  37.7 0.7 copy-done.4
  38.3 0.7 copy-done.6
  39.0 2.9 %shard_map.78 = (f32[512,1024]{1,0:T(8,128)S(1)}, f32[8,512,128]{2,1,0:T(8,128)S(1)}, f32[8,512,128]{2,1,0:T(8,128)S(1)}, f32[512,128]{1,0:T(8,128)S(1)}, f32[512,128]{1,0:T(8,128)S(1)}) custom-call(s32[2]{0:T(128)S(1)} %pad_add_fusion.spot_ref, s32[1]{0:T(128)S(6)} %copy.9.hop_ref, s32[512]{0:T(512)S(1)} %copy-done.4, s32[4,128]{1,0:T(4,128)S(1)} %bitcast.11, ...), custom_call_target="tpu_custom_call" | custom-call | flops 2000000000 | bytes 1048576 | tf_op jit(solution)/shard_map/pallas_call | solution.py:300
  41.9 0.0 collective-permute-done.4.near_ref
  42.0 0.0 copy-start.5
  42.0 2.9 %shard_map.79 = (f32[512,1024]{1,0:T(8,128)S(1)}, f32[8,512,128]{2,1,0:T(8,128)S(1)}, f32[8,512,128]{2,1,0:T(8,128)S(1)}) custom-call(s32[2]{0:T(128)S(1)} %pad_add_fusion.spot_ref, s32[1]{0:T(128)S(6)} %copy.9.hop_ref, s32[512]{0:T(512)S(1)} %copy-done.4, bf16[512,1024]{1,0:T(8,128)(2,1)S(1)} %copy-done.1, ...), custom_call_target="tpu_custom_call" | custom-call | flops 1000000000 | bytes 1048576 | tf_op jit(solution)/shard_map/pallas_call | solution.py:300
  44.8 0.0 collective-permute-done.3.side_ref
  44.9 1.7 %shard_map.80 = (f32[512,1024]{1,0:T(8,128)S(1)}, f32[8,512,128]{2,1,0:T(8,128)S(1)}, f32[8,512,128]{2,1,0:T(8,128)S(1)}, bf16[512,1024]{1,0:T(8,128)(2,1)S(1)}, f32[8,128]{1,0:T(8,128)S(1)}) custom-call(s32[2]{0:T(128)S(1)} %pad_add_fusion.spot_ref, s32[1]{0:T(128)S(6)} %copy.9.hop_ref, s32[512]{0:T(512)S(1)} %copy-done.5, bf16[512,1024]{1,0:T(8,128)(2,1)S(1)} %copy-done.1, ...), custom_call_target="tpu_custom_call" | custom-call | flops 2000000000 | bytes 1048576 | tf_op jit(solution)/shard_map/pallas_call | solution.py:300
  46.6 1.7 %shard_map.81 = (bf16[512,1024]{1,0:T(8,128)(2,1)}, f32[256,128]{1,0:T(8,128)S(1)}) custom-call(s32[2]{0:T(128)S(1)} %pad_add_fusion.spot_ref, s32[1]{0:T(128)S(6)} %copy.9.hop_ref, s32[512]{0:T(512)S(1)} %copy-done.5, bf16[512,1024]{1,0:T(8,128)(2,1)S(1)} %copy-done.1, bf16[2,512,256]{2,1,0:T(8,128)(2,1)S(1)} %collective-permute-done.1.far_ref, ...), custom_call_target="tpu_custom_call" | custom-call | flops 1000000000 | bytes 1048576 | tf_op jit(solution)/shard_map/pallas_call | solution.py:300
  48.3 36.0 %all_to_all.11 = f32[256,1,128]{2,1,0:T(1,128)S(1)} all-to-all(f32[256,1,128]{2,1,0:T(1,128)S(1)} %bitcast.10), channel_id=1, replica_groups=mesh['seq_0'=4,'seq_1'=8,'seq_2'=2,'head'=4] {'seq_0','seq_1','seq_2','h..., dimensions={0} | all-to-all | bytes 262144 | tf_op jit(solution)/shard_map/all_to_all | solution.py:393
  84.3 0.7 shard_map.82
  (8 shorter events, 0.0 us)
Async XLA Ops:
  0.6 1.0 %copy-start.2 = (bf16[512,256]{1,0:T(8,128)(2,1)S(1)}, bf16[512,256]{1,0:T(8,128)(2,1)}, u32[]{:S(2)}) copy-start(bf16[512,256]{1,0:T(8,128)(2,1)} %keys_ref.1) | copy-start | bytes 786436
  1.6 0.9 %copy-start.3 = (bf16[512,256]{1,0:T(8,128)(2,1)S(1)}, bf16[512,256]{1,0:T(8,128)(2,1)}, u32[]{:S(2)}) copy-start(bf16[512,256]{1,0:T(8,128)(2,1)} %values_ref.1) | copy-start | bytes 786436
  2.6 15.0 %collective-permute-start = (bf16[2,512,256]{2,1,0:T(8,128)(2,1)S(1)}, bf16[2,512,256]{2,1,0:T(8,128)(2,1)S(1)}, u32[]{:S(2)}, u32[]{:S(2)}) collective-permute-start(bf16[2,512,256]{2,1,0:T(8,128)(2,1)S(1)} %shard_map.77.own_ref), channel_id=1, source_target_pairs={{0,8},{4,12},{8,16},{12,20},{16,24},{20,28},{24,32},{28,36},{32,40... | collective-permute-start | bytes 1572872 | tf_op jit(solution)/shard_map/ppermute | solution.py:342
  17.6 13.8 %collective-permute-start.1 = (bf16[2,512,256]{2,1,0:T(8,128)(2,1)S(1)}, bf16[2,512,256]{2,1,0:T(8,128)(2,1)S(1)}, u32[]{:S(2)}, u32[]{:S(2)}) collective-permute-start(bf16[2,512,256]{2,1,0:T(8,128)(2,1)S(1)} %collective-permute-done.far_ref), channel_id=1, source_target_pairs={{0,8},{4,12},{8,16},{12,20},{16,24},{20,28},{24,32},{28,36},{32,40... | collective-permute-start | bytes 1572872 | tf_op jit(solution)/shard_map/ppermute | solution.py:342
  21.7 20.2 %collective-permute-start.4 = (bf16[2,512,256]{2,1,0:T(8,128)(2,1)S(1)}, bf16[2,512,256]{2,1,0:T(8,128)(2,1)S(1)}, u32[]{:S(2)}, u32[]{:S(2)}) collective-permute-start(bf16[2,512,256]{2,1,0:T(8,128)(2,1)S(1)} %shard_map.77.own_ref), channel_id=1, source_target_pairs={{0,4},{1,5},{2,6},{3,7},{8,12},{9,13},{10,14},{11,15},{16,20},{17,... | collective-permute-start | bytes 1572872 | tf_op jit(solution)/shard_map/ppermute | solution.py:346
  23.0 21.9 %collective-permute-start.3 = (bf16[2,512,256]{2,1,0:T(8,128)(2,1)S(1)}, bf16[2,512,256]{2,1,0:T(8,128)(2,1)S(1)}, u32[]{:S(2)}, u32[]{:S(2)}) collective-permute-start(bf16[2,512,256]{2,1,0:T(8,128)(2,1)S(1)} %collective-permute-done.far_ref), channel_id=1, source_target_pairs={{0,4},{4,0},{1,5},{5,1},{2,6},{6,2},{3,7},{7,3},{8,12},{12,8},{9,1... | collective-permute-start | bytes 1572872 | tf_op jit(solution)/shard_map/ppermute | solution.py:346
  31.4 15.2 %collective-permute-start.2 = (bf16[2,512,256]{2,1,0:T(8,128)(2,1)S(1)}, bf16[2,512,256]{2,1,0:T(8,128)(2,1)S(1)}, u32[]{:S(2)}, u32[]{:S(2)}) collective-permute-start(bf16[2,512,256]{2,1,0:T(8,128)(2,1)S(1)} %collective-permute-done.1.far_ref), channel_id=1, source_target_pairs={{4,0},{5,1},{6,2},{7,3},{12,8},{13,9},{14,10},{15,11},{20,16},{21,... | collective-permute-start | bytes 1572872 | tf_op jit(solution)/shard_map/ppermute | solution.py:346
  36.4 1.2 %copy-start = (bf16[512,1024]{1,0:T(8,128)(2,1)S(1)}, bf16[512,1024]{1,0:T(8,128)(2,1)}, u32[]{:S(2)}) copy-start(bf16[512,1024]{1,0:T(8,128)(2,1)} %q_ref.7) | copy-start | bytes 3145732
  37.7 0.7 copy-start.4
  38.3 0.7 copy-start.6
  39.0 2.9 %copy-start.1 = (bf16[512,1024]{1,0:T(8,128)(2,1)S(1)}, bf16[512,1024]{1,0:T(8,128)(2,1)}, u32[]{:S(2)}) copy-start(bf16[512,1024]{1,0:T(8,128)(2,1)} %q_ref.7) | copy-start | bytes 3145732
  42.0 2.9 %copy-start.5 = (s32[512]{0:T(512)S(1)}, s32[512]{0:T(512)}, u32[]{:S(2)}) copy-start(s32[512]{0:T(512)} %doc_ref.7) | copy-start | bytes 6148

commit v5 on v4

--- a/solution.py
+++ b/solution.py
@@ -18,6 +18,7 @@
 ROWS = 512
 TILE = 128
 TILES = ROWS // TILE
+PART = 32
 LOCAL_KV = 2
 HEADS = LOCAL_KV * GROUP
 LOWEST = -1e30
@@ -25,8 +26,8 @@
 NOWHERE = ROWS
 
 
-def aligned(start, size):
-    return pl.ds(start if isinstance(start, int) else pl.multiple_of(start, size), size)
+def aligned(start, by, size=None):
+    return pl.ds(start if isinstance(start, int) else pl.multiple_of(start, by), size or by)
 
 
 def tile_rows(tile):
@@ -61,9 +62,7 @@
     return jnp.concatenate([x] * (width // 128), axis=1)
 
 
-def attend(q_ref, block_ref, tile, width, seen, old, new):
-    rows = tile_rows(tile)
-
+def attend(q_ref, block_ref, rows, size, width, seen, old, new):
     def score(kv):
         q = jnp.concatenate([q_ref[rows, columns(h)] for h in heads_of(kv)], axis=0)
         return dot(q, block_ref[0, 0:width, columns(kv)], 1)
@@ -71,9 +70,9 @@
     def weigh(kv, scores):
         rounded, states = [], []
         for g, head in enumerate(heads_of(kv)):
-            part = jnp.where(seen, scores[g * TILE : (g + 1) * TILE], LOWEST)
+            part = jnp.where(seen, scores[g * size : (g + 1) * size], LOWEST)
             top = jnp.max(folded(jnp.maximum, lane_groups(part)), axis=1, keepdims=True)
-            top = jnp.broadcast_to(top, (TILE, 128))
+            top = jnp.broadcast_to(top, (size, 128))
             before = old(head)
             ratio = None
             if before is not None:
@@ -89,7 +88,7 @@
         update = dot(rounded, jnp.concatenate([v, jnp.ones_like(v)], axis=1), 0)
         for g, head in enumerate(heads_of(kv)):
             top, ratio = states[g]
-            part = update[g * TILE : (g + 1) * TILE]
+            part = update[g * size : (g + 1) * size]
             sums, total = part[:, 0:HEAD_WIDTH], part[:, HEAD_WIDTH:]
             if ratio is not None:
                 _, total_old, sums_old = old(head)
@@ -127,27 +126,16 @@
     return store
 
 
-def attend_earlier(q_ref, block_ref, first_ref, tile, offset, old, new):
-    place = (lax.broadcasted_iota(jnp.int32, (TILE, ROWS), 1) + offset).astype(jnp.float32)
-    seen = place >= widened(first_ref[tile_rows(tile), :], ROWS)
-    attend(q_ref, block_ref, tile, ROWS, seen, old, new)
-
-
-def reaches(spot_ref, hop_ref, doc_ref, tile, offset):
+def attend_earlier(q_ref, block_ref, first_ref, rows, size, offset, old, new):
+    place = (lax.broadcasted_iota(jnp.int32, (size, ROWS), 1) + offset).astype(jnp.float32)
+    seen = place >= widened(first_ref[rows, :], ROWS)
+    attend(q_ref, block_ref, rows, size, ROWS, seen, old, new)
+
+
+def reaches(spot_ref, hop_ref, doc_ref, row, offset):
     floor = spot_ref[0] - hop_ref[0] * ROWS
-    earliest = jnp.maximum(doc_ref[tile * TILE], floor) - spot_ref[0]
+    earliest = jnp.maximum(doc_ref[row], floor) - spot_ref[0]
     return (offset < 0) & (offset + ROWS > earliest)
-
-
-def pack_kernel(keys_ref, values_ref, out_ref, sems):
-    copies = [
-        pltpu.make_async_copy(ref, out_ref.at[i], sems.at[i])
-        for i, ref in enumerate((keys_ref, values_ref))
-    ]
-    for copy in copies:
-        copy.start()
-    for copy in copies:
-        copy.wait()
 
 
 def first_kernel(
@@ -167,7 +155,7 @@
         place = lax.broadcasted_iota(jnp.int32, (TILE, width), 1)
         row = lax.broadcasted_iota(jnp.int32, (TILE, width), 0) + tile * TILE
         seen = (place.astype(jnp.float32) >= widened(first, width)) & (place <= row)
-        attend(q_ref, own_ref, tile, width, seen, lambda head: None, writer(state, rows))
+        attend(q_ref, own_ref, rows, TILE, width, seen, lambda head: None, writer(state, rows))
 
 
 def copy_tile(source, target, rows, target_rows):
@@ -176,16 +164,20 @@
         writer(target, target_rows)(head, top, total, sums())
 
 
-def finish(state, rows, mark_ref, out_ref, squares_ref, tile):
-    marks = mark_ref[tile_rows(tile), :]
-    squares = jnp.zeros((TILE, HEAD_WIDTH), jnp.float32)
+def finish(state, rows, size, mark_ref, out_ref, squares_ref, places):
+    squares = jnp.zeros((size, HEAD_WIDTH), jnp.float32)
     for head in range(HEADS):
         _, total, sums = reader(state, rows)(head)
         attended = sums() * (1.0 / total)
-        out_ref[tile_rows(tile), columns(head)] = attended.astype(jnp.bfloat16)
+        out_ref[places, columns(head)] = attended.astype(jnp.bfloat16)
         squares += attended * attended
-    squares *= marks
-    squares_ref[...] += jnp.sum(squares.reshape(TILE // 8, 8, HEAD_WIDTH), axis=0)
+    squares *= mark_ref[places, :]
+    squares_ref[...] += jnp.sum(squares.reshape(size // 8, 8, HEAD_WIDTH), axis=0)
+
+
+def out_copy(from_ref, out_ref, sems, tile):
+    rows = tile_rows(tile)
+    return pltpu.make_async_copy(from_ref.at[rows, :], out_ref.at[rows, :], sems.at[tile])
 
 
 def last_offsets(spot_ref):
@@ -201,12 +193,12 @@
 
     def step(tile, carry):
         rows = tile_rows(tile)
-        needed = reaches(spot_ref, hop_ref, doc_ref, tile, offset)
+        needed = reaches(spot_ref, hop_ref, doc_ref, tile * TILE, offset)
 
         @pl.when(needed)
         def _():
             attend_earlier(
-                q_ref, near_ref, first_ref, tile, offset,
+                q_ref, near_ref, first_ref, rows, TILE, offset,
                 reader(source, rows), writer(state, rows),
             )
 
@@ -221,69 +213,103 @@
 
 def middle_kernel(
     spot_ref, hop_ref, doc_ref, q_ref, far_ref, side_ref, first_ref, mark_ref,
-    acc_in, top_in, tot_in, acc_ref, top_ref, tot_ref, out_ref, squares_ref,
+    acc_in, top_in, tot_in, acc_ref, top_ref, tot_ref, out_ref, squares_ref, done_ref, sems,
 ):
     source, state = (acc_in, top_in, tot_in), (acc_ref, top_ref, tot_ref)
-    odd = spot_ref[1] == 1
     slots = (
         (far_ref, -2 * ROWS),
-        (side_ref, jnp.where(odd, -3 * ROWS, -ROWS)),
+        (side_ref, jnp.where(spot_ref[1] == 1, -3 * ROWS, -ROWS)),
     )
     squares_ref[...] = jnp.zeros_like(squares_ref)
+
+    def is_late(tile):
+        a, b = [
+            reaches(spot_ref, hop_ref, doc_ref, tile * TILE, offset)
+            for offset in last_offsets(spot_ref)
+        ]
+        return a | b
 
     def step(tile, carry):
         rows = tile_rows(tile)
         copy_tile(source, state, rows, rows)
         for block_ref, offset in slots:
 
-            @pl.when(reaches(spot_ref, hop_ref, doc_ref, tile, offset))
+            @pl.when(reaches(spot_ref, hop_ref, doc_ref, tile * TILE, offset))
             def _():
                 attend_earlier(
-                    q_ref, block_ref, first_ref, tile, offset,
+                    q_ref, block_ref, first_ref, rows, TILE, offset,
                     reader(state, rows), writer(state, rows),
                 )
 
-        late = [reaches(spot_ref, hop_ref, doc_ref, tile, o) for o in last_offsets(spot_ref)]
-
-        @pl.when(jnp.logical_not(late[0] | late[1]))
-        def _():
-            finish(state, rows, mark_ref, out_ref, squares_ref, tile)
+        @pl.when(jnp.logical_not(is_late(tile)))
+        def _():
+            finish(state, rows, TILE, mark_ref, done_ref, squares_ref, rows)
+
+        @pl.when(tile > 0)
+        def _():
+            send(tile - 1)
 
         return carry
 
+    def send(tile):
+        @pl.when(jnp.logical_not(is_late(tile)))
+        def _():
+            out_copy(done_ref, out_ref, sems, tile).start()
+
     lax.fori_loop(0, TILES, step, 0)
+    send(TILES - 1)
+    for tile in range(TILES):
+
+        @pl.when(jnp.logical_not(is_late(tile)))
+        def _():
+            out_copy(done_ref, out_ref, sems, tile).wait()
+
+
+def last_offsets(spot_ref):
+    return (-4 * ROWS, jnp.where(spot_ref[1] == 1, NOWHERE, -3 * ROWS))
 
 
 def last_kernel(
     spot_ref, hop_ref, doc_ref, q_ref, far_ref, side_ref, first_ref, mark_ref, acc_in, top_in,
-    tot_in, done_ref, squares_in, out_ref, share_ref, acc_ref, top_ref, tot_ref, squares_ref,
+    tot_in, squares_in, out_in, out_ref, share_ref, acc_ref, top_ref, tot_ref, squares_ref,
+    done_ref, sems,
 ):
     source, state = (acc_in, top_in, tot_in), (acc_ref, top_ref, tot_ref)
-    offsets = last_offsets(spot_ref)
+    slots = list(zip((far_ref, side_ref), last_offsets(spot_ref)))
     squares_ref[...] = squares_in[...]
-    here = slice(0, TILE)
+
+    def late_from(row):
+        a, b = [reaches(spot_ref, hop_ref, doc_ref, row, offset) for _, offset in slots]
+        return a | b
+
+    def absorb(places, size, row):
+        here = slice(0, size)
+        copy_tile(source, state, places, here)
+        for block_ref, offset in slots:
+
+            @pl.when(reaches(spot_ref, hop_ref, doc_ref, row, offset))
+            def _():
+                attend_earlier(
+                    q_ref, block_ref, first_ref, places, size, offset,
+                    reader(state, here), writer(state, here),
+                )
+
+        finish(state, here, size, mark_ref, done_ref, squares_ref, places)
 
     def step(tile, carry):
-        rows = tile_rows(tile)
-        late = [reaches(spot_ref, hop_ref, doc_ref, tile, offset) for offset in offsets]
-
-        @pl.when(late[0] | late[1])
-        def _():
-            copy_tile(source, state, rows, here)
-            for needed, block_ref, offset in zip(late, (far_ref, side_ref), offsets):
-
-                @pl.when(needed)
-                def _():
-                    attend_earlier(
-                        q_ref, block_ref, first_ref, tile, offset,
-                        reader(state, here), writer(state, here),
-                    )
-
-            finish(state, here, mark_ref, out_ref, squares_ref, tile)
-
-        @pl.when(jnp.logical_not(late[0] | late[1]))
-        def _():
-            out_ref[rows, :] = done_ref[rows, :]
+        @pl.when(late_from(tile * TILE))
+        def _():
+            whole = late_from(tile * TILE + PART)
+
+            @pl.when(whole)
+            def _():
+                absorb(tile_rows(tile), TILE, tile * TILE)
+
+            @pl.when(jnp.logical_not(whole))
+            def _():
+                absorb(aligned(tile * TILE, PART), PART, tile * TILE)
+                rest = aligned(tile * TILE + PART, PART, TILE - PART)
+                finish(source, rest, TILE - PART, mark_ref, done_ref, squares_ref, rest)
 
         return carry
 
@@ -292,31 +318,36 @@
     count = jnp.sum(jnp.sum(mark_ref[...].reshape(ROWS // 8, 8, 128), axis=0)) * (1.0 / 128)
     lane = lax.broadcasted_iota(jnp.int32, share_ref.shape, 1)
     share_ref[...] = jnp.where(lane == 0, squares, jnp.where(lane == 1, count, 0.0))
-
-
-def call(kernel, scalars, arrays, out_shapes, flops, scratch=()):
-    smem = pl.BlockSpec(memory_space=pltpu.SMEM)
-    vmem = pl.BlockSpec(memory_space=pltpu.VMEM)
+    for ended in (False, True):
+        for tile in range(TILES):
+
+            @pl.when(late_from(tile * TILE))
+            def _():
+                copy = out_copy(done_ref, out_ref, sems, tile)
+                copy.wait() if ended else copy.start()
+
+
+def call(
+    kernel, scalars, arrays, out_shapes, flops, scratch=(), in_hbm=0, out_hbm=None, alias=None
+):
+    smem, vmem, hbm = [
+        pl.BlockSpec(memory_space=space) for space in (pltpu.SMEM, pltpu.VMEM, pltpu.HBM)
+    ]
     return pl.pallas_call(
         kernel,
         out_shape=out_shapes,
-        in_specs=[smem] * len(scalars) + [vmem] * len(arrays),
-        out_specs=[vmem] * len(out_shapes),
+        in_specs=[smem] * len(scalars) + [vmem] * (len(arrays) - in_hbm) + [hbm] * in_hbm,
+        out_specs=[hbm if i == out_hbm else vmem for i in range(len(out_shapes))],
         scratch_shapes=list(scratch),
+        input_output_aliases=alias or {},
         compiler_params=pltpu.CompilerParams(vmem_limit_bytes=8 * 1024 * 1024),
         cost_estimate=pl.CostEstimate(flops=flops, bytes_accessed=2**20, transcendentals=2**21),
     )(*scalars, *arrays)
 
 
 def packed(keys, values):
-    return pl.pallas_call(
-        pack_kernel,
-        out_shape=jax.ShapeDtypeStruct((2, *keys.shape), keys.dtype),
-        in_specs=[pl.BlockSpec(memory_space=pltpu.HBM)] * 2,
-        out_specs=pl.BlockSpec(memory_space=pltpu.VMEM),
-        scratch_shapes=[pltpu.SemaphoreType.DMA((2,))],
-        compiler_params=pltpu.CompilerParams(vmem_limit_bytes=4 * 1024 * 1024),
-    )(keys, values)
+    pads = ((0, 0), (0, 0))
+    return jnp.pad(keys[None], ((0, 1), *pads)) + jnp.pad(values[None], ((1, 0), *pads))
 
 
 def objective_kernel(copies, shares_ref, out_ref):
@@ -368,19 +399,23 @@
     far_4 = onward(far_2)
     side_2 = across(far_2, [(0, 1), (1, 0)])
     out_shape = jax.ShapeDtypeStruct((ROWS, HEADS * HEAD_WIDTH), jnp.bfloat16)
+    copy_scratch = [pltpu.VMEM(out_shape.shape, jnp.bfloat16), pltpu.SemaphoreType.DMA((TILES,))]
     *state, done, squares = call(
         middle_kernel,
         scalars,
         [queries, far_2, side_2, first, mark, *state],
         state_shapes + [out_shape, f32(8, 128)],
         2 * 10**9,
+        scratch=copy_scratch,
+        out_hbm=3,
     )
     side_3 = across(far_4, [(1, 0)])
     devices = lax.axis_size(SEQ_HEAD)
+    arrays = [queries, far_4, side_3, first, mark, *state, squares, done]
     attention, share = call(
         last_kernel,
         scalars,
-        [queries, far_4, side_3, first, mark, *state, done, squares],
+        arrays,
         [out_shape, f32(devices, 128)],
         10**9,
         scratch=[
@@ -388,7 +423,11 @@
             pltpu.VMEM((HEADS, TILE, 128), jnp.float32),
             pltpu.VMEM((HEADS, TILE, 128), jnp.float32),
             pltpu.VMEM((8, 128), jnp.float32),
+            *copy_scratch,
         ],
+        in_hbm=1,
+        out_hbm=0,
+        alias={len(scalars) + len(arrays) - 1: 0},
     )
     shares = lax.all_to_all(share, SEQ_HEAD, 0, 0, tiled=True)
     return (attention, objective_of(shares, lax.axis_size("head")))

time: 85.3 us -> 84.5 us (level)
  local copies, waits for them, and re-layouts: 4.48 us -> 2.59 us
  other arithmetic: 0.08 us -> 1.14 us
    unnamed x14 -> x8, local copies, waits for them, and re-layouts: 4.48 us -> 2.59 us
    add x0 -> x1, other arithmetic: none -> 1.07 us  [packed(): jnp.pad(keys[None], ((0, 1), *pads))]
  transfers between devices with their start and end apart: 5 -> 5, of which waited for: 2 -> 2; matrix products, arithmetic and copies ran while one was open for 0% -> 0% of each run, Pallas kernels for 9% -> 10%
where the time goes in v5:
time: 84.5 us; the launch traced here: 84.2 us
  blocking collectives  36 us (43%)
  waiting for transfers between devices  17 us (20%)
  starting transfers between devices  16 us (19%)
  Pallas kernels  9.97 us (12%)
  local copies, waits for them, and re-layouts  2.59 us (3%)
  between operations  1.39 us (2%)
  other arithmetic  1.14 us (1%)
    all_to_all x1, blocking collectives, on_device(): shares = lax.all_to_all(share, SEQ_HEAD, 0, 0, tiled=True)  36 us
    ppermute x2, waiting for transfers between devices, onward(): return lax.ppermute(shard, SEQ, [(i, i + 2) for i in range(devices - 2)])  17 us
    pallas_call x4, Pallas kernels, call(): pl.pallas_call(kernel, out_shape=out_shapes, in_specs=[smem] * len(scalar...  9.25 us
    ppermute x2, starting transfers between devices, onward(): return lax.ppermute(shard, SEQ, [(i, i + 2) for i in range(devices - 2)])  8.52 us
    ppermute x3, starting transfers between devices, across(): return lax.ppermute(shard, 'seq_2', pairs)  7.53 us
    unnamed x8, local copies, waits for them, and re-layouts  2.59 us
  transfers between devices with their start and end apart: 5, of which 2 were waited for; matrix products, arithmetic and copies ran while one was open for 0% of the time, Pallas kernels for 10%

profile of v5, /device:TPU:1, one launch (start us, length us, event | category | flops | bytes accessed | tf_op | source)
XLA Modules:
  0.0 84.2 jit_solution(11107018295758385379)
XLA Ops:
  0.6 1.1 %pad_add_fusion.own_ref = bf16[2,512,256]{2,1,0:T(8,128)(2,1)S(1)} fusion(bf16[1,512,256]{2,1,0:T(8,128)(2,1)} %bitcast.15, bf16[1,512,256]{2,1,0:T(8,128)(2,1)} %bitcast.16), kind=kLoop, calls=%fused_computation | loop fusion | flops 262144 | bytes 1048576 | tf_op jit(solution)/shard_map/add | solution.py:350
  1.7 4.4 %collective-permute-start = (bf16[2,512,256]{2,1,0:T(8,128)(2,1)S(1)}, bf16[2,512,256]{2,1,0:T(8,128)(2,1)S(1)}, u32[]{:S(2)}, u32[]{:S(2)}) collective-permute-start(bf16[2,512,256]{2,1,0:T(8,128)(2,1)S(1)} %pad_add_fusion.own_ref), channel_id=1, source_target_pairs={{0,8},{4,12},{8,16},{12,20},{16,24},{20,28},{24,32},{28,36},{32,40... | collective-permute-start | bytes 1572872 | tf_op jit(solution)/shard_map/ppermute | solution.py:373
  6.1 10.6 %collective-permute-done.far_ref = bf16[2,512,256]{2,1,0:T(8,128)(2,1)S(1)} collective-permute-done((bf16[2,512,256]{2,1,0:T(8,128)(2,1)S(1)}, bf16[2,512,256]{2,1,0:T(8,128)(2,1)S(1)}, u32[]{:S(2)}, u32[]{:S(2)}) %collective-permute-start) | collective-permute-done | bytes 524320 | tf_op jit(solution)/shard_map/ppermute | solution.py:373
  16.7 4.1 %collective-permute-start.1 = (bf16[2,512,256]{2,1,0:T(8,128)(2,1)S(1)}, bf16[2,512,256]{2,1,0:T(8,128)(2,1)S(1)}, u32[]{:S(2)}, u32[]{:S(2)}) collective-permute-start(bf16[2,512,256]{2,1,0:T(8,128)(2,1)S(1)} %collective-permute-done.far_ref), channel_id=1, source_target_pairs={{0,8},{4,12},{8,16},{12,20},{16,24},{20,28},{24,32},{28,36},{32,40... | collective-permute-start | bytes 1572872 | tf_op jit(solution)/shard_map/ppermute | solution.py:373
  20.8 1.3 %collective-permute-start.4 = (bf16[2,512,256]{2,1,0:T(8,128)(2,1)S(1)}, bf16[2,512,256]{2,1,0:T(8,128)(2,1)S(1)}, u32[]{:S(2)}, u32[]{:S(2)}) collective-permute-start(bf16[2,512,256]{2,1,0:T(8,128)(2,1)S(1)} %pad_add_fusion.own_ref), channel_id=1, source_target_pairs={{0,4},{1,5},{2,6},{3,7},{8,12},{9,13},{10,14},{11,15},{16,20},{17,... | collective-permute-start | bytes 1572872 | tf_op jit(solution)/shard_map/ppermute | solution.py:377
  22.1 1.9 %collective-permute-start.3 = (bf16[2,512,256]{2,1,0:T(8,128)(2,1)S(1)}, bf16[2,512,256]{2,1,0:T(8,128)(2,1)S(1)}, u32[]{:S(2)}, u32[]{:S(2)}) collective-permute-start(bf16[2,512,256]{2,1,0:T(8,128)(2,1)S(1)} %collective-permute-done.far_ref), channel_id=1, source_target_pairs={{0,4},{4,0},{1,5},{5,1},{2,6},{6,2},{3,7},{7,3},{8,12},{12,8},{9,1... | collective-permute-start | bytes 1572872 | tf_op jit(solution)/shard_map/ppermute | solution.py:377
  24.0 6.5 %collective-permute-done.1.far_ref = bf16[2,512,256]{2,1,0:T(8,128)(2,1)S(1)} collective-permute-done((bf16[2,512,256]{2,1,0:T(8,128)(2,1)S(1)}, bf16[2,512,256]{2,1,0:T(8,128)(2,1)S(1)}, u32[]{:S(2)}, u32[]{:S(2)}) %collective-permute-start.1) | collective-permute-done | bytes 524320 | tf_op jit(solution)/shard_map/ppermute | solution.py:373
  30.5 4.3 %collective-permute-start.2 = (bf16[2,512,256]{2,1,0:T(8,128)(2,1)S(1)}, bf16[2,512,256]{2,1,0:T(8,128)(2,1)S(1)}, u32[]{:S(2)}, u32[]{:S(2)}) collective-permute-start(bf16[2,512,256]{2,1,0:T(8,128)(2,1)S(1)} %collective-permute-done.1.far_ref), channel_id=1, source_target_pairs={{4,0},{5,1},{6,2},{7,3},{12,8},{13,9},{14,10},{15,11},{20,16},{21,... | collective-permute-start | bytes 1572872 | tf_op jit(solution)/shard_map/ppermute | solution.py:377
  34.8 0.1 pad_add_fusion.1.spot_ref
  35.5 0.0 copy-start
  35.5 1.2 %copy-done = bf16[512,1024]{1,0:T(8,128)(2,1)S(1)} copy-done((bf16[512,1024]{1,0:T(8,128)(2,1)S(1)}, bf16[512,1024]{1,0:T(8,128)(2,1)}, u32[]{:S(2)}) %copy-start) | copy-done | bytes 1048600
  36.8 0.0 copy-start.2
  36.8 0.7 copy-done.2
  37.5 0.7 copy-done.3
  38.1 2.9 %shard_map.77 = (f32[512,1024]{1,0:T(8,128)S(1)}, f32[8,512,128]{2,1,0:T(8,128)S(1)}, f32[8,512,128]{2,1,0:T(8,128)S(1)}, f32[512,128]{1,0:T(8,128)S(1)}, f32[512,128]{1,0:T(8,128)S(1)}) custom-call(s32[2]{0:T(128)S(1)} %pad_add_fusion.1.spot_ref, s32[1]{0:T(128)S(6)} %copy.11.hop_ref, s32[512]{0:T(512)S(1)} %copy-done.2, s32[4,128]{1,0:T(4,128)S(1)} %bitcast.13, ...), custom_call_target="tpu_custom_call" | custom-call | flops 2000000000 | bytes 1048576 | tf_op jit(solution)/shard_map/pallas_call | solution.py:336
  41.0 0.0 collective-permute-done.4.near_ref
  41.0 0.0 copy-done.1
  41.0 2.9 %shard_map.78 = (f32[512,1024]{1,0:T(8,128)S(1)}, f32[8,512,128]{2,1,0:T(8,128)S(1)}, f32[8,512,128]{2,1,0:T(8,128)S(1)}) custom-call(s32[2]{0:T(128)S(1)} %pad_add_fusion.1.spot_ref, s32[1]{0:T(128)S(6)} %copy.11.hop_ref, s32[512]{0:T(512)S(1)} %copy-done.2, bf16[512,1024]{1,0:T(8,128)(2,1)S(1)} %copy-done.1, ...), custom_call_target="tpu_custom_call" | custom-call | flops 1000000000 | bytes 1048576 | tf_op jit(solution)/shard_map/pallas_call | solution.py:336
  43.9 0.0 collective-permute-done.3.side_ref
  43.9 2.6 %shard_map.79 = (f32[512,1024]{1,0:T(8,128)S(1)}, f32[8,512,128]{2,1,0:T(8,128)S(1)}, f32[8,512,128]{2,1,0:T(8,128)S(1)}, bf16[512,1024]{1,0:T(8,128)(2,1)}, f32[8,128]{1,0:T(8,128)S(1)}) custom-call(s32[2]{0:T(128)S(1)} %pad_add_fusion.1.spot_ref, s32[1]{0:T(128)S(6)} %copy.11.hop_ref, s32[512]{0:T(512)S(1)} %copy-done.2, bf16[512,1024]{1,0:T(8,128)(2,1)S(1)} %copy-done.1, ...), custom_call_target="tpu_custom_call" | custom-call | flops 2000000000 | bytes 1048576 | tf_op jit(solution)/shard_map/pallas_call | solution.py:336
  46.5 0.0 collective-permute-done.2.side_ref
  46.5 0.9 %shard_map.80 = (bf16[512,1024]{1,0:T(8,128)(2,1)}, f32[256,128]{1,0:T(8,128)S(1)}) custom-call(s32[2]{0:T(128)S(1)} %pad_add_fusion.1.spot_ref, s32[1]{0:T(128)S(6)} %copy.11.hop_ref, s32[512]{0:T(512)S(1)} %copy-done.2, bf16[512,1024]{1,0:T(8,128)(2,1)S(1)} %copy-done.1, ...), custom_call_target="tpu_custom_call", output_to_operand_aliasing={{0}: (12, {})} | custom-call | flops 1000000000 | bytes 1048576 | tf_op jit(solution)/shard_map/pallas_call | solution.py:336
  47.5 36.0 %all_to_all.11 = f32[256,1,128]{2,1,0:T(1,128)S(1)} all-to-all(f32[256,1,128]{2,1,0:T(1,128)S(1)} %bitcast.12), channel_id=1, replica_groups=mesh['seq_0'=4,'seq_1'=8,'seq_2'=2,'head'=4] {'seq_0','seq_1','seq_2','h..., dimensions={0} | all-to-all | bytes 262144 | tf_op jit(solution)/shard_map/all_to_all | solution.py:432
  83.5 0.7 shard_map.81
  (2 shorter events, 0.0 us)
Async XLA Ops:
  1.7 15.0 %collective-permute-start = (bf16[2,512,256]{2,1,0:T(8,128)(2,1)S(1)}, bf16[2,512,256]{2,1,0:T(8,128)(2,1)S(1)}, u32[]{:S(2)}, u32[]{:S(2)}) collective-permute-start(bf16[2,512,256]{2,1,0:T(8,128)(2,1)S(1)} %pad_add_fusion.own_ref), channel_id=1, source_target_pairs={{0,8},{4,12},{8,16},{12,20},{16,24},{20,28},{24,32},{28,36},{32,40... | collective-permute-start | bytes 1572872 | tf_op jit(solution)/shard_map/ppermute | solution.py:373
  16.7 13.8 %collective-permute-start.1 = (bf16[2,512,256]{2,1,0:T(8,128)(2,1)S(1)}, bf16[2,512,256]{2,1,0:T(8,128)(2,1)S(1)}, u32[]{:S(2)}, u32[]{:S(2)}) collective-permute-start(bf16[2,512,256]{2,1,0:T(8,128)(2,1)S(1)} %collective-permute-done.far_ref), channel_id=1, source_target_pairs={{0,8},{4,12},{8,16},{12,20},{16,24},{20,28},{24,32},{28,36},{32,40... | collective-permute-start | bytes 1572872 | tf_op jit(solution)/shard_map/ppermute | solution.py:373
  20.8 20.2 %collective-permute-start.4 = (bf16[2,512,256]{2,1,0:T(8,128)(2,1)S(1)}, bf16[2,512,256]{2,1,0:T(8,128)(2,1)S(1)}, u32[]{:S(2)}, u32[]{:S(2)}) collective-permute-start(bf16[2,512,256]{2,1,0:T(8,128)(2,1)S(1)} %pad_add_fusion.own_ref), channel_id=1, source_target_pairs={{0,4},{1,5},{2,6},{3,7},{8,12},{9,13},{10,14},{11,15},{16,20},{17,... | collective-permute-start | bytes 1572872 | tf_op jit(solution)/shard_map/ppermute | solution.py:377
  22.1 21.8 %collective-permute-start.3 = (bf16[2,512,256]{2,1,0:T(8,128)(2,1)S(1)}, bf16[2,512,256]{2,1,0:T(8,128)(2,1)S(1)}, u32[]{:S(2)}, u32[]{:S(2)}) collective-permute-start(bf16[2,512,256]{2,1,0:T(8,128)(2,1)S(1)} %collective-permute-done.far_ref), channel_id=1, source_target_pairs={{0,4},{4,0},{1,5},{5,1},{2,6},{6,2},{3,7},{7,3},{8,12},{12,8},{9,1... | collective-permute-start | bytes 1572872 | tf_op jit(solution)/shard_map/ppermute | solution.py:377
  30.5 16.0 %collective-permute-start.2 = (bf16[2,512,256]{2,1,0:T(8,128)(2,1)S(1)}, bf16[2,512,256]{2,1,0:T(8,128)(2,1)S(1)}, u32[]{:S(2)}, u32[]{:S(2)}) collective-permute-start(bf16[2,512,256]{2,1,0:T(8,128)(2,1)S(1)} %collective-permute-done.1.far_ref), channel_id=1, source_target_pairs={{4,0},{5,1},{6,2},{7,3},{12,8},{13,9},{14,10},{15,11},{20,16},{21,... | collective-permute-start | bytes 1572872 | tf_op jit(solution)/shard_map/ppermute | solution.py:377
  35.5 1.2 %copy-start = (bf16[512,1024]{1,0:T(8,128)(2,1)S(1)}, bf16[512,1024]{1,0:T(8,128)(2,1)}, u32[]{:S(2)}) copy-start(bf16[512,1024]{1,0:T(8,128)(2,1)} %q_ref.7) | copy-start | bytes 3145732
  36.8 0.7 copy-start.2
  37.4 0.7 copy-start.3
  38.1 2.9 %copy-start.1 = (bf16[512,1024]{1,0:T(8,128)(2,1)S(1)}, bf16[512,1024]{1,0:T(8,128)(2,1)}, u32[]{:S(2)}) copy-start(bf16[512,1024]{1,0:T(8,128)(2,1)} %q_ref.7) | copy-start | bytes 3145732

commit v6 on v5

--- a/solution.py
+++ b/solution.py
@@ -180,31 +180,28 @@
     return pltpu.make_async_copy(from_ref.at[rows, :], out_ref.at[rows, :], sems.at[tile])
 
 
-def last_offsets(spot_ref):
-    return (-4 * ROWS, jnp.where(spot_ref[1] == 1, NOWHERE, -3 * ROWS))
+def on_core(spot_ref, core, distance):
+    return jnp.where(spot_ref[1] == core, -distance * ROWS, NOWHERE)
 
 
 def near_kernel(
-    spot_ref, hop_ref, doc_ref, q_ref, near_ref, first_ref, acc_in, top_in, tot_in,
+    spot_ref, hop_ref, doc_ref, q_ref, near_ref, far_ref, first_ref, acc_in, top_in, tot_in,
     acc_ref, top_ref, tot_ref,
 ):
     source, state = (acc_in, top_in, tot_in), (acc_ref, top_ref, tot_ref)
-    offset = jnp.where(spot_ref[1] == 1, -ROWS, NOWHERE)
+    slots = ((near_ref, on_core(spot_ref, 1, 1)), (far_ref, on_core(spot_ref, 1, 2)))
 
     def step(tile, carry):
         rows = tile_rows(tile)
-        needed = reaches(spot_ref, hop_ref, doc_ref, tile * TILE, offset)
-
-        @pl.when(needed)
-        def _():
-            attend_earlier(
-                q_ref, near_ref, first_ref, rows, TILE, offset,
-                reader(source, rows), writer(state, rows),
-            )
-
-        @pl.when(jnp.logical_not(needed))
-        def _():
-            copy_tile(source, state, rows, rows)
+        copy_tile(source, state, rows, rows)
+        for block_ref, offset in slots:
+
+            @pl.when(reaches(spot_ref, hop_ref, doc_ref, tile * TILE, offset))
+            def _():
+                attend_earlier(
+                    q_ref, block_ref, first_ref, rows, TILE, offset,
+                    reader(state, rows), writer(state, rows),
+                )
 
         return carry
 
@@ -212,22 +209,19 @@
 
 
 def middle_kernel(
-    spot_ref, hop_ref, doc_ref, q_ref, far_ref, side_ref, first_ref, mark_ref,
+    spot_ref, hop_ref, doc_ref, q_ref, near_ref, far_ref, side_ref, first_ref, mark_ref,
     acc_in, top_in, tot_in, acc_ref, top_ref, tot_ref, out_ref, squares_ref, done_ref, sems,
 ):
     source, state = (acc_in, top_in, tot_in), (acc_ref, top_ref, tot_ref)
     slots = (
-        (far_ref, -2 * ROWS),
-        (side_ref, jnp.where(spot_ref[1] == 1, -3 * ROWS, -ROWS)),
+        (near_ref, on_core(spot_ref, 0, 1)),
+        (far_ref, on_core(spot_ref, 0, 2)),
+        (side_ref, on_core(spot_ref, 1, 3)),
     )
     squares_ref[...] = jnp.zeros_like(squares_ref)
 
     def is_late(tile):
-        a, b = [
-            reaches(spot_ref, hop_ref, doc_ref, tile * TILE, offset)
-            for offset in last_offsets(spot_ref)
-        ]
-        return a | b
+        return late_from(spot_ref, hop_ref, doc_ref, tile * TILE)
 
     def step(tile, carry):
         rows = tile_rows(tile)
@@ -265,22 +259,24 @@
             out_copy(done_ref, out_ref, sems, tile).wait()
 
 
-def last_offsets(spot_ref):
-    return (-4 * ROWS, jnp.where(spot_ref[1] == 1, NOWHERE, -3 * ROWS))
+def late_from(spot_ref, hop_ref, doc_ref, row):
+    offset = jnp.where(spot_ref[1] == 1, -4 * ROWS, -3 * ROWS)
+    return reaches(spot_ref, hop_ref, doc_ref, row, offset)
 
 
 def last_kernel(
-    spot_ref, hop_ref, doc_ref, q_ref, far_ref, side_ref, first_ref, mark_ref, acc_in, top_in,
-    tot_in, squares_in, out_in, out_ref, share_ref, acc_ref, top_ref, tot_ref, squares_ref,
+    spot_ref, hop_ref, doc_ref, q_ref, odd_ref, even_ref, side_ref, first_ref, mark_ref, acc_in,
+    top_in, tot_in, squares_in, out_in, out_ref, share_ref, acc_ref, top_ref, tot_ref, squares_ref,
     done_ref, sems,
 ):
     source, state = (acc_in, top_in, tot_in), (acc_ref, top_ref, tot_ref)
-    slots = list(zip((far_ref, side_ref), last_offsets(spot_ref)))
+    slots = (
+        (odd_ref, on_core(spot_ref, 1, 4)),
+        (side_ref, on_core(spot_ref, 0, 3)),
+        (even_ref, on_core(spot_ref, 0, 4)),
+    )
+    late = functools.partial(late_from, spot_ref, hop_ref, doc_ref)
     squares_ref[...] = squares_in[...]
-
-    def late_from(row):
-        a, b = [reaches(spot_ref, hop_ref, doc_ref, row, offset) for _, offset in slots]
-        return a | b
 
     def absorb(places, size, row):
         here = slice(0, size)
@@ -297,9 +293,9 @@
         finish(state, here, size, mark_ref, done_ref, squares_ref, places)
 
     def step(tile, carry):
-        @pl.when(late_from(tile * TILE))
+        @pl.when(late(tile * TILE))
         def _():
-            whole = late_from(tile * TILE + PART)
+            whole = late(tile * TILE + PART)
 
             @pl.when(whole)
             def _():
@@ -321,7 +317,7 @@
     for ended in (False, True):
         for tile in range(TILES):
 
-            @pl.when(late_from(tile * TILE))
+            @pl.when(late(tile * TILE))
             def _():
                 copy = out_copy(done_ref, out_ref, sems, tile)
                 copy.wait() if ended else copy.start()
@@ -368,13 +364,12 @@
     )(shares).reshape(())
 
 
-def onward(shard):
-    devices = lax.axis_size(SEQ)
-    return lax.ppermute(shard, SEQ, [(i, i + 2) for i in range(devices - 2)])
-
-
-def across(shard, pairs):
-    return lax.ppermute(shard, "seq_2", pairs)
+def onward(shard, core):
+    return lax.ppermute(shard, SEQ, [(i, i + 2) for i in range(core, lax.axis_size(SEQ) - 2, 2)])
+
+
+def across(shard, core):
+    return lax.ppermute(shard, "seq_2", [(core, 1 - core)])
 
 
 def f32(*shape):
@@ -385,8 +380,9 @@
     spot = jnp.stack([lax.axis_index(SEQ) * ROWS, lax.axis_index("seq_2")])
     scalars = [spot, hop_counts, doc_start]
     own = packed(keys, values)
-    far_2 = onward(own)
-    side_1 = across(own, [(0, 1)])
+    odd_2 = onward(own, 1)
+    side_1 = across(own, 0)
+    even_2 = onward(own, 0)
     state_shapes = [f32(ROWS, HEADS * HEAD_WIDTH), f32(HEADS, ROWS, 128), f32(HEADS, ROWS, 128)]
     *state, first, mark = call(
         first_kernel,
@@ -395,23 +391,27 @@
         state_shapes + [f32(ROWS, 128)] * 2,
         2 * 10**9,
     )
-    state = call(near_kernel, scalars, [queries, side_1, first, *state], state_shapes, 10**9)
-    far_4 = onward(far_2)
-    side_2 = across(far_2, [(0, 1), (1, 0)])
+    odd_4 = onward(odd_2, 1)
+    side_2 = across(odd_2, 1)
+    state = call(
+        near_kernel, scalars, [queries, side_1, odd_2, first, *state], state_shapes, 2 * 10**9
+    )
+    even_4 = onward(even_2, 0)
+    side_3 = across(even_2, 0)
     out_shape = jax.ShapeDtypeStruct((ROWS, HEADS * HEAD_WIDTH), jnp.bfloat16)
     copy_scratch = [pltpu.VMEM(out_shape.shape, jnp.bfloat16), pltpu.SemaphoreType.DMA((TILES,))]
     *state, done, squares = call(
         middle_kernel,
         scalars,
-        [queries, far_2, side_2, first, mark, *state],
+        [queries, side_2, even_2, side_3, first, mark, *state],
         state_shapes + [out_shape, f32(8, 128)],
         2 * 10**9,
         scratch=copy_scratch,
         out_hbm=3,
     )
-    side_3 = across(far_4, [(1, 0)])
+    side_4 = across(odd_4, 1)
     devices = lax.axis_size(SEQ_HEAD)
-    arrays = [queries, far_4, side_3, first, mark, *state, squares, done]
+    arrays = [queries, odd_4, even_4, side_4, first, mark, *state, squares, done]
     attention, share = call(
         last_kernel,
         scalars,

time: 84.5 us -> 83.1 us (0.983)
  waiting for transfers between devices: 17 us -> 9.49 us
  starting transfers between devices: 16 us -> 21.7 us
  blocking collectives: 36 us -> 34.6 us
  Pallas kernels: 9.97 us -> 10.9 us
    ppermute x5 -> x8, waiting for transfers between devices: 17 us -> 9.49 us  [the longest x4 9.48 us: onward(): lax.ppermute(shard, SEQ, [(i, i + 2) for i in range(core, lax.axis_size(S...]
    ppermute x5 -> x8, starting transfers between devices: 16 us -> 21.7 us  [the longest x4 11.9 us: across(): return lax.ppermute(shard, 'seq_2', [(core, 1 - core)])]
    all_to_all x1, blocking collectives: 36 us -> 34.6 us  [on_device(): shares = lax.all_to_all(share, SEQ_HEAD, 0, 0, tiled=True)]
    pallas_call x4, Pallas kernels: 9.25 us -> 10.2 us  [call(): pl.pallas_call(kernel, out_shape=out_shapes, in_specs=[smem] * len(scalar...]
  transfers between devices with their start and end apart: 5 -> 8, of which waited for: 2 -> 1; matrix products, arithmetic and copies ran while one was open for 0% -> 0% of each run, Pallas kernels for 10% -> 11%
where the time goes in v6:
time: 83.1 us; the launch traced here: 82.7 us
  blocking collectives  34.6 us (42%)
  starting transfers between devices  21.7 us (26%)
  Pallas kernels  10.9 us (13%)
  waiting for transfers between devices  9.49 us (11%)
  local copies, waits for them, and re-layouts  2.59 us (3%)
  other arithmetic  1.93 us (2%)
  between operations  1.45 us (2%)
    all_to_all x1, blocking collectives, on_device(): shares = lax.all_to_all(share, SEQ_HEAD, 0, 0, tiled=True)  34.6 us
    ppermute x4, starting transfers between devices, across(): return lax.ppermute(shard, 'seq_2', [(core, 1 - core)])  11.9 us
    pallas_call x4, Pallas kernels, call(): pl.pallas_call(kernel, out_shape=out_shapes, in_specs=[smem] * len(scalar...  10.2 us
    ppermute x4, starting transfers between devices, onward(): lax.ppermute(shard, SEQ, [(i, i + 2) for i in range(core, lax.axis_size(S...  9.78 us
    ppermute x4, waiting for transfers between devices, onward(): lax.ppermute(shard, SEQ, [(i, i + 2) for i in range(core, lax.axis_size(S...  9.48 us
    unnamed x8, local copies, waits for them, and re-layouts  2.59 us
    add x1, other arithmetic, packed(): jnp.pad(keys[None], ((0, 1), *pads))  1.86 us
  transfers between devices with their start and end apart: 8, of which 1 were waited for; matrix products, arithmetic and copies ran while one was open for 0% of the time, Pallas kernels for 11%

profile of v6, /device:TPU:1, one launch (start us, length us, event | category | flops | bytes accessed | tf_op | source)
XLA Modules:
  0.0 82.7 jit_solution(5547989683996547259)
XLA Ops:
  0.6 1.9 %pad_add_fusion.own_ref = bf16[2,512,256]{2,1,0:T(8,128)(2,1)} fusion(bf16[1,512,256]{2,1,0:T(8,128)(2,1)} %bitcast.15, bf16[1,512,256]{2,1,0:T(8,128)(2,1)} %bitcast.16), kind=kLoop, calls=%fused_computation | loop fusion | flops 262144 | bytes 1048576 | tf_op jit(solution)/shard_map/add | solution.py:346
  2.5 4.4 %collective-permute-start = (bf16[2,512,256]{2,1,0:T(8,128)(2,1)}, bf16[2,512,256]{2,1,0:T(8,128)(2,1)S(1)}, u32[]{:S(2)}, u32[]{:S(2)}) collective-permute-start(bf16[2,512,256]{2,1,0:T(8,128)(2,1)} %pad_add_fusion.own_ref), channel_id=1, source_target_pairs={{4,12},{12,20},{20,28},{28,36},{36,44},{44,52},{52,60},{60,68},{68... | collective-permute-start | bytes 1572872 | tf_op jit(solution)/shard_map/ppermute | solution.py:368
  6.9 0.7 collective-permute-start.2
  7.6 9.5 %collective-permute-done.far_ref = bf16[2,512,256]{2,1,0:T(8,128)(2,1)S(1)} collective-permute-done((bf16[2,512,256]{2,1,0:T(8,128)(2,1)}, bf16[2,512,256]{2,1,0:T(8,128)(2,1)S(1)}, u32[]{:S(2)}, u32[]{:S(2)}) %collective-permute-start) | collective-permute-done | bytes 524320 | tf_op jit(solution)/shard_map/ppermute | solution.py:368
  17.0 4.0 %collective-permute-start.1 = (bf16[2,512,256]{2,1,0:T(8,128)(2,1)S(1)}, bf16[2,512,256]{2,1,0:T(8,128)(2,1)S(1)}, u32[]{:S(2)}, u32[]{:S(2)}) collective-permute-start(bf16[2,512,256]{2,1,0:T(8,128)(2,1)S(1)} %collective-permute-done.far_ref), channel_id=1, source_target_pairs={{4,12},{12,20},{20,28},{28,36},{36,44},{44,52},{52,60},{60,68},{68... | collective-permute-start | bytes 1572872 | tf_op jit(solution)/shard_map/ppermute | solution.py:368
  21.1 1.3 %collective-permute-start.7 = (bf16[2,512,256]{2,1,0:T(8,128)(2,1)}, bf16[2,512,256]{2,1,0:T(8,128)(2,1)S(1)}, u32[]{:S(2)}, u32[]{:S(2)}) collective-permute-start(bf16[2,512,256]{2,1,0:T(8,128)(2,1)} %pad_add_fusion.own_ref), channel_id=1, source_target_pairs={{0,4},{1,5},{2,6},{3,7},{8,12},{9,13},{10,14},{11,15},{16,20},{17,... | collective-permute-start | bytes 1572872 | tf_op jit(solution)/shard_map/ppermute | solution.py:372
  22.4 3.1 %collective-permute-start.5 = (bf16[2,512,256]{2,1,0:T(8,128)(2,1)S(1)}, bf16[2,512,256]{2,1,0:T(8,128)(2,1)S(1)}, u32[]{:S(2)}, u32[]{:S(2)}) collective-permute-start(bf16[2,512,256]{2,1,0:T(8,128)(2,1)S(1)} %collective-permute-done.far_ref), channel_id=1, source_target_pairs={{4,0},{5,1},{6,2},{7,3},{12,8},{13,9},{14,10},{15,11},{20,16},{21,... | collective-permute-start | bytes 1572872 | tf_op jit(solution)/shard_map/ppermute | solution.py:372
  25.5 1.3 %collective-permute-start.6 = (bf16[2,512,256]{2,1,0:T(8,128)(2,1)S(1)}, bf16[2,512,256]{2,1,0:T(8,128)(2,1)S(1)}, u32[]{:S(2)}, u32[]{:S(2)}) collective-permute-start(bf16[2,512,256]{2,1,0:T(8,128)(2,1)S(1)} %collective-permute-done.2.far_ref), channel_id=1, source_target_pairs={{0,4},{1,5},{2,6},{3,7},{8,12},{9,13},{10,14},{11,15},{16,20},{17,... | collective-permute-start | bytes 1572872 | tf_op jit(solution)/shard_map/ppermute | solution.py:372
  27.4 0.1 pad_add_fusion.1.spot_ref
  27.5 0.7 collective-permute-start.3
  28.2 6.2 %collective-permute-start.4 = (bf16[2,512,256]{2,1,0:T(8,128)(2,1)S(1)}, bf16[2,512,256]{2,1,0:T(8,128)(2,1)S(1)}, u32[]{:S(2)}, u32[]{:S(2)}) collective-permute-start(bf16[2,512,256]{2,1,0:T(8,128)(2,1)S(1)} %collective-permute-done.1.odd_ref), channel_id=1, source_target_pairs={{4,0},{5,1},{6,2},{7,3},{12,8},{13,9},{14,10},{15,11},{20,16},{21,... | collective-permute-start | bytes 1572872 | tf_op jit(solution)/shard_map/ppermute | solution.py:372
  34.4 0.0 copy-start
  34.5 1.2 %copy-done = bf16[512,1024]{1,0:T(8,128)(2,1)S(1)} copy-done((bf16[512,1024]{1,0:T(8,128)(2,1)S(1)}, bf16[512,1024]{1,0:T(8,128)(2,1)}, u32[]{:S(2)}) %copy-start) | copy-done | bytes 1048600
  35.7 0.7 copy-done.2
  36.4 0.7 copy-done.3
  37.0 3.5 %shard_map.77 = (f32[512,1024]{1,0:T(8,128)S(1)}, f32[8,512,128]{2,1,0:T(8,128)S(1)}, f32[8,512,128]{2,1,0:T(8,128)S(1)}, f32[512,128]{1,0:T(8,128)S(1)}, f32[512,128]{1,0:T(8,128)S(1)}) custom-call(s32[2]{0:T(128)S(1)} %pad_add_fusion.1.spot_ref, s32[1]{0:T(128)S(6)} %copy.11.hop_ref, s32[512]{0:T(512)S(1)} %copy-done.2, s32[4,128]{1,0:T(4,128)S(1)} %bitcast.13, ...), custom_call_target="tpu_custom_call" | custom-call | flops 2000000000 | bytes 1048576 | tf_op jit(solution)/shard_map/pallas_call | solution.py:332
  40.5 0.0 collective-permute-done.7.near_ref
  40.5 3.2 %shard_map.78 = (f32[512,1024]{1,0:T(8,128)S(1)}, f32[8,512,128]{2,1,0:T(8,128)S(1)}, f32[8,512,128]{2,1,0:T(8,128)S(1)}) custom-call(s32[2]{0:T(128)S(1)} %pad_add_fusion.1.spot_ref, s32[1]{0:T(128)S(6)} %copy.11.hop_ref, s32[512]{0:T(512)S(1)} %copy-done.2, bf16[512,1024]{1,0:T(8,128)(2,1)S(1)} %copy-done.1, ...), custom_call_target="tpu_custom_call" | custom-call | flops 2000000000 | bytes 1048576 | tf_op jit(solution)/shard_map/pallas_call | solution.py:332
  43.7 0.0 collective-permute-done.5.near_ref
  43.8 0.0 collective-permute-done.6.side_ref
  43.8 2.6 %shard_map.79 = (f32[512,1024]{1,0:T(8,128)S(1)}, f32[8,512,128]{2,1,0:T(8,128)S(1)}, f32[8,512,128]{2,1,0:T(8,128)S(1)}, bf16[512,1024]{1,0:T(8,128)(2,1)}, f32[8,128]{1,0:T(8,128)S(1)}) custom-call(s32[2]{0:T(128)S(1)} %pad_add_fusion.1.spot_ref, s32[1]{0:T(128)S(6)} %copy.11.hop_ref, s32[512]{0:T(512)S(1)} %copy-done.2, bf16[512,1024]{1,0:T(8,128)(2,1)S(1)} %copy-done.1, ...), custom_call_target="tpu_custom_call" | custom-call | flops 2000000000 | bytes 1048576 | tf_op jit(solution)/shard_map/pallas_call | solution.py:332
  46.4 0.9 %shard_map.80 = (bf16[512,1024]{1,0:T(8,128)(2,1)}, f32[256,128]{1,0:T(8,128)S(1)}) custom-call(s32[2]{0:T(128)S(1)} %pad_add_fusion.1.spot_ref, s32[1]{0:T(128)S(6)} %copy.11.hop_ref, s32[512]{0:T(512)S(1)} %copy-done.2, bf16[512,1024]{1,0:T(8,128)(2,1)S(1)} %copy-done.1, ...), custom_call_target="tpu_custom_call", output_to_operand_aliasing={{0}: (13, {})} | custom-call | flops 1000000000 | bytes 1048576 | tf_op jit(solution)/shard_map/pallas_call | solution.py:332
  47.3 34.6 %all_to_all.11 = f32[256,1,128]{2,1,0:T(1,128)S(1)} all-to-all(f32[256,1,128]{2,1,0:T(1,128)S(1)} %bitcast.12), channel_id=1, replica_groups=mesh['seq_0'=4,'seq_1'=8,'seq_2'=2,'head'=4] {'seq_0','seq_1','seq_2','h..., dimensions={0} | all-to-all | bytes 262144 | tf_op jit(solution)/shard_map/all_to_all | solution.py:432
  82.0 0.7 shard_map.81
  (8 shorter events, 0.0 us)
Async XLA Ops:
  2.5 14.6 %collective-permute-start = (bf16[2,512,256]{2,1,0:T(8,128)(2,1)}, bf16[2,512,256]{2,1,0:T(8,128)(2,1)S(1)}, u32[]{:S(2)}, u32[]{:S(2)}) collective-permute-start(bf16[2,512,256]{2,1,0:T(8,128)(2,1)} %pad_add_fusion.own_ref), channel_id=1, source_target_pairs={{4,12},{12,20},{20,28},{28,36},{36,44},{44,52},{52,60},{60,68},{68... | collective-permute-start | bytes 1572872 | tf_op jit(solution)/shard_map/ppermute | solution.py:368
  6.9 18.6 %collective-permute-start.2 = (bf16[2,512,256]{2,1,0:T(8,128)(2,1)}, bf16[2,512,256]{2,1,0:T(8,128)(2,1)S(1)}, u32[]{:S(2)}, u32[]{:S(2)}) collective-permute-start(bf16[2,512,256]{2,1,0:T(8,128)(2,1)} %pad_add_fusion.own_ref), channel_id=1, source_target_pairs={{0,8},{8,16},{16,24},{24,32},{32,40},{40,48},{48,56},{56,64},{64,7... | collective-permute-start | bytes 1572872 | tf_op jit(solution)/shard_map/ppermute | solution.py:368
  17.0 11.2 %collective-permute-start.1 = (bf16[2,512,256]{2,1,0:T(8,128)(2,1)S(1)}, bf16[2,512,256]{2,1,0:T(8,128)(2,1)S(1)}, u32[]{:S(2)}, u32[]{:S(2)}) collective-permute-start(bf16[2,512,256]{2,1,0:T(8,128)(2,1)S(1)} %collective-permute-done.far_ref), channel_id=1, source_target_pairs={{4,12},{12,20},{20,28},{28,36},{36,44},{44,52},{52,60},{60,68},{68... | collective-permute-start | bytes 1572872 | tf_op jit(solution)/shard_map/ppermute | solution.py:368
  21.1 19.4 %collective-permute-start.7 = (bf16[2,512,256]{2,1,0:T(8,128)(2,1)}, bf16[2,512,256]{2,1,0:T(8,128)(2,1)S(1)}, u32[]{:S(2)}, u32[]{:S(2)}) collective-permute-start(bf16[2,512,256]{2,1,0:T(8,128)(2,1)} %pad_add_fusion.own_ref), channel_id=1, source_target_pairs={{0,4},{1,5},{2,6},{3,7},{8,12},{9,13},{10,14},{11,15},{16,20},{17,... | collective-permute-start | bytes 1572872 | tf_op jit(solution)/shard_map/ppermute | solution.py:372
  22.4 21.4 %collective-permute-start.5 = (bf16[2,512,256]{2,1,0:T(8,128)(2,1)S(1)}, bf16[2,512,256]{2,1,0:T(8,128)(2,1)S(1)}, u32[]{:S(2)}, u32[]{:S(2)}) collective-permute-start(bf16[2,512,256]{2,1,0:T(8,128)(2,1)S(1)} %collective-permute-done.far_ref), channel_id=1, source_target_pairs={{4,0},{5,1},{6,2},{7,3},{12,8},{13,9},{14,10},{15,11},{20,16},{21,... | collective-permute-start | bytes 1572872 | tf_op jit(solution)/shard_map/ppermute | solution.py:372
  25.5 18.3 %collective-permute-start.6 = (bf16[2,512,256]{2,1,0:T(8,128)(2,1)S(1)}, bf16[2,512,256]{2,1,0:T(8,128)(2,1)S(1)}, u32[]{:S(2)}, u32[]{:S(2)}) collective-permute-start(bf16[2,512,256]{2,1,0:T(8,128)(2,1)S(1)} %collective-permute-done.2.far_ref), channel_id=1, source_target_pairs={{0,4},{1,5},{2,6},{3,7},{8,12},{9,13},{10,14},{11,15},{16,20},{17,... | collective-permute-start | bytes 1572872 | tf_op jit(solution)/shard_map/ppermute | solution.py:372
  27.5 18.9 %collective-permute-start.3 = (bf16[2,512,256]{2,1,0:T(8,128)(2,1)S(1)}, bf16[2,512,256]{2,1,0:T(8,128)(2,1)S(1)}, u32[]{:S(2)}, u32[]{:S(2)}) collective-permute-start(bf16[2,512,256]{2,1,0:T(8,128)(2,1)S(1)} %collective-permute-done.2.far_ref), channel_id=1, source_target_pairs={{0,8},{8,16},{16,24},{24,32},{32,40},{40,48},{48,56},{56,64},{64,7... | collective-permute-start | bytes 1572872 | tf_op jit(solution)/shard_map/ppermute | solution.py:368
  28.2 18.2 %collective-permute-start.4 = (bf16[2,512,256]{2,1,0:T(8,128)(2,1)S(1)}, bf16[2,512,256]{2,1,0:T(8,128)(2,1)S(1)}, u32[]{:S(2)}, u32[]{:S(2)}) collective-permute-start(bf16[2,512,256]{2,1,0:T(8,128)(2,1)S(1)} %collective-permute-done.1.odd_ref), channel_id=1, source_target_pairs={{4,0},{5,1},{6,2},{7,3},{12,8},{13,9},{14,10},{15,11},{20,16},{21,... | collective-permute-start | bytes 1572872 | tf_op jit(solution)/shard_map/ppermute | solution.py:372
  34.4 1.2 %copy-start = (bf16[512,1024]{1,0:T(8,128)(2,1)S(1)}, bf16[512,1024]{1,0:T(8,128)(2,1)}, u32[]{:S(2)}) copy-start(bf16[512,1024]{1,0:T(8,128)(2,1)} %q_ref.7) | copy-start | bytes 3145732
  35.7 0.7 copy-start.2
  36.4 0.7 copy-start.3
  37.0 3.5 %copy-start.1 = (bf16[512,1024]{1,0:T(8,128)(2,1)S(1)}, bf16[512,1024]{1,0:T(8,128)(2,1)}, u32[]{:S(2)}) copy-start(bf16[512,1024]{1,0:T(8,128)(2,1)} %q_ref.7) | copy-start | bytes 3145732

commit v7 on v5

--- a/solution.py
+++ b/solution.py
@@ -19,6 +19,7 @@
 TILE = 128
 TILES = ROWS // TILE
 PART = 32
+PAIR = 2 * TILE
 LOCAL_KV = 2
 HEADS = LOCAL_KV * GROUP
 LOWEST = -1e30
@@ -62,12 +63,16 @@
     return jnp.concatenate([x] * (width // 128), axis=1)
 
 
-def attend(q_ref, block_ref, rows, size, width, seen, old, new):
-    def score(kv):
+def attend(q_ref, block_ref, parts, size):
+    steps = [(part, kv) for part in parts for kv in range(LOCAL_KV)]
+
+    def score(step):
+        (rows, width, *_), kv = step
         q = jnp.concatenate([q_ref[rows, columns(h)] for h in heads_of(kv)], axis=0)
         return dot(q, block_ref[0, 0:width, columns(kv)], 1)
 
-    def weigh(kv, scores):
+    def weigh(step, scores):
+        (_, width, seen, old, _), kv = step
         rounded, states = [], []
         for g, head in enumerate(heads_of(kv)):
             part = jnp.where(seen, scores[g * size : (g + 1) * size], LOWEST)
@@ -83,7 +88,8 @@
             rounded.append(weights.astype(jnp.bfloat16))
         return jnp.concatenate(rounded, axis=0), states
 
-    def add(kv, rounded, states):
+    def add(step, rounded, states):
+        (_, width, _, old, new), kv = step
         v = block_ref[1, 0:width, columns(kv)]
         update = dot(rounded, jnp.concatenate([v, jnp.ones_like(v)], axis=1), 0)
         for g, head in enumerate(heads_of(kv)):
@@ -95,14 +101,13 @@
                 sums, total = sums_old() * ratio + sums, total_old * ratio + total
             new(head, top, total, sums)
 
-    scores = score(0)
-    pending = None
-    for kv in range(LOCAL_KV):
-        ahead = score(kv + 1) if kv + 1 < LOCAL_KV else None
-        weighed = weigh(kv, scores)
+    scores, pending = score(steps[0]), None
+    for at, step in enumerate(steps):
+        ahead = score(steps[at + 1]) if at + 1 < len(steps) else None
+        weighed = weigh(step, scores)
         if pending is not None:
             add(*pending)
-        scores, pending = ahead, (kv, *weighed)
+        scores, pending = ahead, (step, *weighed)
     add(*pending)
 
 
@@ -126,10 +131,21 @@
     return store
 
 
-def attend_earlier(q_ref, block_ref, first_ref, rows, size, offset, old, new):
-    place = (lax.broadcasted_iota(jnp.int32, (size, ROWS), 1) + offset).astype(jnp.float32)
-    seen = place >= widened(first_ref[rows, :], ROWS)
-    attend(q_ref, block_ref, rows, size, ROWS, seen, old, new)
+def attend_earlier(q_ref, block_ref, first_ref, places, size, offset, source, state):
+    parts = []
+    for rows, rows_in, rows_out in places:
+        place = (lax.broadcasted_iota(jnp.int32, (size, ROWS), 1) + offset).astype(jnp.float32)
+        seen = place >= widened(first_ref[rows, :], ROWS)
+        parts.append((rows, ROWS, seen, reader(source, rows_in), writer(state, rows_out)))
+    attend(q_ref, block_ref, parts, size)
+
+
+def pair_rows(pair):
+    return [aligned(pair * PAIR + i, TILE) for i in range(0, PAIR, TILE)]
+
+
+def same(rows):
+    return [(r, r, r) for r in rows]
 
 
 def reaches(spot_ref, hop_ref, doc_ref, row, offset):
@@ -144,6 +160,7 @@
 ):
     floor = spot_ref[0] - hop_ref[0] * ROWS
     state = (acc_ref, top_ref, tot_ref)
+    parts = []
     for tile in range(TILES):
         width = (tile + 1) * TILE
         rows = tile_rows(tile)
@@ -155,7 +172,8 @@
         place = lax.broadcasted_iota(jnp.int32, (TILE, width), 1)
         row = lax.broadcasted_iota(jnp.int32, (TILE, width), 0) + tile * TILE
         seen = (place.astype(jnp.float32) >= widened(first, width)) & (place <= row)
-        attend(q_ref, own_ref, rows, TILE, width, seen, lambda head: None, writer(state, rows))
+        parts.append((rows, width, seen, lambda head: None, writer(state, rows)))
+    attend(q_ref, own_ref, parts, TILE)
 
 
 def copy_tile(source, target, rows, target_rows):
@@ -180,35 +198,33 @@
     return pltpu.make_async_copy(from_ref.at[rows, :], out_ref.at[rows, :], sems.at[tile])
 
 
-def last_offsets(spot_ref):
-    return (-4 * ROWS, jnp.where(spot_ref[1] == 1, NOWHERE, -3 * ROWS))
-
-
 def near_kernel(
     spot_ref, hop_ref, doc_ref, q_ref, near_ref, first_ref, acc_in, top_in, tot_in,
     acc_ref, top_ref, tot_ref,
 ):
     source, state = (acc_in, top_in, tot_in), (acc_ref, top_ref, tot_ref)
-    offset = jnp.where(spot_ref[1] == 1, -ROWS, NOWHERE)
-
-    def step(tile, carry):
-        rows = tile_rows(tile)
-        needed = reaches(spot_ref, hop_ref, doc_ref, tile * TILE, offset)
+    offset = on_core(spot_ref, 1, 1)
+
+    def step(pair, carry):
+        rows = pair_rows(pair)
+        needed = reaches(spot_ref, hop_ref, doc_ref, pair * PAIR, offset)
 
         @pl.when(needed)
         def _():
-            attend_earlier(
-                q_ref, near_ref, first_ref, rows, TILE, offset,
-                reader(source, rows), writer(state, rows),
-            )
+            attend_earlier(q_ref, near_ref, first_ref, same(rows), TILE, offset, source, state)
 
         @pl.when(jnp.logical_not(needed))
         def _():
-            copy_tile(source, state, rows, rows)
+            for part in rows:
+                copy_tile(source, state, part, part)
 
         return carry
 
-    lax.fori_loop(0, TILES, step, 0)
+    lax.fori_loop(0, ROWS // PAIR, step, 0)
+
+
+def on_core(spot_ref, core, distance):
+    return jnp.where(spot_ref[1] == core, -distance * ROWS, NOWHERE)
 
 
 def middle_kernel(
@@ -216,38 +232,39 @@
     acc_in, top_in, tot_in, acc_ref, top_ref, tot_ref, out_ref, squares_ref, done_ref, sems,
 ):
     source, state = (acc_in, top_in, tot_in), (acc_ref, top_ref, tot_ref)
-    slots = (
-        (far_ref, -2 * ROWS),
-        (side_ref, jnp.where(spot_ref[1] == 1, -3 * ROWS, -ROWS)),
-    )
+    offsets = (-2 * ROWS, jnp.where(spot_ref[1] == 1, -3 * ROWS, -ROWS))
     squares_ref[...] = jnp.zeros_like(squares_ref)
 
     def is_late(tile):
-        a, b = [
-            reaches(spot_ref, hop_ref, doc_ref, tile * TILE, offset)
-            for offset in last_offsets(spot_ref)
-        ]
-        return a | b
-
-    def step(tile, carry):
-        rows = tile_rows(tile)
-        copy_tile(source, state, rows, rows)
-        for block_ref, offset in slots:
-
-            @pl.when(reaches(spot_ref, hop_ref, doc_ref, tile * TILE, offset))
+        return late_from(spot_ref, hop_ref, doc_ref, tile * TILE)
+
+    def step(pair, carry):
+        rows = pair_rows(pair)
+        far, side = [reaches(spot_ref, hop_ref, doc_ref, pair * PAIR, offset) for offset in offsets]
+
+        @pl.when(far)
+        def _():
+            attend_earlier(q_ref, far_ref, first_ref, same(rows), TILE, offsets[0], source, state)
+
+        @pl.when(jnp.logical_not(far))
+        def _():
+            for part in rows:
+                copy_tile(source, state, part, part)
+
+        @pl.when(side)
+        def _():
+            attend_earlier(q_ref, side_ref, first_ref, same(rows), TILE, offsets[1], state, state)
+
+        for i, part in enumerate(rows):
+
+            @pl.when(jnp.logical_not(is_late(pair * len(rows) + i)))
             def _():
-                attend_earlier(
-                    q_ref, block_ref, first_ref, rows, TILE, offset,
-                    reader(state, rows), writer(state, rows),
-                )
-
-        @pl.when(jnp.logical_not(is_late(tile)))
-        def _():
-            finish(state, rows, TILE, mark_ref, done_ref, squares_ref, rows)
-
-        @pl.when(tile > 0)
-        def _():
-            send(tile - 1)
+                finish(state, part, TILE, mark_ref, done_ref, squares_ref, part)
+
+        @pl.when(pair > 0)
+        def _():
+            for i in range(len(rows)):
+                send((pair - 1) * len(rows) + i)
 
         return carry
 
@@ -256,8 +273,9 @@
         def _():
             out_copy(done_ref, out_ref, sems, tile).start()
 
-    lax.fori_loop(0, TILES, step, 0)
-    send(TILES - 1)
+    lax.fori_loop(0, ROWS // PAIR, step, 0)
+    for tile in range(TILES - PAIR // TILE, TILES):
+        send(tile)
     for tile in range(TILES):
 
         @pl.when(jnp.logical_not(is_late(tile)))
@@ -265,22 +283,24 @@
             out_copy(done_ref, out_ref, sems, tile).wait()
 
 
-def last_offsets(spot_ref):
-    return (-4 * ROWS, jnp.where(spot_ref[1] == 1, NOWHERE, -3 * ROWS))
+def late_from(spot_ref, hop_ref, doc_ref, row):
+    offset = jnp.where(spot_ref[1] == 1, -4 * ROWS, -3 * ROWS)
+    return reaches(spot_ref, hop_ref, doc_ref, row, offset)
 
 
 def last_kernel(
-    spot_ref, hop_ref, doc_ref, q_ref, far_ref, side_ref, first_ref, mark_ref, acc_in, top_in,
-    tot_in, squares_in, out_in, out_ref, share_ref, acc_ref, top_ref, tot_ref, squares_ref,
+    spot_ref, hop_ref, doc_ref, q_ref, odd_ref, even_ref, side_ref, first_ref, mark_ref, acc_in,
+    top_in, tot_in, squares_in, out_in, out_ref, share_ref, acc_ref, top_ref, tot_ref, squares_ref,
     done_ref, sems,
 ):
     source, state = (acc_in, top_in, tot_in), (acc_ref, top_ref, tot_ref)
-    slots = list(zip((far_ref, side_ref), last_offsets(spot_ref)))
+    slots = (
+        (odd_ref, on_core(spot_ref, 1, 4)),
+        (side_ref, on_core(spot_ref, 0, 3)),
+        (even_ref, on_core(spot_ref, 0, 4)),
+    )
+    late = functools.partial(late_from, spot_ref, hop_ref, doc_ref)
     squares_ref[...] = squares_in[...]
-
-    def late_from(row):
-        a, b = [reaches(spot_ref, hop_ref, doc_ref, row, offset) for _, offset in slots]
-        return a | b
 
     def absorb(places, size, row):
         here = slice(0, size)
@@ -290,16 +310,15 @@
             @pl.when(reaches(spot_ref, hop_ref, doc_ref, row, offset))
             def _():
                 attend_earlier(
-                    q_ref, block_ref, first_ref, places, size, offset,
-                    reader(state, here), writer(state, here),
+                    q_ref, block_ref, first_ref, [(places, here, here)], size, offset, state, state
                 )
 
         finish(state, here, size, mark_ref, done_ref, squares_ref, places)
 
     def step(tile, carry):
-        @pl.when(late_from(tile * TILE))
-        def _():
-            whole = late_from(tile * TILE + PART)
+        @pl.when(late(tile * TILE))
+        def _():
+            whole = late(tile * TILE + PART)
 
             @pl.when(whole)
             def _():
@@ -321,7 +340,7 @@
     for ended in (False, True):
         for tile in range(TILES):
 
-            @pl.when(late_from(tile * TILE))
+            @pl.when(late(tile * TILE))
             def _():
                 copy = out_copy(done_ref, out_ref, sems, tile)
                 copy.wait() if ended else copy.start()
@@ -368,9 +387,9 @@
     )(shares).reshape(())
 
 
-def onward(shard):
-    devices = lax.axis_size(SEQ)
-    return lax.ppermute(shard, SEQ, [(i, i + 2) for i in range(devices - 2)])
+def onward(shard, cores):
+    blocks = range(lax.axis_size(SEQ) - 2)
+    return lax.ppermute(shard, SEQ, [(i, i + 2) for i in blocks if i % 2 in cores])
 
 
 def across(shard, pairs):
@@ -385,7 +404,7 @@
     spot = jnp.stack([lax.axis_index(SEQ) * ROWS, lax.axis_index("seq_2")])
     scalars = [spot, hop_counts, doc_start]
     own = packed(keys, values)
-    far_2 = onward(own)
+    far_2 = onward(own, (0, 1))
     side_1 = across(own, [(0, 1)])
     state_shapes = [f32(ROWS, HEADS * HEAD_WIDTH), f32(HEADS, ROWS, 128), f32(HEADS, ROWS, 128)]
     *state, first, mark = call(
@@ -396,8 +415,9 @@
         2 * 10**9,
     )
     state = call(near_kernel, scalars, [queries, side_1, first, *state], state_shapes, 10**9)
-    far_4 = onward(far_2)
+    odd_4 = onward(far_2, (1,))
     side_2 = across(far_2, [(0, 1), (1, 0)])
+    even_4 = onward(far_2, (0,))
     out_shape = jax.ShapeDtypeStruct((ROWS, HEADS * HEAD_WIDTH), jnp.bfloat16)
     copy_scratch = [pltpu.VMEM(out_shape.shape, jnp.bfloat16), pltpu.SemaphoreType.DMA((TILES,))]
     *state, done, squares = call(
@@ -409,9 +429,9 @@
         scratch=copy_scratch,
         out_hbm=3,
     )
-    side_3 = across(far_4, [(1, 0)])
+    side_3 = across(odd_4, [(1, 0)])
     devices = lax.axis_size(SEQ_HEAD)
-    arrays = [queries, far_4, side_3, first, mark, *state, squares, done]
+    arrays = [queries, odd_4, even_4, side_3, first, mark, *state, squares, done]
     attention, share = call(
         last_kernel,
         scalars,

time: 84.5 us -> 77.5 us (0.917)
  waiting for transfers between devices: 17 us -> 13.4 us
  starting transfers between devices: 16 us -> 14 us
  blocking collectives: 36 us -> 34.5 us
    ppermute x2 -> x3, waiting for transfers between devices: 17 us -> 13.4 us  [onward(): lax.ppermute(shard, SEQ, [(i, i + 2) for i in blocks if i % 2 in cores])]
    ppermute x3, starting transfers between devices: 7.53 us -> 4.8 us  [across(): return lax.ppermute(shard, 'seq_2', pairs)]
    all_to_all x1, blocking collectives: 36 us -> 34.5 us  [on_device(): shares = lax.all_to_all(share, SEQ_HEAD, 0, 0, tiled=True)]
    ppermute x2 -> x3, starting transfers between devices: 8.52 us -> 9.2 us  [onward(): lax.ppermute(shard, SEQ, [(i, i + 2) for i in blocks if i % 2 in cores])]
  transfers between devices with their start and end apart: 5 -> 6, of which waited for: 2 -> 2; matrix products, arithmetic and copies ran while one was open for 0% -> 0% of each run, Pallas kernels for 10% -> 11%
where the time goes in v7:
time: 77.5 us; the launch traced here: 77.2 us
  blocking collectives  34.5 us (45%)
  starting transfers between devices  14 us (18%)
  waiting for transfers between devices  13.4 us (17%)
  Pallas kernels  10 us (13%)
  local copies, waits for them, and re-layouts  2.59 us (3%)
  between operations  1.57 us (2%)
  other arithmetic  1.14 us (1%)
    all_to_all x1, blocking collectives, on_device(): shares = lax.all_to_all(share, SEQ_HEAD, 0, 0, tiled=True)  34.5 us
    ppermute x3, waiting for transfers between devices, onward(): lax.ppermute(shard, SEQ, [(i, i + 2) for i in blocks if i % 2 in cores])  13.4 us
    pallas_call x4, Pallas kernels, call(): pl.pallas_call(kernel, out_shape=out_shapes, in_specs=[smem] * len(scalar...  9.29 us
    ppermute x3, starting transfers between devices, onward(): lax.ppermute(shard, SEQ, [(i, i + 2) for i in blocks if i % 2 in cores])  9.2 us
    ppermute x3, starting transfers between devices, across(): return lax.ppermute(shard, 'seq_2', pairs)  4.8 us
    unnamed x8, local copies, waits for them, and re-layouts  2.59 us
  transfers between devices with their start and end apart: 6, of which 2 were waited for; matrix products, arithmetic and copies ran while one was open for 0% of the time, Pallas kernels for 11%

profile of v7, /device:TPU:1, one launch (start us, length us, event | category | flops | bytes accessed | tf_op | source)
XLA Modules:
  0.0 77.2 jit_solution(7440770891502394662)
XLA Ops:
  0.6 1.1 %pad_add_fusion.own_ref = bf16[2,512,256]{2,1,0:T(8,128)(2,1)S(1)} fusion(bf16[1,512,256]{2,1,0:T(8,128)(2,1)} %bitcast.15, bf16[1,512,256]{2,1,0:T(8,128)(2,1)} %bitcast.16), kind=kLoop, calls=%fused_computation | loop fusion | flops 262144 | bytes 1048576 | tf_op jit(solution)/shard_map/add | solution.py:369
  1.7 4.4 %collective-permute-start = (bf16[2,512,256]{2,1,0:T(8,128)(2,1)S(1)}, bf16[2,512,256]{2,1,0:T(8,128)(2,1)S(1)}, u32[]{:S(2)}, u32[]{:S(2)}) collective-permute-start(bf16[2,512,256]{2,1,0:T(8,128)(2,1)S(1)} %pad_add_fusion.own_ref), channel_id=1, source_target_pairs={{0,8},{4,12},{8,16},{12,20},{16,24},{20,28},{24,32},{28,36},{32,40... | collective-permute-start | bytes 1572872 | tf_op jit(solution)/shard_map/ppermute | solution.py:392
  6.1 10.6 %collective-permute-done.far_ref = bf16[2,512,256]{2,1,0:T(8,128)(2,1)S(1)} collective-permute-done((bf16[2,512,256]{2,1,0:T(8,128)(2,1)S(1)}, bf16[2,512,256]{2,1,0:T(8,128)(2,1)S(1)}, u32[]{:S(2)}, u32[]{:S(2)}) %collective-permute-start) | collective-permute-done | bytes 524320 | tf_op jit(solution)/shard_map/ppermute | solution.py:392
  16.7 4.1 %collective-permute-start.1 = (bf16[2,512,256]{2,1,0:T(8,128)(2,1)S(1)}, bf16[2,512,256]{2,1,0:T(8,128)(2,1)S(1)}, u32[]{:S(2)}, u32[]{:S(2)}) collective-permute-start(bf16[2,512,256]{2,1,0:T(8,128)(2,1)S(1)} %collective-permute-done.far_ref), channel_id=1, source_target_pairs={{4,12},{12,20},{20,28},{28,36},{36,44},{44,52},{52,60},{60,68},{68... | collective-permute-start | bytes 1572872 | tf_op jit(solution)/shard_map/ppermute | solution.py:392
  20.8 1.3 %collective-permute-start.5 = (bf16[2,512,256]{2,1,0:T(8,128)(2,1)S(1)}, bf16[2,512,256]{2,1,0:T(8,128)(2,1)S(1)}, u32[]{:S(2)}, u32[]{:S(2)}) collective-permute-start(bf16[2,512,256]{2,1,0:T(8,128)(2,1)S(1)} %pad_add_fusion.own_ref), channel_id=1, source_target_pairs={{0,4},{1,5},{2,6},{3,7},{8,12},{9,13},{10,14},{11,15},{16,20},{17,... | collective-permute-start | bytes 1572872 | tf_op jit(solution)/shard_map/ppermute | solution.py:396
  22.1 1.2 %collective-permute-start.4 = (bf16[2,512,256]{2,1,0:T(8,128)(2,1)S(1)}, bf16[2,512,256]{2,1,0:T(8,128)(2,1)S(1)}, u32[]{:S(2)}, u32[]{:S(2)}) collective-permute-start(bf16[2,512,256]{2,1,0:T(8,128)(2,1)S(1)} %collective-permute-done.far_ref), channel_id=1, source_target_pairs={{0,4},{4,0},{1,5},{5,1},{2,6},{6,2},{3,7},{7,3},{8,12},{12,8},{9,1... | collective-permute-start | bytes 1572872 | tf_op jit(solution)/shard_map/ppermute | solution.py:396
  23.3 0.7 collective-permute-start.2
  24.0 2.8 %collective-permute-done.1.odd_ref = bf16[2,512,256]{2,1,0:T(8,128)(2,1)S(1)} collective-permute-done((bf16[2,512,256]{2,1,0:T(8,128)(2,1)S(1)}, bf16[2,512,256]{2,1,0:T(8,128)(2,1)S(1)}, u32[]{:S(2)}, u32[]{:S(2)}) %collective-permute-start.1) | collective-permute-done | bytes 524320 | tf_op jit(solution)/shard_map/ppermute | solution.py:392
  26.9 2.3 %collective-permute-start.3 = (bf16[2,512,256]{2,1,0:T(8,128)(2,1)S(1)}, bf16[2,512,256]{2,1,0:T(8,128)(2,1)S(1)}, u32[]{:S(2)}, u32[]{:S(2)}) collective-permute-start(bf16[2,512,256]{2,1,0:T(8,128)(2,1)S(1)} %collective-permute-done.1.odd_ref), channel_id=1, source_target_pairs={{4,0},{5,1},{6,2},{7,3},{12,8},{13,9},{14,10},{15,11},{20,16},{21,... | collective-permute-start | bytes 1572872 | tf_op jit(solution)/shard_map/ppermute | solution.py:396
  29.1 0.1 pad_add_fusion.1.spot_ref
  29.9 0.0 copy-start
  29.9 1.2 %copy-done = bf16[512,1024]{1,0:T(8,128)(2,1)S(1)} copy-done((bf16[512,1024]{1,0:T(8,128)(2,1)S(1)}, bf16[512,1024]{1,0:T(8,128)(2,1)}, u32[]{:S(2)}) %copy-start) | copy-done | bytes 1048600
  31.1 0.7 copy-done.2
  31.8 0.7 copy-done.3
  32.5 2.9 %shard_map.77 = (f32[512,1024]{1,0:T(8,128)S(1)}, f32[8,512,128]{2,1,0:T(8,128)S(1)}, f32[8,512,128]{2,1,0:T(8,128)S(1)}, f32[512,128]{1,0:T(8,128)S(1)}, f32[512,128]{1,0:T(8,128)S(1)}) custom-call(s32[2]{0:T(128)S(1)} %pad_add_fusion.1.spot_ref, s32[1]{0:T(128)S(6)} %copy.11.hop_ref, s32[512]{0:T(512)S(1)} %copy-done.2, s32[4,128]{1,0:T(4,128)S(1)} %bitcast.13, ...), custom_call_target="tpu_custom_call" | custom-call | flops 2000000000 | bytes 1048576 | tf_op jit(solution)/shard_map/pallas_call | solution.py:355
  35.4 0.0 collective-permute-done.5.near_ref
  35.4 2.9 %shard_map.78 = (f32[512,1024]{1,0:T(8,128)S(1)}, f32[8,512,128]{2,1,0:T(8,128)S(1)}, f32[8,512,128]{2,1,0:T(8,128)S(1)}) custom-call(s32[2]{0:T(128)S(1)} %pad_add_fusion.1.spot_ref, s32[1]{0:T(128)S(6)} %copy.11.hop_ref, s32[512]{0:T(512)S(1)} %copy-done.2, bf16[512,1024]{1,0:T(8,128)(2,1)S(1)} %copy-done.1, ...), custom_call_target="tpu_custom_call" | custom-call | flops 1000000000 | bytes 1048576 | tf_op jit(solution)/shard_map/pallas_call | solution.py:355
  38.2 0.0 collective-permute-done.4.side_ref
  38.2 2.7 %shard_map.79 = (f32[512,1024]{1,0:T(8,128)S(1)}, f32[8,512,128]{2,1,0:T(8,128)S(1)}, f32[8,512,128]{2,1,0:T(8,128)S(1)}, bf16[512,1024]{1,0:T(8,128)(2,1)}, f32[8,128]{1,0:T(8,128)S(1)}) custom-call(s32[2]{0:T(128)S(1)} %pad_add_fusion.1.spot_ref, s32[1]{0:T(128)S(6)} %copy.11.hop_ref, s32[512]{0:T(512)S(1)} %copy-done.2, bf16[512,1024]{1,0:T(8,128)(2,1)S(1)} %copy-done.1, ...), custom_call_target="tpu_custom_call" | custom-call | flops 2000000000 | bytes 1048576 | tf_op jit(solution)/shard_map/pallas_call | solution.py:355
  40.9 0.0 collective-permute-done.2.even_ref
  40.9 0.0 collective-permute-done.3.side_ref
  40.9 0.9 %shard_map.80 = (bf16[512,1024]{1,0:T(8,128)(2,1)}, f32[256,128]{1,0:T(8,128)S(1)}) custom-call(s32[2]{0:T(128)S(1)} %pad_add_fusion.1.spot_ref, s32[1]{0:T(128)S(6)} %copy.11.hop_ref, s32[512]{0:T(512)S(1)} %copy-done.2, bf16[512,1024]{1,0:T(8,128)(2,1)S(1)} %copy-done.1, ...), custom_call_target="tpu_custom_call", output_to_operand_aliasing={{0}: (13, {})} | custom-call | flops 1000000000 | bytes 1048576 | tf_op jit(solution)/shard_map/pallas_call | solution.py:355
  41.8 34.5 %all_to_all.11 = f32[256,1,128]{2,1,0:T(1,128)S(1)} all-to-all(f32[256,1,128]{2,1,0:T(1,128)S(1)} %bitcast.12), channel_id=1, replica_groups=mesh['seq_0'=4,'seq_1'=8,'seq_2'=2,'head'=4] {'seq_0','seq_1','seq_2','h..., dimensions={0} | all-to-all | bytes 262144 | tf_op jit(solution)/shard_map/all_to_all | solution.py:452
  76.3 0.7 shard_map.81
  (4 shorter events, 0.0 us)
Async XLA Ops:
  1.7 15.0 %collective-permute-start = (bf16[2,512,256]{2,1,0:T(8,128)(2,1)S(1)}, bf16[2,512,256]{2,1,0:T(8,128)(2,1)S(1)}, u32[]{:S(2)}, u32[]{:S(2)}) collective-permute-start(bf16[2,512,256]{2,1,0:T(8,128)(2,1)S(1)} %pad_add_fusion.own_ref), channel_id=1, source_target_pairs={{0,8},{4,12},{8,16},{12,20},{16,24},{20,28},{24,32},{28,36},{32,40... | collective-permute-start | bytes 1572872 | tf_op jit(solution)/shard_map/ppermute | solution.py:392
  16.7 10.2 %collective-permute-start.1 = (bf16[2,512,256]{2,1,0:T(8,128)(2,1)S(1)}, bf16[2,512,256]{2,1,0:T(8,128)(2,1)S(1)}, u32[]{:S(2)}, u32[]{:S(2)}) collective-permute-start(bf16[2,512,256]{2,1,0:T(8,128)(2,1)S(1)} %collective-permute-done.far_ref), channel_id=1, source_target_pairs={{4,12},{12,20},{20,28},{28,36},{36,44},{44,52},{52,60},{60,68},{68... | collective-permute-start | bytes 1572872 | tf_op jit(solution)/shard_map/ppermute | solution.py:392
  20.8 14.6 %collective-permute-start.5 = (bf16[2,512,256]{2,1,0:T(8,128)(2,1)S(1)}, bf16[2,512,256]{2,1,0:T(8,128)(2,1)S(1)}, u32[]{:S(2)}, u32[]{:S(2)}) collective-permute-start(bf16[2,512,256]{2,1,0:T(8,128)(2,1)S(1)} %pad_add_fusion.own_ref), channel_id=1, source_target_pairs={{0,4},{1,5},{2,6},{3,7},{8,12},{9,13},{10,14},{11,15},{16,20},{17,... | collective-permute-start | bytes 1572872 | tf_op jit(solution)/shard_map/ppermute | solution.py:396
  22.1 16.1 %collective-permute-start.4 = (bf16[2,512,256]{2,1,0:T(8,128)(2,1)S(1)}, bf16[2,512,256]{2,1,0:T(8,128)(2,1)S(1)}, u32[]{:S(2)}, u32[]{:S(2)}) collective-permute-start(bf16[2,512,256]{2,1,0:T(8,128)(2,1)S(1)} %collective-permute-done.far_ref), channel_id=1, source_target_pairs={{0,4},{4,0},{1,5},{5,1},{2,6},{6,2},{3,7},{7,3},{8,12},{12,8},{9,1... | collective-permute-start | bytes 1572872 | tf_op jit(solution)/shard_map/ppermute | solution.py:396
  23.3 17.6 %collective-permute-start.2 = (bf16[2,512,256]{2,1,0:T(8,128)(2,1)S(1)}, bf16[2,512,256]{2,1,0:T(8,128)(2,1)S(1)}, u32[]{:S(2)}, u32[]{:S(2)}) collective-permute-start(bf16[2,512,256]{2,1,0:T(8,128)(2,1)S(1)} %collective-permute-done.far_ref), channel_id=1, source_target_pairs={{0,8},{8,16},{16,24},{24,32},{32,40},{40,48},{48,56},{56,64},{64,7... | collective-permute-start | bytes 1572872 | tf_op jit(solution)/shard_map/ppermute | solution.py:392
  26.9 14.1 %collective-permute-start.3 = (bf16[2,512,256]{2,1,0:T(8,128)(2,1)S(1)}, bf16[2,512,256]{2,1,0:T(8,128)(2,1)S(1)}, u32[]{:S(2)}, u32[]{:S(2)}) collective-permute-start(bf16[2,512,256]{2,1,0:T(8,128)(2,1)S(1)} %collective-permute-done.1.odd_ref), channel_id=1, source_target_pairs={{4,0},{5,1},{6,2},{7,3},{12,8},{13,9},{14,10},{15,11},{20,16},{21,... | collective-permute-start | bytes 1572872 | tf_op jit(solution)/shard_map/ppermute | solution.py:396
  29.9 1.2 %copy-start = (bf16[512,1024]{1,0:T(8,128)(2,1)S(1)}, bf16[512,1024]{1,0:T(8,128)(2,1)}, u32[]{:S(2)}) copy-start(bf16[512,1024]{1,0:T(8,128)(2,1)} %q_ref.7) | copy-start | bytes 3145732
  31.1 0.7 copy-start.2
  31.8 0.7 copy-start.3
  32.5 2.9 %copy-start.1 = (bf16[512,1024]{1,0:T(8,128)(2,1)S(1)}, bf16[512,1024]{1,0:T(8,128)(2,1)}, u32[]{:S(2)}) copy-start(bf16[512,1024]{1,0:T(8,128)(2,1)} %q_ref.7) | copy-start | bytes 3145732

commit v8 on v7

--- a/solution.py
+++ b/solution.py
@@ -227,60 +227,93 @@
     return jnp.where(spot_ref[1] == core, -distance * ROWS, NOWHERE)
 
 
-def middle_kernel(
+def side_offset(spot_ref):
+    return jnp.where(spot_ref[1] == 1, -3 * ROWS, -ROWS)
+
+
+def far_kernel(
     spot_ref, hop_ref, doc_ref, q_ref, far_ref, side_ref, first_ref, mark_ref,
-    acc_in, top_in, tot_in, acc_ref, top_ref, tot_ref, out_ref, squares_ref, done_ref, sems,
+    acc_in, top_in, tot_in, acc_ref, top_ref, tot_ref, done_ref, squares_ref,
 ):
     source, state = (acc_in, top_in, tot_in), (acc_ref, top_ref, tot_ref)
-    offsets = (-2 * ROWS, jnp.where(spot_ref[1] == 1, -3 * ROWS, -ROWS))
+    far, side = -2 * ROWS, side_offset(spot_ref)
     squares_ref[...] = jnp.zeros_like(squares_ref)
-
-    def is_late(tile):
-        return late_from(spot_ref, hop_ref, doc_ref, tile * TILE)
 
     def step(pair, carry):
         rows = pair_rows(pair)
-        far, side = [reaches(spot_ref, hop_ref, doc_ref, pair * PAIR, offset) for offset in offsets]
-
-        @pl.when(far)
-        def _():
-            attend_earlier(q_ref, far_ref, first_ref, same(rows), TILE, offsets[0], source, state)
-
-        @pl.when(jnp.logical_not(far))
+        needed = reaches(spot_ref, hop_ref, doc_ref, pair * PAIR, far)
+
+        @pl.when(needed)
+        def _():
+            attend_earlier(q_ref, far_ref, first_ref, same(rows), TILE, far, source, state)
+
+        @pl.when(jnp.logical_not(needed))
         def _():
             for part in rows:
                 copy_tile(source, state, part, part)
 
-        @pl.when(side)
-        def _():
-            attend_earlier(q_ref, side_ref, first_ref, same(rows), TILE, offsets[1], state, state)
-
-        for i, part in enumerate(rows):
-
-            @pl.when(jnp.logical_not(is_late(pair * len(rows) + i)))
-            def _():
-                finish(state, part, TILE, mark_ref, done_ref, squares_ref, part)
-
-        @pl.when(pair > 0)
-        def _():
-            for i in range(len(rows)):
-                send((pair - 1) * len(rows) + i)
-
         return carry
 
-    def send(tile):
-        @pl.when(jnp.logical_not(is_late(tile)))
-        def _():
-            out_copy(done_ref, out_ref, sems, tile).start()
-
     lax.fori_loop(0, ROWS // PAIR, step, 0)
-    for tile in range(TILES - PAIR // TILE, TILES):
-        send(tile)
+
+    @pl.when(reaches(spot_ref, hop_ref, doc_ref, 0, side))
+    def _():
+        attend_earlier(q_ref, side_ref, first_ref, same(pair_rows(0)), TILE, side, state, state)
+
+    for tile in range(PAIR // TILE):
+
+        @pl.when(jnp.logical_not(late_from(spot_ref, hop_ref, doc_ref, tile * TILE)))
+        def _():
+            rows = tile_rows(tile)
+            finish(state, rows, TILE, mark_ref, done_ref, squares_ref, rows)
+
+
+def side_kernel(
+    spot_ref, hop_ref, doc_ref, q_ref, side_ref, first_ref, mark_ref, acc_in, top_in, tot_in,
+    done_in, squares_in, acc_ref, top_ref, tot_ref, out_ref, squares_ref, done_ref, sems,
+):
+    source, state = (acc_in, top_in, tot_in), (acc_ref, top_ref, tot_ref)
+    side = side_offset(spot_ref)
+    early, after = range(PAIR // TILE), range(PAIR // TILE, TILES)
+    squares_ref[...] = squares_in[...]
+
+    def if_done(tile, act):
+        pl.when(jnp.logical_not(late_from(spot_ref, hop_ref, doc_ref, tile * TILE)))(act)
+
+    def moved(tile, act):
+        copy = out_copy(done_in if tile in early else done_ref, out_ref, sems, tile)
+        if_done(tile, getattr(copy, act))
+
+    for tile in early:
+        moved(tile, "start")
+
+        @pl.when(late_from(spot_ref, hop_ref, doc_ref, tile * TILE))
+        def _():
+            copy_tile(source, state, tile_rows(tile), tile_rows(tile))
+
+    rows = pair_rows(1)
+    needed = reaches(spot_ref, hop_ref, doc_ref, PAIR, side)
+
+    @pl.when(needed)
+    def _():
+        attend_earlier(q_ref, side_ref, first_ref, same(rows), TILE, side, source, state)
+
+    @pl.when(jnp.logical_not(needed))
+    def _():
+        for part in rows:
+            copy_tile(source, state, part, part)
+
+    for tile in after:
+
+        def act():
+            part = tile_rows(tile)
+            finish(state, part, TILE, mark_ref, done_ref, squares_ref, part)
+
+        if_done(tile, act)
+    for tile in after:
+        moved(tile, "start")
     for tile in range(TILES):
-
-        @pl.when(jnp.logical_not(is_late(tile)))
-        def _():
-            out_copy(done_ref, out_ref, sems, tile).wait()
+        moved(tile, "wait")
 
 
 def late_from(spot_ref, hop_ref, doc_ref, row):
@@ -421,15 +454,22 @@
     out_shape = jax.ShapeDtypeStruct((ROWS, HEADS * HEAD_WIDTH), jnp.bfloat16)
     copy_scratch = [pltpu.VMEM(out_shape.shape, jnp.bfloat16), pltpu.SemaphoreType.DMA((TILES,))]
     *state, done, squares = call(
-        middle_kernel,
+        far_kernel,
         scalars,
         [queries, far_2, side_2, first, mark, *state],
         state_shapes + [out_shape, f32(8, 128)],
         2 * 10**9,
+    )
+    side_3 = across(odd_4, [(1, 0)])
+    *state, done, squares = call(
+        side_kernel,
+        scalars,
+        [queries, side_2, first, mark, *state, done, squares],
+        state_shapes + [out_shape, f32(8, 128)],
+        10**9,
         scratch=copy_scratch,
         out_hbm=3,
     )
-    side_3 = across(odd_4, [(1, 0)])
     devices = lax.axis_size(SEQ_HEAD)
     arrays = [queries, odd_4, even_4, side_3, first, mark, *state, squares, done]
     attention, share = call(

time: 77.5 us -> 76.7 us (0.990)
  blocking collectives: 34.5 us -> 32.9 us
  Pallas kernels: 10 us -> 10.8 us
    all_to_all x1, blocking collectives: 34.5 us -> 32.9 us  [on_device(): shares = lax.all_to_all(share, SEQ_HEAD, 0, 0, tiled=True)]
    pallas_call x4 -> x5, Pallas kernels: 9.29 us -> 10.1 us  [call(): pl.pallas_call(kernel, out_shape=out_shapes, in_specs=[smem] * len(scalar...]
  transfers between devices with their start and end apart: 6 -> 6, of which waited for: 2 -> 2; matrix products, arithmetic and copies ran while one was open for 0% -> 0% of each run, Pallas kernels for 11% -> 12%
where the time goes in v8:
time: 76.7 us; the launch traced here: 76.4 us
  blocking collectives  32.9 us (43%)
  starting transfers between devices  14.7 us (19%)
  waiting for transfers between devices  12.7 us (17%)
  Pallas kernels  10.8 us (14%)
  local copies, waits for them, and re-layouts  2.59 us (3%)
  between operations  1.57 us (2%)
  other arithmetic  1.14 us (1%)
    all_to_all x1, blocking collectives, on_device(): shares = lax.all_to_all(share, SEQ_HEAD, 0, 0, tiled=True)  32.9 us
    ppermute x3, waiting for transfers between devices, onward(): lax.ppermute(shard, SEQ, [(i, i + 2) for i in blocks if i % 2 in cores])  12.7 us
    pallas_call x5, Pallas kernels, call(): pl.pallas_call(kernel, out_shape=out_shapes, in_specs=[smem] * len(scalar...  10.1 us
    ppermute x3, starting transfers between devices, onward(): lax.ppermute(shard, SEQ, [(i, i + 2) for i in blocks if i % 2 in cores])  9.2 us
    ppermute x3, starting transfers between devices, across(): return lax.ppermute(shard, 'seq_2', pairs)  5.51 us
    unnamed x8, local copies, waits for them, and re-layouts  2.59 us
  transfers between devices with their start and end apart: 6, of which 2 were waited for; matrix products, arithmetic and copies ran while one was open for 0% of the time, Pallas kernels for 12%

profile of v8, /device:TPU:1, one launch (start us, length us, event | category | flops | bytes accessed | tf_op | source)
XLA Modules:
  0.0 76.4 jit_solution(14041630166526728739)
XLA Ops:
  0.6 1.1 %pad_add_fusion.own_ref = bf16[2,512,256]{2,1,0:T(8,128)(2,1)S(1)} fusion(bf16[1,512,256]{2,1,0:T(8,128)(2,1)} %bitcast.15, bf16[1,512,256]{2,1,0:T(8,128)(2,1)} %bitcast.16), kind=kLoop, calls=%fused_computation | loop fusion | flops 262144 | bytes 1048576 | tf_op jit(solution)/shard_map/add | solution.py:402
  1.7 4.4 %collective-permute-start = (bf16[2,512,256]{2,1,0:T(8,128)(2,1)S(1)}, bf16[2,512,256]{2,1,0:T(8,128)(2,1)S(1)}, u32[]{:S(2)}, u32[]{:S(2)}) collective-permute-start(bf16[2,512,256]{2,1,0:T(8,128)(2,1)S(1)} %pad_add_fusion.own_ref), channel_id=1, source_target_pairs={{0,8},{4,12},{8,16},{12,20},{16,24},{20,28},{24,32},{28,36},{32,40... | collective-permute-start | bytes 1572872 | tf_op jit(solution)/shard_map/ppermute | solution.py:425
  6.1 10.6 %collective-permute-done.far_ref = bf16[2,512,256]{2,1,0:T(8,128)(2,1)S(1)} collective-permute-done((bf16[2,512,256]{2,1,0:T(8,128)(2,1)S(1)}, bf16[2,512,256]{2,1,0:T(8,128)(2,1)S(1)}, u32[]{:S(2)}, u32[]{:S(2)}) %collective-permute-start) | collective-permute-done | bytes 524320 | tf_op jit(solution)/shard_map/ppermute | solution.py:425
  16.7 4.1 %collective-permute-start.1 = (bf16[2,512,256]{2,1,0:T(8,128)(2,1)S(1)}, bf16[2,512,256]{2,1,0:T(8,128)(2,1)S(1)}, u32[]{:S(2)}, u32[]{:S(2)}) collective-permute-start(bf16[2,512,256]{2,1,0:T(8,128)(2,1)S(1)} %collective-permute-done.far_ref), channel_id=1, source_target_pairs={{4,12},{12,20},{20,28},{28,36},{36,44},{44,52},{52,60},{60,68},{68... | collective-permute-start | bytes 1572872 | tf_op jit(solution)/shard_map/ppermute | solution.py:425
  20.8 1.3 %collective-permute-start.5 = (bf16[2,512,256]{2,1,0:T(8,128)(2,1)S(1)}, bf16[2,512,256]{2,1,0:T(8,128)(2,1)S(1)}, u32[]{:S(2)}, u32[]{:S(2)}) collective-permute-start(bf16[2,512,256]{2,1,0:T(8,128)(2,1)S(1)} %pad_add_fusion.own_ref), channel_id=1, source_target_pairs={{0,4},{1,5},{2,6},{3,7},{8,12},{9,13},{10,14},{11,15},{16,20},{17,... | collective-permute-start | bytes 1572872 | tf_op jit(solution)/shard_map/ppermute | solution.py:429
  22.1 1.2 %collective-permute-start.4 = (bf16[2,512,256]{2,1,0:T(8,128)(2,1)S(1)}, bf16[2,512,256]{2,1,0:T(8,128)(2,1)S(1)}, u32[]{:S(2)}, u32[]{:S(2)}) collective-permute-start(bf16[2,512,256]{2,1,0:T(8,128)(2,1)S(1)} %collective-permute-done.far_ref), channel_id=1, source_target_pairs={{0,4},{4,0},{1,5},{5,1},{2,6},{6,2},{3,7},{7,3},{8,12},{12,8},{9,1... | collective-permute-start | bytes 1572872 | tf_op jit(solution)/shard_map/ppermute | solution.py:429
  24.0 0.1 pad_add_fusion.1.spot_ref
  24.1 0.7 collective-permute-start.2
  24.8 2.1 %collective-permute-done.1.odd_ref = bf16[2,512,256]{2,1,0:T(8,128)(2,1)S(1)} collective-permute-done((bf16[2,512,256]{2,1,0:T(8,128)(2,1)S(1)}, bf16[2,512,256]{2,1,0:T(8,128)(2,1)S(1)}, u32[]{:S(2)}, u32[]{:S(2)}) %collective-permute-start.1) | collective-permute-done | bytes 524320 | tf_op jit(solution)/shard_map/ppermute | solution.py:425
  26.9 3.0 %collective-permute-start.3 = (bf16[2,512,256]{2,1,0:T(8,128)(2,1)S(1)}, bf16[2,512,256]{2,1,0:T(8,128)(2,1)S(1)}, u32[]{:S(2)}, u32[]{:S(2)}) collective-permute-start(bf16[2,512,256]{2,1,0:T(8,128)(2,1)S(1)} %collective-permute-done.1.odd_ref), channel_id=1, source_target_pairs={{4,0},{5,1},{6,2},{7,3},{12,8},{13,9},{14,10},{15,11},{20,16},{21,... | collective-permute-start | bytes 1572872 | tf_op jit(solution)/shard_map/ppermute | solution.py:429
  29.9 0.0 copy-start
  29.9 1.2 %copy-done = bf16[512,1024]{1,0:T(8,128)(2,1)S(1)} copy-done((bf16[512,1024]{1,0:T(8,128)(2,1)S(1)}, bf16[512,1024]{1,0:T(8,128)(2,1)}, u32[]{:S(2)}) %copy-start) | copy-done | bytes 1048600
  31.1 0.7 copy-done.2
  31.8 0.7 copy-done.3
  32.4 2.9 %shard_map.77 = (f32[512,1024]{1,0:T(8,128)S(1)}, f32[8,512,128]{2,1,0:T(8,128)S(1)}, f32[8,512,128]{2,1,0:T(8,128)S(1)}, f32[512,128]{1,0:T(8,128)S(1)}, f32[512,128]{1,0:T(8,128)S(1)}) custom-call(s32[2]{0:T(128)S(1)} %pad_add_fusion.1.spot_ref, s32[1]{0:T(128)S(6)} %copy.11.hop_ref, s32[512]{0:T(512)S(1)} %copy-done.2, s32[4,128]{1,0:T(4,128)S(1)} %bitcast.13, ...), custom_call_target="tpu_custom_call" | custom-call | flops 2000000000 | bytes 1048576 | tf_op jit(solution)/shard_map/pallas_call | solution.py:388
  35.3 0.0 collective-permute-done.5.near_ref
  35.4 2.7 %shard_map.78 = (f32[512,1024]{1,0:T(8,128)S(1)}, f32[8,512,128]{2,1,0:T(8,128)S(1)}, f32[8,512,128]{2,1,0:T(8,128)S(1)}) custom-call(s32[2]{0:T(128)S(1)} %pad_add_fusion.1.spot_ref, s32[1]{0:T(128)S(6)} %copy.11.hop_ref, s32[512]{0:T(512)S(1)} %copy-done.2, bf16[512,1024]{1,0:T(8,128)(2,1)S(1)} %copy-done.1, ...), custom_call_target="tpu_custom_call" | custom-call | flops 1000000000 | bytes 1048576 | tf_op jit(solution)/shard_map/pallas_call | solution.py:388
  38.1 0.0 collective-permute-done.4.side_ref
  38.1 1.4 %shard_map.79 = (f32[512,1024]{1,0:T(8,128)S(1)}, f32[8,512,128]{2,1,0:T(8,128)S(1)}, f32[8,512,128]{2,1,0:T(8,128)S(1)}, bf16[512,1024]{1,0:T(8,128)(2,1)S(1)}, f32[8,128]{1,0:T(8,128)S(1)}) custom-call(s32[2]{0:T(128)S(1)} %pad_add_fusion.1.spot_ref, s32[1]{0:T(128)S(6)} %copy.11.hop_ref, s32[512]{0:T(512)S(1)} %copy-done.2, ...), custom_call_target="tpu_custom_call" | custom-call | flops 2000000000 | bytes 1048576 | tf_op jit(solution)/shard_map/pallas_call | solution.py:388
  39.5 2.2 %shard_map.80 = (f32[512,1024]{1,0:T(8,128)S(1)}, f32[8,512,128]{2,1,0:T(8,128)S(1)}, f32[8,512,128]{2,1,0:T(8,128)S(1)}, bf16[512,1024]{1,0:T(8,128)(2,1)}, f32[8,128]{1,0:T(8,128)S(1)}) custom-call(s32[2]{0:T(128)S(1)} %pad_add_fusion.1.spot_ref, s32[1]{0:T(128)S(6)} %copy.11.hop_ref, s32[512]{0:T(512)S(1)} %copy-done.2, bf16[512,1024]{1,0:T(8,128)(2,1)S(1)} %copy-done.1, ...), custom_call_target="tpu_custom_call" | custom-call | flops 1000000000 | bytes 1048576 | tf_op jit(solution)/shard_map/pallas_call | solution.py:388
  41.7 0.0 collective-permute-done.2.even_ref
  41.7 0.9 %shard_map.81 = (bf16[512,1024]{1,0:T(8,128)(2,1)}, f32[256,128]{1,0:T(8,128)S(1)}) custom-call(s32[2]{0:T(128)S(1)} %pad_add_fusion.1.spot_ref, s32[1]{0:T(128)S(6)} %copy.11.hop_ref, s32[512]{0:T(512)S(1)} %copy-done.2, bf16[512,1024]{1,0:T(8,128)(2,1)S(1)} %copy-done.1, ...), custom_call_target="tpu_custom_call", output_to_operand_aliasing={{0}: (13, {})} | custom-call | flops 1000000000 | bytes 1048576 | tf_op jit(solution)/shard_map/pallas_call | solution.py:388
  42.6 32.9 %all_to_all.11 = f32[256,1,128]{2,1,0:T(1,128)S(1)} all-to-all(f32[256,1,128]{2,1,0:T(1,128)S(1)} %bitcast.12), channel_id=1, replica_groups=mesh['seq_0'=4,'seq_1'=8,'seq_2'=2,'head'=4] {'seq_0','seq_1','seq_2','h..., dimensions={0} | all-to-all | bytes 262144 | tf_op jit(solution)/shard_map/all_to_all | solution.py:492
  75.5 0.7 shard_map.82
  (5 shorter events, 0.0 us)
Async XLA Ops:
  1.7 15.0 %collective-permute-start = (bf16[2,512,256]{2,1,0:T(8,128)(2,1)S(1)}, bf16[2,512,256]{2,1,0:T(8,128)(2,1)S(1)}, u32[]{:S(2)}, u32[]{:S(2)}) collective-permute-start(bf16[2,512,256]{2,1,0:T(8,128)(2,1)S(1)} %pad_add_fusion.own_ref), channel_id=1, source_target_pairs={{0,8},{4,12},{8,16},{12,20},{16,24},{20,28},{24,32},{28,36},{32,40... | collective-permute-start | bytes 1572872 | tf_op jit(solution)/shard_map/ppermute | solution.py:425
  16.7 10.2 %collective-permute-start.1 = (bf16[2,512,256]{2,1,0:T(8,128)(2,1)S(1)}, bf16[2,512,256]{2,1,0:T(8,128)(2,1)S(1)}, u32[]{:S(2)}, u32[]{:S(2)}) collective-permute-start(bf16[2,512,256]{2,1,0:T(8,128)(2,1)S(1)} %collective-permute-done.far_ref), channel_id=1, source_target_pairs={{4,12},{12,20},{20,28},{28,36},{36,44},{44,52},{52,60},{60,68},{68... | collective-permute-start | bytes 1572872 | tf_op jit(solution)/shard_map/ppermute | solution.py:425
  20.8 14.5 %collective-permute-start.5 = (bf16[2,512,256]{2,1,0:T(8,128)(2,1)S(1)}, bf16[2,512,256]{2,1,0:T(8,128)(2,1)S(1)}, u32[]{:S(2)}, u32[]{:S(2)}) collective-permute-start(bf16[2,512,256]{2,1,0:T(8,128)(2,1)S(1)} %pad_add_fusion.own_ref), channel_id=1, source_target_pairs={{0,4},{1,5},{2,6},{3,7},{8,12},{9,13},{10,14},{11,15},{16,20},{17,... | collective-permute-start | bytes 1572872 | tf_op jit(solution)/shard_map/ppermute | solution.py:429
  22.1 16.0 %collective-permute-start.4 = (bf16[2,512,256]{2,1,0:T(8,128)(2,1)S(1)}, bf16[2,512,256]{2,1,0:T(8,128)(2,1)S(1)}, u32[]{:S(2)}, u32[]{:S(2)}) collective-permute-start(bf16[2,512,256]{2,1,0:T(8,128)(2,1)S(1)} %collective-permute-done.far_ref), channel_id=1, source_target_pairs={{0,4},{4,0},{1,5},{5,1},{2,6},{6,2},{3,7},{7,3},{8,12},{12,8},{9,1... | collective-permute-start | bytes 1572872 | tf_op jit(solution)/shard_map/ppermute | solution.py:429
  24.1 17.6 %collective-permute-start.2 = (bf16[2,512,256]{2,1,0:T(8,128)(2,1)S(1)}, bf16[2,512,256]{2,1,0:T(8,128)(2,1)S(1)}, u32[]{:S(2)}, u32[]{:S(2)}) collective-permute-start(bf16[2,512,256]{2,1,0:T(8,128)(2,1)S(1)} %collective-permute-done.far_ref), channel_id=1, source_target_pairs={{0,8},{8,16},{16,24},{24,32},{32,40},{40,48},{48,56},{56,64},{64,7... | collective-permute-start | bytes 1572872 | tf_op jit(solution)/shard_map/ppermute | solution.py:425
  26.9 14.8 %collective-permute-start.3 = (bf16[2,512,256]{2,1,0:T(8,128)(2,1)S(1)}, bf16[2,512,256]{2,1,0:T(8,128)(2,1)S(1)}, u32[]{:S(2)}, u32[]{:S(2)}) collective-permute-start(bf16[2,512,256]{2,1,0:T(8,128)(2,1)S(1)} %collective-permute-done.1.odd_ref), channel_id=1, source_target_pairs={{4,0},{5,1},{6,2},{7,3},{12,8},{13,9},{14,10},{15,11},{20,16},{21,... | collective-permute-start | bytes 1572872 | tf_op jit(solution)/shard_map/ppermute | solution.py:429
  29.9 1.2 %copy-start = (bf16[512,1024]{1,0:T(8,128)(2,1)S(1)}, bf16[512,1024]{1,0:T(8,128)(2,1)}, u32[]{:S(2)}) copy-start(bf16[512,1024]{1,0:T(8,128)(2,1)} %q_ref.9) | copy-start | bytes 3145732
  31.1 0.7 copy-start.2
  31.8 0.7 copy-start.3
  32.4 2.9 %copy-start.1 = (bf16[512,1024]{1,0:T(8,128)(2,1)S(1)}, bf16[512,1024]{1,0:T(8,128)(2,1)}, u32[]{:S(2)}) copy-start(bf16[512,1024]{1,0:T(8,128)(2,1)} %q_ref.9) | copy-start | bytes 3145732

commit v9 on v8

--- a/solution.py
+++ b/solution.py
@@ -437,8 +437,9 @@
     spot = jnp.stack([lax.axis_index(SEQ) * ROWS, lax.axis_index("seq_2")])
     scalars = [spot, hop_counts, doc_start]
     own = packed(keys, values)
-    far_2 = onward(own, (0, 1))
+    odd_2 = onward(own, (1,))
     side_1 = across(own, [(0, 1)])
+    even_2 = onward(own, (0,))
     state_shapes = [f32(ROWS, HEADS * HEAD_WIDTH), f32(HEADS, ROWS, 128), f32(HEADS, ROWS, 128)]
     *state, first, mark = call(
         first_kernel,
@@ -447,10 +448,11 @@
         state_shapes + [f32(ROWS, 128)] * 2,
         2 * 10**9,
     )
+    odd_4 = onward(odd_2, (1,))
     state = call(near_kernel, scalars, [queries, side_1, first, *state], state_shapes, 10**9)
-    odd_4 = onward(far_2, (1,))
+    even_4 = onward(even_2, (0,))
+    far_2 = odd_2 + even_2
     side_2 = across(far_2, [(0, 1), (1, 0)])
-    even_4 = onward(far_2, (0,))
     out_shape = jax.ShapeDtypeStruct((ROWS, HEADS * HEAD_WIDTH), jnp.bfloat16)
     copy_scratch = [pltpu.VMEM(out_shape.shape, jnp.bfloat16), pltpu.SemaphoreType.DMA((TILES,))]
     *state, done, squares = call(

time: 76.7 us -> 76.3 us (level)
  waiting for transfers between devices: 12.7 us -> 8.43 us
  starting transfers between devices: 14.7 us -> 17.7 us
  other arithmetic: 1.14 us -> 3.2 us
  local copies, waits for them, and re-layouts: 2.59 us -> 0.8 us
    ppermute x3 -> x4, waiting for transfers between devices: 12.7 us -> 8.42 us  [onward(): lax.ppermute(shard, SEQ, [(i, i + 2) for i in blocks if i % 2 in cores])]
    unnamed x8, local copies, waits for them, and re-layouts: 2.59 us -> 0.8 us
    ppermute x3, starting transfers between devices: 5.51 us -> 7.19 us  [across(): return lax.ppermute(shard, 'seq_2', pairs)]
    ppermute x3 -> x4, starting transfers between devices: 9.2 us -> 10.5 us  [onward(): lax.ppermute(shard, SEQ, [(i, i + 2) for i in blocks if i % 2 in cores])]
    add x0 -> x1, other arithmetic: none -> 1.18 us  [on_device(): far_2 = odd_2 + even_2]
    add x1, other arithmetic: 1.07 us -> 1.95 us  [packed(): jnp.pad(keys[None], ((0, 1), *pads))]
  transfers between devices with their start and end apart: 6 -> 7, of which waited for: 2 -> 2; matrix products, arithmetic and copies ran while one was open for 0% -> 2% of each run, Pallas kernels for 12% -> 13%
where the time goes in v9:
time: 76.3 us; the launch traced here: 76 us
  blocking collectives  32.9 us (43%)
  starting transfers between devices  17.7 us (23%)
  Pallas kernels  11.3 us (15%)
  waiting for transfers between devices  8.43 us (11%)
  other arithmetic  3.2 us (4%)
  between operations  1.62 us (2%)
  local copies, waits for them, and re-layouts  0.8 us (1%)
    all_to_all x1, blocking collectives, on_device(): shares = lax.all_to_all(share, SEQ_HEAD, 0, 0, tiled=True)  32.9 us
    pallas_call x5, Pallas kernels, call(): pl.pallas_call(kernel, out_shape=out_shapes, in_specs=[smem] * len(scalar...  10.5 us
    ppermute x4, starting transfers between devices, onward(): lax.ppermute(shard, SEQ, [(i, i + 2) for i in blocks if i % 2 in cores])  10.5 us
    ppermute x4, waiting for transfers between devices, onward(): lax.ppermute(shard, SEQ, [(i, i + 2) for i in blocks if i % 2 in cores])  8.42 us
    ppermute x3, starting transfers between devices, across(): return lax.ppermute(shard, 'seq_2', pairs)  7.19 us
    add x1, other arithmetic, packed(): jnp.pad(keys[None], ((0, 1), *pads))  1.95 us
  transfers between devices with their start and end apart: 7, of which 2 were waited for; matrix products, arithmetic and copies ran while one was open for 2% of the time, Pallas kernels for 13%

profile of v9, /device:TPU:1, one launch (start us, length us, event | category | flops | bytes accessed | tf_op | source)
XLA Modules:
  0.0 76.0 jit_solution(5809882990244401904)
XLA Ops:
  0.7 1.9 %pad_add_fusion.own_ref = bf16[2,512,256]{2,1,0:T(8,128)(2,1)} fusion(bf16[1,512,256]{2,1,0:T(8,128)(2,1)} %bitcast.15, bf16[1,512,256]{2,1,0:T(8,128)(2,1)} %bitcast.16), kind=kLoop, calls=%fused_computation | loop fusion | flops 262144 | bytes 1048576 | tf_op jit(solution)/shard_map/add | solution.py:402
  2.6 5.1 %collective-permute-start = (bf16[2,512,256]{2,1,0:T(8,128)(2,1)}, bf16[2,512,256]{2,1,0:T(8,128)(2,1)}, u32[]{:S(2)}, u32[]{:S(2)}) collective-permute-start(bf16[2,512,256]{2,1,0:T(8,128)(2,1)} %pad_add_fusion.own_ref), channel_id=1, source_target_pairs={{4,12},{12,20},{20,28},{28,36},{36,44},{44,52},{52,60},{60,68},{68... | collective-permute-start | bytes 1572872 | tf_op jit(solution)/shard_map/ppermute | solution.py:425
  7.8 0.7 collective-permute-start.2
  8.4 8.0 %collective-permute-done = bf16[2,512,256]{2,1,0:T(8,128)(2,1)} collective-permute-done((bf16[2,512,256]{2,1,0:T(8,128)(2,1)}, bf16[2,512,256]{2,1,0:T(8,128)(2,1)}, u32[]{:S(2)}, u32[]{:S(2)}) %collective-permute-start) | collective-permute-done | bytes 524320 | tf_op jit(solution)/shard_map/ppermute | solution.py:425
  16.4 4.0 %collective-permute-start.1 = (bf16[2,512,256]{2,1,0:T(8,128)(2,1)}, bf16[2,512,256]{2,1,0:T(8,128)(2,1)S(1)}, u32[]{:S(2)}, u32[]{:S(2)}) collective-permute-start(bf16[2,512,256]{2,1,0:T(8,128)(2,1)} %collective-permute-done), channel_id=1, source_target_pairs={{4,12},{12,20},{20,28},{28,36},{36,44},{44,52},{52,60},{60,68},{68... | collective-permute-start | bytes 1572872 | tf_op jit(solution)/shard_map/ppermute | solution.py:425
  20.5 1.3 %collective-permute-start.6 = (bf16[2,512,256]{2,1,0:T(8,128)(2,1)}, bf16[2,512,256]{2,1,0:T(8,128)(2,1)S(1)}, u32[]{:S(2)}, u32[]{:S(2)}) collective-permute-start(bf16[2,512,256]{2,1,0:T(8,128)(2,1)} %pad_add_fusion.own_ref), channel_id=1, source_target_pairs={{0,4},{1,5},{2,6},{3,7},{8,12},{9,13},{10,14},{11,15},{16,20},{17,... | collective-permute-start | bytes 1572872 | tf_op jit(solution)/shard_map/ppermute | solution.py:429
  21.8 0.0 collective-permute-done.2
  21.8 0.8 %copy-done.3 = bf16[2,512,256]{2,1,0:T(8,128)(2,1)} copy-done((bf16[2,512,256]{2,1,0:T(8,128)(2,1)}, bf16[2,512,256]{2,1,0:T(8,128)(2,1)S(1)}, u32[]{:S(2)}) %copy-start.3) | copy-done | bytes 524312
  22.6 1.2 %add.19.far_ref = bf16[2,512,256]{2,1,0:T(8,128)(2,1)S(1)} add(bf16[2,512,256]{2,1,0:T(8,128)(2,1)} %collective-permute-done, bf16[2,512,256]{2,1,0:T(8,128)(2,1)S(1)} %collective-permute-done.2) | non-fusion elementwise | flops 262144 | bytes 1572864 | tf_op jit(solution)/shard_map/add | solution.py:454
  23.7 1.2 %collective-permute-start.5 = (bf16[2,512,256]{2,1,0:T(8,128)(2,1)S(1)}, bf16[2,512,256]{2,1,0:T(8,128)(2,1)S(1)}, u32[]{:S(2)}, u32[]{:S(2)}) collective-permute-start(bf16[2,512,256]{2,1,0:T(8,128)(2,1)S(1)} %add.19.far_ref), channel_id=1, source_target_pairs={{0,4},{4,0},{1,5},{5,1},{2,6},{6,2},{3,7},{7,3},{8,12},{12,8},{9,1... | collective-permute-start | bytes 1572872 | tf_op jit(solution)/shard_map/ppermute | solution.py:429
  25.6 0.1 pad_add_fusion.1.spot_ref
  25.7 0.7 collective-permute-start.3
  26.4 0.4 collective-permute-done.1.odd_ref
  26.8 4.7 %collective-permute-start.4 = (bf16[2,512,256]{2,1,0:T(8,128)(2,1)S(1)}, bf16[2,512,256]{2,1,0:T(8,128)(2,1)S(1)}, u32[]{:S(2)}, u32[]{:S(2)}) collective-permute-start(bf16[2,512,256]{2,1,0:T(8,128)(2,1)S(1)} %collective-permute-done.1.odd_ref), channel_id=1, source_target_pairs={{4,0},{5,1},{6,2},{7,3},{12,8},{13,9},{14,10},{15,11},{20,16},{21,... | collective-permute-start | bytes 1572872 | tf_op jit(solution)/shard_map/ppermute | solution.py:429
  31.5 3.4 %shard_map.77 = (f32[512,1024]{1,0:T(8,128)S(1)}, f32[8,512,128]{2,1,0:T(8,128)S(1)}, f32[8,512,128]{2,1,0:T(8,128)S(1)}, f32[512,128]{1,0:T(8,128)S(1)}, f32[512,128]{1,0:T(8,128)S(1)}) custom-call(s32[2]{0:T(128)S(1)} %pad_add_fusion.1.spot_ref, s32[1]{0:T(128)S(6)} %copy.11.hop_ref, s32[512]{0:T(512)S(1)} %copy-done.1, s32[4,128]{1,0:T(4,128)S(1)} %bitcast.13, ...), custom_call_target="tpu_custom_call" | custom-call | flops 2000000000 | bytes 1048576 | tf_op jit(solution)/shard_map/pallas_call | solution.py:388
  34.9 0.0 collective-permute-done.6.near_ref
  34.9 2.7 %shard_map.78 = (f32[512,1024]{1,0:T(8,128)S(1)}, f32[8,512,128]{2,1,0:T(8,128)S(1)}, f32[8,512,128]{2,1,0:T(8,128)S(1)}) custom-call(s32[2]{0:T(128)S(1)} %pad_add_fusion.1.spot_ref, s32[1]{0:T(128)S(6)} %copy.11.hop_ref, s32[512]{0:T(512)S(1)} %copy-done.1, bf16[512,1024]{1,0:T(8,128)(2,1)S(1)} %copy-done, ...), custom_call_target="tpu_custom_call" | custom-call | flops 1000000000 | bytes 1048576 | tf_op jit(solution)/shard_map/pallas_call | solution.py:388
  37.6 0.0 collective-permute-done.5.side_ref
  37.7 1.4 %shard_map.79 = (f32[512,1024]{1,0:T(8,128)S(1)}, f32[8,512,128]{2,1,0:T(8,128)S(1)}, f32[8,512,128]{2,1,0:T(8,128)S(1)}, bf16[512,1024]{1,0:T(8,128)(2,1)S(1)}, f32[8,128]{1,0:T(8,128)S(1)}) custom-call(s32[2]{0:T(128)S(1)} %pad_add_fusion.1.spot_ref, s32[1]{0:T(128)S(6)} %copy.11.hop_ref, s32[512]{0:T(512)S(1)} %copy-done.1, ...), custom_call_target="tpu_custom_call" | custom-call | flops 2000000000 | bytes 1048576 | tf_op jit(solution)/shard_map/pallas_call | solution.py:388
  39.1 2.2 %shard_map.80 = (f32[512,1024]{1,0:T(8,128)S(1)}, f32[8,512,128]{2,1,0:T(8,128)S(1)}, f32[8,512,128]{2,1,0:T(8,128)S(1)}, bf16[512,1024]{1,0:T(8,128)(2,1)}, f32[8,128]{1,0:T(8,128)S(1)}) custom-call(s32[2]{0:T(128)S(1)} %pad_add_fusion.1.spot_ref, s32[1]{0:T(128)S(6)} %copy.11.hop_ref, s32[512]{0:T(512)S(1)} %copy-done.1, bf16[512,1024]{1,0:T(8,128)(2,1)S(1)} %copy-done, ...), custom_call_target="tpu_custom_call" | custom-call | flops 1000000000 | bytes 1048576 | tf_op jit(solution)/shard_map/pallas_call | solution.py:388
  41.2 0.0 collective-permute-done.3.even_ref
  41.2 0.9 %shard_map.81 = (bf16[512,1024]{1,0:T(8,128)(2,1)}, f32[256,128]{1,0:T(8,128)S(1)}) custom-call(s32[2]{0:T(128)S(1)} %pad_add_fusion.1.spot_ref, s32[1]{0:T(128)S(6)} %copy.11.hop_ref, s32[512]{0:T(512)S(1)} %copy-done.1, bf16[512,1024]{1,0:T(8,128)(2,1)S(1)} %copy-done, ...), custom_call_target="tpu_custom_call", output_to_operand_aliasing={{0}: (13, {})} | custom-call | flops 1000000000 | bytes 1048576 | tf_op jit(solution)/shard_map/pallas_call | solution.py:388
  42.2 32.9 %all_to_all.11 = f32[256,1,128]{2,1,0:T(1,128)S(1)} all-to-all(f32[256,1,128]{2,1,0:T(1,128)S(1)} %bitcast.12), channel_id=1, replica_groups=mesh['seq_0'=4,'seq_1'=8,'seq_2'=2,'head'=4] {'seq_0','seq_1','seq_2','h..., dimensions={0} | all-to-all | bytes 262144 | tf_op jit(solution)/shard_map/all_to_all | solution.py:494
  75.1 0.7 shard_map.82
  (8 shorter events, 0.0 us)
Async XLA Ops:
  0.6 30.9 %copy-start.1 = (s32[512]{0:T(512)S(1)}, s32[512]{0:T(512)}, u32[]{:S(2)}) copy-start(s32[512]{0:T(512)} %doc_ref.9) | copy-start | bytes 6148
  0.6 30.9 %copy-start.2 = (s32[512]{0:T(512)S(1)}, s32[512]{0:T(512)}, u32[]{:S(2)}) copy-start(s32[512]{0:T(512)} %param.11) | copy-start | bytes 6148
  0.7 30.9 %copy-start = (bf16[512,1024]{1,0:T(8,128)(2,1)S(1)}, bf16[512,1024]{1,0:T(8,128)(2,1)}, u32[]{:S(2)}) copy-start(bf16[512,1024]{1,0:T(8,128)(2,1)} %q_ref.9) | copy-start | bytes 3145732
  2.6 13.8 %collective-permute-start = (bf16[2,512,256]{2,1,0:T(8,128)(2,1)}, bf16[2,512,256]{2,1,0:T(8,128)(2,1)}, u32[]{:S(2)}, u32[]{:S(2)}) collective-permute-start(bf16[2,512,256]{2,1,0:T(8,128)(2,1)} %pad_add_fusion.own_ref), channel_id=1, source_target_pairs={{4,12},{12,20},{20,28},{28,36},{36,44},{44,52},{52,60},{60,68},{68... | collective-permute-start | bytes 1572872 | tf_op jit(solution)/shard_map/ppermute | solution.py:425
  7.8 14.0 %collective-permute-start.2 = (bf16[2,512,256]{2,1,0:T(8,128)(2,1)}, bf16[2,512,256]{2,1,0:T(8,128)(2,1)S(1)}, u32[]{:S(2)}, u32[]{:S(2)}) collective-permute-start(bf16[2,512,256]{2,1,0:T(8,128)(2,1)} %pad_add_fusion.own_ref), channel_id=1, source_target_pairs={{0,8},{8,16},{16,24},{24,32},{32,40},{40,48},{48,56},{56,64},{64,7... | collective-permute-start | bytes 1572872 | tf_op jit(solution)/shard_map/ppermute | solution.py:425
  16.4 10.4 %collective-permute-start.1 = (bf16[2,512,256]{2,1,0:T(8,128)(2,1)}, bf16[2,512,256]{2,1,0:T(8,128)(2,1)S(1)}, u32[]{:S(2)}, u32[]{:S(2)}) collective-permute-start(bf16[2,512,256]{2,1,0:T(8,128)(2,1)} %collective-permute-done), channel_id=1, source_target_pairs={{4,12},{12,20},{20,28},{28,36},{36,44},{44,52},{52,60},{60,68},{68... | collective-permute-start | bytes 1572872 | tf_op jit(solution)/shard_map/ppermute | solution.py:425
  20.5 14.5 %collective-permute-start.6 = (bf16[2,512,256]{2,1,0:T(8,128)(2,1)}, bf16[2,512,256]{2,1,0:T(8,128)(2,1)S(1)}, u32[]{:S(2)}, u32[]{:S(2)}) collective-permute-start(bf16[2,512,256]{2,1,0:T(8,128)(2,1)} %pad_add_fusion.own_ref), channel_id=1, source_target_pairs={{0,4},{1,5},{2,6},{3,7},{8,12},{9,13},{10,14},{11,15},{16,20},{17,... | collective-permute-start | bytes 1572872 | tf_op jit(solution)/shard_map/ppermute | solution.py:429
  21.8 0.8 %copy-start.3 = (bf16[2,512,256]{2,1,0:T(8,128)(2,1)}, bf16[2,512,256]{2,1,0:T(8,128)(2,1)S(1)}, u32[]{:S(2)}) copy-start(bf16[2,512,256]{2,1,0:T(8,128)(2,1)S(1)} %collective-permute-done.2) | copy-start | bytes 1572868
  23.7 13.9 %collective-permute-start.5 = (bf16[2,512,256]{2,1,0:T(8,128)(2,1)S(1)}, bf16[2,512,256]{2,1,0:T(8,128)(2,1)S(1)}, u32[]{:S(2)}, u32[]{:S(2)}) collective-permute-start(bf16[2,512,256]{2,1,0:T(8,128)(2,1)S(1)} %add.19.far_ref), channel_id=1, source_target_pairs={{0,4},{4,0},{1,5},{5,1},{2,6},{6,2},{3,7},{7,3},{8,12},{12,8},{9,1... | collective-permute-start | bytes 1572872 | tf_op jit(solution)/shard_map/ppermute | solution.py:429
  25.7 15.5 %collective-permute-start.3 = (bf16[2,512,256]{2,1,0:T(8,128)(2,1)}, bf16[2,512,256]{2,1,0:T(8,128)(2,1)S(1)}, u32[]{:S(2)}, u32[]{:S(2)}) collective-permute-start(bf16[2,512,256]{2,1,0:T(8,128)(2,1)} %copy-done.3), channel_id=1, source_target_pairs={{0,8},{8,16},{16,24},{24,32},{32,40},{40,48},{48,56},{56,64},{64,7... | collective-permute-start | bytes 1572872 | tf_op jit(solution)/shard_map/ppermute | solution.py:425
  26.8 14.4 %collective-permute-start.4 = (bf16[2,512,256]{2,1,0:T(8,128)(2,1)S(1)}, bf16[2,512,256]{2,1,0:T(8,128)(2,1)S(1)}, u32[]{:S(2)}, u32[]{:S(2)}) collective-permute-start(bf16[2,512,256]{2,1,0:T(8,128)(2,1)S(1)} %collective-permute-done.1.odd_ref), channel_id=1, source_target_pairs={{4,0},{5,1},{6,2},{7,3},{12,8},{13,9},{14,10},{15,11},{20,16},{21,... | collective-permute-start | bytes 1572872 | tf_op jit(solution)/shard_map/ppermute | solution.py:429

commit v10 on v9

--- a/solution.py
+++ b/solution.py
@@ -155,8 +155,8 @@
 
 
 def first_kernel(
-    spot_ref, hop_ref, doc_ref, starts_ref, marks_ref, q_ref, own_ref,
-    acc_ref, top_ref, tot_ref, first_ref, mark_ref,
+    spot_ref, hop_ref, doc_ref, starts_ref, q_ref, own_ref,
+    acc_ref, top_ref, tot_ref, first_ref,
 ):
     floor = spot_ref[0] - hop_ref[0] * ROWS
     state = (acc_ref, top_ref, tot_ref)
@@ -167,8 +167,6 @@
         starts = jnp.maximum(starts_ref[tile : tile + 1, :], floor) - spot_ref[0]
         first = jnp.broadcast_to(starts.astype(jnp.float32), (TILE, 128)).T
         first_ref[rows, :] = first
-        marks = marks_ref[tile : tile + 1, :].astype(jnp.float32)
-        mark_ref[rows, :] = jnp.broadcast_to(marks, (TILE, 128)).T
         place = lax.broadcasted_iota(jnp.int32, (TILE, width), 1)
         row = lax.broadcasted_iota(jnp.int32, (TILE, width), 0) + tile * TILE
         seen = (place.astype(jnp.float32) >= widened(first, width)) & (place <= row)
@@ -198,20 +196,14 @@
     return pltpu.make_async_copy(from_ref.at[rows, :], out_ref.at[rows, :], sems.at[tile])
 
 
-def near_kernel(
-    spot_ref, hop_ref, doc_ref, q_ref, near_ref, first_ref, acc_in, top_in, tot_in,
-    acc_ref, top_ref, tot_ref,
-):
-    source, state = (acc_in, top_in, tot_in), (acc_ref, top_ref, tot_ref)
-    offset = on_core(spot_ref, 1, 1)
-
+def one_block(spot_ref, hop_ref, doc_ref, q_ref, block_ref, first_ref, source, state, offset):
     def step(pair, carry):
         rows = pair_rows(pair)
         needed = reaches(spot_ref, hop_ref, doc_ref, pair * PAIR, offset)
 
         @pl.when(needed)
         def _():
-            attend_earlier(q_ref, near_ref, first_ref, same(rows), TILE, offset, source, state)
+            attend_earlier(q_ref, block_ref, first_ref, same(rows), TILE, offset, source, state)
 
         @pl.when(jnp.logical_not(needed))
         def _():
@@ -223,6 +215,15 @@
     lax.fori_loop(0, ROWS // PAIR, step, 0)
 
 
+def near_kernel(
+    spot_ref, hop_ref, doc_ref, q_ref, near_ref, first_ref, acc_in, top_in, tot_in,
+    acc_ref, top_ref, tot_ref,
+):
+    source, state = (acc_in, top_in, tot_in), (acc_ref, top_ref, tot_ref)
+    offset = on_core(spot_ref, 1, 1)
+    one_block(spot_ref, hop_ref, doc_ref, q_ref, near_ref, first_ref, source, state, offset)
+
+
 def on_core(spot_ref, core, distance):
     return jnp.where(spot_ref[1] == core, -distance * ROWS, NOWHERE)
 
@@ -232,85 +233,54 @@
 
 
 def far_kernel(
-    spot_ref, hop_ref, doc_ref, q_ref, far_ref, side_ref, first_ref, mark_ref,
-    acc_in, top_in, tot_in, acc_ref, top_ref, tot_ref, done_ref, squares_ref,
+    spot_ref, hop_ref, doc_ref, q_ref, far_ref, first_ref, marks_ref, acc_in, top_in, tot_in,
+    acc_ref, top_ref, tot_ref, mark_ref,
 ):
     source, state = (acc_in, top_in, tot_in), (acc_ref, top_ref, tot_ref)
-    far, side = -2 * ROWS, side_offset(spot_ref)
+    for tile in range(TILES):
+        marks = marks_ref[tile : tile + 1, :].astype(jnp.float32)
+        mark_ref[tile_rows(tile), :] = jnp.broadcast_to(marks, (TILE, 128)).T
+    one_block(spot_ref, hop_ref, doc_ref, q_ref, far_ref, first_ref, source, state, -2 * ROWS)
+
+
+def side_kernel(
+    spot_ref, hop_ref, doc_ref, q_ref, side_ref, first_ref, mark_ref, acc_in, top_in, tot_in,
+    acc_ref, top_ref, tot_ref, out_ref, squares_ref, done_ref, sems,
+):
+    source, state = (acc_in, top_in, tot_in), (acc_ref, top_ref, tot_ref)
+    offset = side_offset(spot_ref)
     squares_ref[...] = jnp.zeros_like(squares_ref)
 
-    def step(pair, carry):
+    def if_done(tile, act):
+        pl.when(jnp.logical_not(late_from(spot_ref, hop_ref, doc_ref, tile * TILE)))(act)
+
+    def moved(tile, act):
+        if_done(tile, getattr(out_copy(done_ref, out_ref, sems, tile), act))
+
+    per_pair = PAIR // TILE
+    for pair in range(ROWS // PAIR):
         rows = pair_rows(pair)
-        needed = reaches(spot_ref, hop_ref, doc_ref, pair * PAIR, far)
+        needed = reaches(spot_ref, hop_ref, doc_ref, pair * PAIR, offset)
 
         @pl.when(needed)
         def _():
-            attend_earlier(q_ref, far_ref, first_ref, same(rows), TILE, far, source, state)
+            attend_earlier(q_ref, side_ref, first_ref, same(rows), TILE, offset, source, state)
 
         @pl.when(jnp.logical_not(needed))
         def _():
             for part in rows:
                 copy_tile(source, state, part, part)
 
-        return carry
-
-    lax.fori_loop(0, ROWS // PAIR, step, 0)
-
-    @pl.when(reaches(spot_ref, hop_ref, doc_ref, 0, side))
-    def _():
-        attend_earlier(q_ref, side_ref, first_ref, same(pair_rows(0)), TILE, side, state, state)
-
-    for tile in range(PAIR // TILE):
-
-        @pl.when(jnp.logical_not(late_from(spot_ref, hop_ref, doc_ref, tile * TILE)))
-        def _():
-            rows = tile_rows(tile)
-            finish(state, rows, TILE, mark_ref, done_ref, squares_ref, rows)
-
-
-def side_kernel(
-    spot_ref, hop_ref, doc_ref, q_ref, side_ref, first_ref, mark_ref, acc_in, top_in, tot_in,
-    done_in, squares_in, acc_ref, top_ref, tot_ref, out_ref, squares_ref, done_ref, sems,
-):
-    source, state = (acc_in, top_in, tot_in), (acc_ref, top_ref, tot_ref)
-    side = side_offset(spot_ref)
-    early, after = range(PAIR // TILE), range(PAIR // TILE, TILES)
-    squares_ref[...] = squares_in[...]
-
-    def if_done(tile, act):
-        pl.when(jnp.logical_not(late_from(spot_ref, hop_ref, doc_ref, tile * TILE)))(act)
-
-    def moved(tile, act):
-        copy = out_copy(done_in if tile in early else done_ref, out_ref, sems, tile)
-        if_done(tile, getattr(copy, act))
-
-    for tile in early:
-        moved(tile, "start")
-
-        @pl.when(late_from(spot_ref, hop_ref, doc_ref, tile * TILE))
-        def _():
-            copy_tile(source, state, tile_rows(tile), tile_rows(tile))
-
-    rows = pair_rows(1)
-    needed = reaches(spot_ref, hop_ref, doc_ref, PAIR, side)
-
-    @pl.when(needed)
-    def _():
-        attend_earlier(q_ref, side_ref, first_ref, same(rows), TILE, side, source, state)
-
-    @pl.when(jnp.logical_not(needed))
-    def _():
-        for part in rows:
-            copy_tile(source, state, part, part)
-
-    for tile in after:
-
-        def act():
-            part = tile_rows(tile)
-            finish(state, part, TILE, mark_ref, done_ref, squares_ref, part)
-
-        if_done(tile, act)
-    for tile in after:
+        for i, part in enumerate(rows):
+
+            def act():
+                finish(state, part, TILE, mark_ref, done_ref, squares_ref, part)
+
+            if_done(pair * per_pair + i, act)
+        if pair:
+            for i in range(per_pair):
+                moved((pair - 1) * per_pair + i, "start")
+    for tile in range(TILES - per_pair, TILES):
         moved(tile, "start")
     for tile in range(TILES):
         moved(tile, "wait")
@@ -441,11 +411,11 @@
     side_1 = across(own, [(0, 1)])
     even_2 = onward(own, (0,))
     state_shapes = [f32(ROWS, HEADS * HEAD_WIDTH), f32(HEADS, ROWS, 128), f32(HEADS, ROWS, 128)]
-    *state, first, mark = call(
+    *state, first = call(
         first_kernel,
         scalars,
-        [doc_start.reshape(TILES, TILE), loss_mask.reshape(TILES, TILE), queries, own],
-        state_shapes + [f32(ROWS, 128)] * 2,
+        [doc_start.reshape(TILES, TILE), queries, own],
+        state_shapes + [f32(ROWS, 128)],
         2 * 10**9,
     )
     odd_4 = onward(odd_2, (1,))
@@ -455,18 +425,18 @@
     side_2 = across(far_2, [(0, 1), (1, 0)])
     out_shape = jax.ShapeDtypeStruct((ROWS, HEADS * HEAD_WIDTH), jnp.bfloat16)
     copy_scratch = [pltpu.VMEM(out_shape.shape, jnp.bfloat16), pltpu.SemaphoreType.DMA((TILES,))]
-    *state, done, squares = call(
+    *state, mark = call(
         far_kernel,
         scalars,
-        [queries, far_2, side_2, first, mark, *state],
-        state_shapes + [out_shape, f32(8, 128)],
-        2 * 10**9,
+        [queries, far_2, first, loss_mask.reshape(TILES, TILE), *state],
+        state_shapes + [f32(ROWS, 128)],
+        10**9,
     )
     side_3 = across(odd_4, [(1, 0)])
     *state, done, squares = call(
         side_kernel,
         scalars,
-        [queries, side_2, first, mark, *state, done, squares],
+        [queries, side_2, first, mark, *state],
         state_shapes + [out_shape, f32(8, 128)],
         10**9,
         scratch=copy_scratch,

time: 76.3 us -> 76.6 us (level)
  no operation moved by 1% of the time
where the time goes in v10:
time: 76.6 us; the launch traced here: 76.3 us
  blocking collectives  32.7 us (43%)
  starting transfers between devices  17 us (22%)
  Pallas kernels  11.8 us (15%)
  waiting for transfers between devices  9.15 us (12%)
  other arithmetic  3.2 us (4%)
  between operations  1.62 us (2%)
  local copies, waits for them, and re-layouts  0.8 us (1%)
    all_to_all x1, blocking collectives, on_device(): shares = lax.all_to_all(share, SEQ_HEAD, 0, 0, tiled=True)  32.7 us
    pallas_call x5, Pallas kernels, call(): pl.pallas_call(kernel, out_shape=out_shapes, in_specs=[smem] * len(scalar...  11.1 us
    ppermute x4, starting transfers between devices, onward(): lax.ppermute(shard, SEQ, [(i, i + 2) for i in blocks if i % 2 in cores])  10.5 us
    ppermute x4, waiting for transfers between devices, onward(): lax.ppermute(shard, SEQ, [(i, i + 2) for i in blocks if i % 2 in cores])  9.14 us
    ppermute x3, starting transfers between devices, across(): return lax.ppermute(shard, 'seq_2', pairs)  6.47 us
    add x1, other arithmetic, packed(): jnp.pad(keys[None], ((0, 1), *pads))  1.95 us
  transfers between devices with their start and end apart: 7, of which 2 were waited for; matrix products, arithmetic and copies ran while one was open for 2% of the time, Pallas kernels for 13%

profile of v10, /device:TPU:1, one launch (start us, length us, event | category | flops | bytes accessed | tf_op | source)
XLA Modules:
  0.0 76.3 jit_solution(2831799254761484597)
XLA Ops:
  0.7 1.9 %pad_add_fusion.own_ref = bf16[2,512,256]{2,1,0:T(8,128)(2,1)} fusion(bf16[1,512,256]{2,1,0:T(8,128)(2,1)} %bitcast.15, bf16[1,512,256]{2,1,0:T(8,128)(2,1)} %bitcast.16), kind=kLoop, calls=%fused_computation | loop fusion | flops 262144 | bytes 1048576 | tf_op jit(solution)/shard_map/add | solution.py:372
  2.6 5.2 %collective-permute-start = (bf16[2,512,256]{2,1,0:T(8,128)(2,1)}, bf16[2,512,256]{2,1,0:T(8,128)(2,1)}, u32[]{:S(2)}, u32[]{:S(2)}) collective-permute-start(bf16[2,512,256]{2,1,0:T(8,128)(2,1)} %pad_add_fusion.own_ref), channel_id=1, source_target_pairs={{4,12},{12,20},{20,28},{28,36},{36,44},{44,52},{52,60},{60,68},{68... | collective-permute-start | bytes 1572872 | tf_op jit(solution)/shard_map/ppermute | solution.py:395
  7.8 0.7 collective-permute-start.2
  8.4 8.0 %collective-permute-done = bf16[2,512,256]{2,1,0:T(8,128)(2,1)} collective-permute-done((bf16[2,512,256]{2,1,0:T(8,128)(2,1)}, bf16[2,512,256]{2,1,0:T(8,128)(2,1)}, u32[]{:S(2)}, u32[]{:S(2)}) %collective-permute-start) | collective-permute-done | bytes 524320 | tf_op jit(solution)/shard_map/ppermute | solution.py:395
  16.4 4.0 %collective-permute-start.1 = (bf16[2,512,256]{2,1,0:T(8,128)(2,1)}, bf16[2,512,256]{2,1,0:T(8,128)(2,1)S(1)}, u32[]{:S(2)}, u32[]{:S(2)}) collective-permute-start(bf16[2,512,256]{2,1,0:T(8,128)(2,1)} %collective-permute-done), channel_id=1, source_target_pairs={{4,12},{12,20},{20,28},{28,36},{36,44},{44,52},{52,60},{60,68},{68... | collective-permute-start | bytes 1572872 | tf_op jit(solution)/shard_map/ppermute | solution.py:395
  20.4 1.3 %collective-permute-start.5 = (bf16[2,512,256]{2,1,0:T(8,128)(2,1)}, bf16[2,512,256]{2,1,0:T(8,128)(2,1)S(1)}, u32[]{:S(2)}, u32[]{:S(2)}) collective-permute-start(bf16[2,512,256]{2,1,0:T(8,128)(2,1)} %pad_add_fusion.own_ref), channel_id=1, source_target_pairs={{0,4},{1,5},{2,6},{3,7},{8,12},{9,13},{10,14},{11,15},{16,20},{17,... | collective-permute-start | bytes 1572872 | tf_op jit(solution)/shard_map/ppermute | solution.py:399
  21.7 0.0 collective-permute-done.2
  21.7 0.8 %copy-done.3 = bf16[2,512,256]{2,1,0:T(8,128)(2,1)} copy-done((bf16[2,512,256]{2,1,0:T(8,128)(2,1)}, bf16[2,512,256]{2,1,0:T(8,128)(2,1)S(1)}, u32[]{:S(2)}) %copy-start.3) | copy-done | bytes 524312
  22.5 1.2 %add.19.far_ref = bf16[2,512,256]{2,1,0:T(8,128)(2,1)S(1)} add(bf16[2,512,256]{2,1,0:T(8,128)(2,1)} %collective-permute-done, bf16[2,512,256]{2,1,0:T(8,128)(2,1)S(1)} %collective-permute-done.2) | non-fusion elementwise | flops 262144 | bytes 1572864 | tf_op jit(solution)/shard_map/add | solution.py:424
  23.7 1.2 %collective-permute-start.6 = (bf16[2,512,256]{2,1,0:T(8,128)(2,1)S(1)}, bf16[2,512,256]{2,1,0:T(8,128)(2,1)S(1)}, u32[]{:S(2)}, u32[]{:S(2)}) collective-permute-start(bf16[2,512,256]{2,1,0:T(8,128)(2,1)S(1)} %add.19.far_ref), channel_id=1, source_target_pairs={{0,4},{4,0},{1,5},{5,1},{2,6},{6,2},{3,7},{7,3},{8,12},{12,8},{9,1... | collective-permute-start | bytes 1572872 | tf_op jit(solution)/shard_map/ppermute | solution.py:399
  25.0 0.7 collective-permute-start.3
  25.6 1.2 %collective-permute-done.1.odd_ref = bf16[2,512,256]{2,1,0:T(8,128)(2,1)S(1)} collective-permute-done((bf16[2,512,256]{2,1,0:T(8,128)(2,1)}, bf16[2,512,256]{2,1,0:T(8,128)(2,1)S(1)}, u32[]{:S(2)}, u32[]{:S(2)}) %collective-permute-start.1) | collective-permute-done | bytes 524320 | tf_op jit(solution)/shard_map/ppermute | solution.py:395
  26.8 3.9 %collective-permute-start.4 = (bf16[2,512,256]{2,1,0:T(8,128)(2,1)S(1)}, bf16[2,512,256]{2,1,0:T(8,128)(2,1)S(1)}, u32[]{:S(2)}, u32[]{:S(2)}) collective-permute-start(bf16[2,512,256]{2,1,0:T(8,128)(2,1)S(1)} %collective-permute-done.1.odd_ref), channel_id=1, source_target_pairs={{4,0},{5,1},{6,2},{7,3},{12,8},{13,9},{14,10},{15,11},{20,16},{21,... | collective-permute-start | bytes 1572872 | tf_op jit(solution)/shard_map/ppermute | solution.py:399
  30.8 0.1 pad_add_fusion.1.spot_ref
  31.5 3.4 %shard_map.77 = (f32[512,1024]{1,0:T(8,128)S(1)}, f32[8,512,128]{2,1,0:T(8,128)S(1)}, f32[8,512,128]{2,1,0:T(8,128)S(1)}, f32[512,128]{1,0:T(8,128)S(1)}) custom-call(s32[2]{0:T(128)S(1)} %pad_add_fusion.1.spot_ref, s32[1]{0:T(128)S(6)} %copy.11.hop_ref, s32[512]{0:T(512)S(1)} %copy-done.1, s32[4,128]{1,0:T(4,128)S(1)} %bitcast.13, ...), custom_call_target="tpu_custom_call" | custom-call | flops 2000000000 | bytes 1048576 | tf_op jit(solution)/shard_map/pallas_call | solution.py:358
  34.9 0.0 collective-permute-done.5.near_ref
  34.9 0.0 copy-start.2
  34.9 2.7 %shard_map.78 = (f32[512,1024]{1,0:T(8,128)S(1)}, f32[8,512,128]{2,1,0:T(8,128)S(1)}, f32[8,512,128]{2,1,0:T(8,128)S(1)}) custom-call(s32[2]{0:T(128)S(1)} %pad_add_fusion.1.spot_ref, s32[1]{0:T(128)S(6)} %copy.11.hop_ref, s32[512]{0:T(512)S(1)} %copy-done.1, bf16[512,1024]{1,0:T(8,128)(2,1)S(1)} %copy-done, ...), custom_call_target="tpu_custom_call" | custom-call | flops 1000000000 | bytes 1048576 | tf_op jit(solution)/shard_map/pallas_call | solution.py:358
  37.6 1.2 %shard_map.79 = (f32[512,1024]{1,0:T(8,128)S(1)}, f32[8,512,128]{2,1,0:T(8,128)S(1)}, f32[8,512,128]{2,1,0:T(8,128)S(1)}, f32[512,128]{1,0:T(8,128)S(1)}) custom-call(s32[2]{0:T(128)S(1)} %pad_add_fusion.1.spot_ref, s32[1]{0:T(128)S(6)} %copy.11.hop_ref, s32[512]{0:T(512)S(1)} %copy-done.1, bf16[512,1024]{1,0:T(8,128)(2,1)S(1)} %copy-done, ...), custom_call_target="tpu_custom_call" | custom-call | flops 1000000000 | bytes 1048576 | tf_op jit(solution)/shard_map/pallas_call | solution.py:358
  38.9 0.0 collective-permute-done.6.side_ref
  38.9 2.8 %shard_map.80 = (f32[512,1024]{1,0:T(8,128)S(1)}, f32[8,512,128]{2,1,0:T(8,128)S(1)}, f32[8,512,128]{2,1,0:T(8,128)S(1)}, bf16[512,1024]{1,0:T(8,128)(2,1)}, f32[8,128]{1,0:T(8,128)S(1)}) custom-call(s32[2]{0:T(128)S(1)} %pad_add_fusion.1.spot_ref, s32[1]{0:T(128)S(6)} %copy.11.hop_ref, s32[512]{0:T(512)S(1)} %copy-done.1, bf16[512,1024]{1,0:T(8,128)(2,1)S(1)} %copy-done, ...), custom_call_target="tpu_custom_call" | custom-call | flops 1000000000 | bytes 1048576 | tf_op jit(solution)/shard_map/pallas_call | solution.py:358
  41.8 0.9 %shard_map.81 = (bf16[512,1024]{1,0:T(8,128)(2,1)}, f32[256,128]{1,0:T(8,128)S(1)}) custom-call(s32[2]{0:T(128)S(1)} %pad_add_fusion.1.spot_ref, s32[1]{0:T(128)S(6)} %copy.11.hop_ref, s32[512]{0:T(512)S(1)} %copy-done.1, bf16[512,1024]{1,0:T(8,128)(2,1)S(1)} %copy-done, ...), custom_call_target="tpu_custom_call", output_to_operand_aliasing={{0}: (13, {})} | custom-call | flops 1000000000 | bytes 1048576 | tf_op jit(solution)/shard_map/pallas_call | solution.py:358
  42.7 32.7 %all_to_all.11 = f32[256,1,128]{2,1,0:T(1,128)S(1)} all-to-all(f32[256,1,128]{2,1,0:T(1,128)S(1)} %bitcast.12), channel_id=1, replica_groups=mesh['seq_0'=4,'seq_1'=8,'seq_2'=2,'head'=4] {'seq_0','seq_1','seq_2','h..., dimensions={0} | all-to-all | bytes 262144 | tf_op jit(solution)/shard_map/all_to_all | solution.py:464
  75.4 0.7 shard_map.82
  (8 shorter events, 0.0 us)
Async XLA Ops:
  0.6 30.9 %copy-start.1 = (s32[512]{0:T(512)S(1)}, s32[512]{0:T(512)}, u32[]{:S(2)}) copy-start(s32[512]{0:T(512)} %doc_ref.9) | copy-start | bytes 6148
  0.6 30.9 %copy-start = (bf16[512,1024]{1,0:T(8,128)(2,1)S(1)}, bf16[512,1024]{1,0:T(8,128)(2,1)}, u32[]{:S(2)}) copy-start(bf16[512,1024]{1,0:T(8,128)(2,1)} %q_ref.9) | copy-start | bytes 3145732
  2.6 13.8 %collective-permute-start = (bf16[2,512,256]{2,1,0:T(8,128)(2,1)}, bf16[2,512,256]{2,1,0:T(8,128)(2,1)}, u32[]{:S(2)}, u32[]{:S(2)}) collective-permute-start(bf16[2,512,256]{2,1,0:T(8,128)(2,1)} %pad_add_fusion.own_ref), channel_id=1, source_target_pairs={{4,12},{12,20},{20,28},{28,36},{36,44},{44,52},{52,60},{60,68},{68... | collective-permute-start | bytes 1572872 | tf_op jit(solution)/shard_map/ppermute | solution.py:395
  7.8 14.0 %collective-permute-start.2 = (bf16[2,512,256]{2,1,0:T(8,128)(2,1)}, bf16[2,512,256]{2,1,0:T(8,128)(2,1)S(1)}, u32[]{:S(2)}, u32[]{:S(2)}) collective-permute-start(bf16[2,512,256]{2,1,0:T(8,128)(2,1)} %pad_add_fusion.own_ref), channel_id=1, source_target_pairs={{0,8},{8,16},{16,24},{24,32},{32,40},{40,48},{48,56},{56,64},{64,7... | collective-permute-start | bytes 1572872 | tf_op jit(solution)/shard_map/ppermute | solution.py:395
  16.4 10.4 %collective-permute-start.1 = (bf16[2,512,256]{2,1,0:T(8,128)(2,1)}, bf16[2,512,256]{2,1,0:T(8,128)(2,1)S(1)}, u32[]{:S(2)}, u32[]{:S(2)}) collective-permute-start(bf16[2,512,256]{2,1,0:T(8,128)(2,1)} %collective-permute-done), channel_id=1, source_target_pairs={{4,12},{12,20},{20,28},{28,36},{36,44},{44,52},{52,60},{60,68},{68... | collective-permute-start | bytes 1572872 | tf_op jit(solution)/shard_map/ppermute | solution.py:395
  20.4 14.5 %collective-permute-start.5 = (bf16[2,512,256]{2,1,0:T(8,128)(2,1)}, bf16[2,512,256]{2,1,0:T(8,128)(2,1)S(1)}, u32[]{:S(2)}, u32[]{:S(2)}) collective-permute-start(bf16[2,512,256]{2,1,0:T(8,128)(2,1)} %pad_add_fusion.own_ref), channel_id=1, source_target_pairs={{0,4},{1,5},{2,6},{3,7},{8,12},{9,13},{10,14},{11,15},{16,20},{17,... | collective-permute-start | bytes 1572872 | tf_op jit(solution)/shard_map/ppermute | solution.py:399
  21.7 0.8 %copy-start.3 = (bf16[2,512,256]{2,1,0:T(8,128)(2,1)}, bf16[2,512,256]{2,1,0:T(8,128)(2,1)S(1)}, u32[]{:S(2)}) copy-start(bf16[2,512,256]{2,1,0:T(8,128)(2,1)S(1)} %collective-permute-done.2) | copy-start | bytes 1572868
  23.7 15.2 %collective-permute-start.6 = (bf16[2,512,256]{2,1,0:T(8,128)(2,1)S(1)}, bf16[2,512,256]{2,1,0:T(8,128)(2,1)S(1)}, u32[]{:S(2)}, u32[]{:S(2)}) collective-permute-start(bf16[2,512,256]{2,1,0:T(8,128)(2,1)S(1)} %add.19.far_ref), channel_id=1, source_target_pairs={{0,4},{4,0},{1,5},{5,1},{2,6},{6,2},{3,7},{7,3},{8,12},{12,8},{9,1... | collective-permute-start | bytes 1572872 | tf_op jit(solution)/shard_map/ppermute | solution.py:399
  25.0 16.8 %collective-permute-start.3 = (bf16[2,512,256]{2,1,0:T(8,128)(2,1)}, bf16[2,512,256]{2,1,0:T(8,128)(2,1)S(1)}, u32[]{:S(2)}, u32[]{:S(2)}) collective-permute-start(bf16[2,512,256]{2,1,0:T(8,128)(2,1)} %copy-done.3), channel_id=1, source_target_pairs={{0,8},{8,16},{16,24},{24,32},{32,40},{40,48},{48,56},{56,64},{64,7... | collective-permute-start | bytes 1572872 | tf_op jit(solution)/shard_map/ppermute | solution.py:395
  26.8 14.9 %collective-permute-start.4 = (bf16[2,512,256]{2,1,0:T(8,128)(2,1)S(1)}, bf16[2,512,256]{2,1,0:T(8,128)(2,1)S(1)}, u32[]{:S(2)}, u32[]{:S(2)}) collective-permute-start(bf16[2,512,256]{2,1,0:T(8,128)(2,1)S(1)} %collective-permute-done.1.odd_ref), channel_id=1, source_target_pairs={{4,0},{5,1},{6,2},{7,3},{12,8},{13,9},{14,10},{15,11},{20,16},{21,... | collective-permute-start | bytes 1572872 | tf_op jit(solution)/shard_map/ppermute | solution.py:399
  34.9 2.7 %copy-start.2 = (s32[512]{0:T(512)S(1)}, s32[512]{0:T(512)}, u32[]{:S(2)}) copy-start(s32[512]{0:T(512)} %param.11) | copy-start | bytes 6148

commit v11 on v10

--- a/solution.py
+++ b/solution.py
@@ -280,9 +280,7 @@
         if pair:
             for i in range(per_pair):
                 moved((pair - 1) * per_pair + i, "start")
-    for tile in range(TILES - per_pair, TILES):
-        moved(tile, "start")
-    for tile in range(TILES):
+    for tile in range(per_pair):
         moved(tile, "wait")
 
 
@@ -293,8 +291,8 @@
 
 def last_kernel(
     spot_ref, hop_ref, doc_ref, q_ref, odd_ref, even_ref, side_ref, first_ref, mark_ref, acc_in,
-    top_in, tot_in, squares_in, out_in, out_ref, share_ref, acc_ref, top_ref, tot_ref, squares_ref,
-    done_ref, sems,
+    top_in, tot_in, squares_in, done_in, out_in, out_ref, share_ref, acc_ref, top_ref, tot_ref,
+    squares_ref, done_ref, sems,
 ):
     source, state = (acc_in, top_in, tot_in), (acc_ref, top_ref, tot_ref)
     slots = (
@@ -303,6 +301,13 @@
         (even_ref, on_core(spot_ref, 0, 4)),
     )
     late = functools.partial(late_from, spot_ref, hop_ref, doc_ref)
+
+    def moved(tile, act):
+        copy = out_copy(done_in, out_ref, sems, tile)
+        pl.when(jnp.logical_not(late(tile * TILE)))(getattr(copy, act))
+
+    for tile in range(PAIR // TILE, TILES):
+        moved(tile, "start")
     squares_ref[...] = squares_in[...]
 
     def absorb(places, size, row):
@@ -347,6 +352,8 @@
             def _():
                 copy = out_copy(done_ref, out_ref, sems, tile)
                 copy.wait() if ended else copy.start()
+    for tile in range(PAIR // TILE, TILES):
+        moved(tile, "wait")
 
 
 def call(
@@ -433,17 +440,17 @@
         10**9,
     )
     side_3 = across(odd_4, [(1, 0)])
-    *state, done, squares = call(
+    *state, out, squares, done = call(
         side_kernel,
         scalars,
         [queries, side_2, first, mark, *state],
-        state_shapes + [out_shape, f32(8, 128)],
-        10**9,
-        scratch=copy_scratch,
+        state_shapes + [out_shape, f32(8, 128), out_shape],
+        2 * 10**9,
+        scratch=[pltpu.SemaphoreType.DMA((TILES,))],
         out_hbm=3,
     )
     devices = lax.axis_size(SEQ_HEAD)
-    arrays = [queries, odd_4, even_4, side_3, first, mark, *state, squares, done]
+    arrays = [queries, odd_4, even_4, side_3, first, mark, *state, squares, done, out]
     attention, share = call(
         last_kernel,
         scalars,

time: 76.6 us -> 76.9 us (level)
  no operation moved by 1% of the time
where the time goes in v11:
time: 76.9 us; the launch traced here: 76.5 us
  blocking collectives  32.6 us (42%)
  starting transfers between devices  17.7 us (23%)
  Pallas kernels  12.1 us (16%)
  waiting for transfers between devices  8.43 us (11%)
  other arithmetic  3.2 us (4%)
  between operations  1.62 us (2%)
  local copies, waits for them, and re-layouts  0.81 us (1%)
    all_to_all x1, blocking collectives, on_device(): shares = lax.all_to_all(share, SEQ_HEAD, 0, 0, tiled=True)  32.6 us
    pallas_call x5, Pallas kernels, call(): pl.pallas_call(kernel, out_shape=out_shapes, in_specs=[smem] * len(scalar...  11.4 us
    ppermute x4, starting transfers between devices, onward(): lax.ppermute(shard, SEQ, [(i, i + 2) for i in blocks if i % 2 in cores])  10.5 us
    ppermute x4, waiting for transfers between devices, onward(): lax.ppermute(shard, SEQ, [(i, i + 2) for i in blocks if i % 2 in cores])  8.42 us
    ppermute x3, starting transfers between devices, across(): return lax.ppermute(shard, 'seq_2', pairs)  7.19 us
    add x1, other arithmetic, packed(): jnp.pad(keys[None], ((0, 1), *pads))  1.95 us
  transfers between devices with their start and end apart: 7, of which 2 were waited for; matrix products, arithmetic and copies ran while one was open for 2% of the time, Pallas kernels for 13%

profile of v11, /device:TPU:1, one launch (start us, length us, event | category | flops | bytes accessed | tf_op | source)
XLA Modules:
  0.0 76.5 jit_solution(1392135291773755204)
XLA Ops:
  0.7 1.9 %pad_add_fusion.own_ref = bf16[2,512,256]{2,1,0:T(8,128)(2,1)} fusion(bf16[1,512,256]{2,1,0:T(8,128)(2,1)} %bitcast.15, bf16[1,512,256]{2,1,0:T(8,128)(2,1)} %bitcast.16), kind=kLoop, calls=%fused_computation | loop fusion | flops 262144 | bytes 1048576 | tf_op jit(solution)/shard_map/add | solution.py:379
  2.6 5.1 %collective-permute-start = (bf16[2,512,256]{2,1,0:T(8,128)(2,1)}, bf16[2,512,256]{2,1,0:T(8,128)(2,1)}, u32[]{:S(2)}, u32[]{:S(2)}) collective-permute-start(bf16[2,512,256]{2,1,0:T(8,128)(2,1)} %pad_add_fusion.own_ref), channel_id=1, source_target_pairs={{4,12},{12,20},{20,28},{28,36},{36,44},{44,52},{52,60},{60,68},{68... | collective-permute-start | bytes 1572872 | tf_op jit(solution)/shard_map/ppermute | solution.py:402
  7.7 0.7 collective-permute-start.2
  8.4 8.0 %collective-permute-done = bf16[2,512,256]{2,1,0:T(8,128)(2,1)} collective-permute-done((bf16[2,512,256]{2,1,0:T(8,128)(2,1)}, bf16[2,512,256]{2,1,0:T(8,128)(2,1)}, u32[]{:S(2)}, u32[]{:S(2)}) %collective-permute-start) | collective-permute-done | bytes 524320 | tf_op jit(solution)/shard_map/ppermute | solution.py:402
  16.4 4.0 %collective-permute-start.1 = (bf16[2,512,256]{2,1,0:T(8,128)(2,1)}, bf16[2,512,256]{2,1,0:T(8,128)(2,1)S(1)}, u32[]{:S(2)}, u32[]{:S(2)}) collective-permute-start(bf16[2,512,256]{2,1,0:T(8,128)(2,1)} %collective-permute-done), channel_id=1, source_target_pairs={{4,12},{12,20},{20,28},{28,36},{36,44},{44,52},{52,60},{60,68},{68... | collective-permute-start | bytes 1572872 | tf_op jit(solution)/shard_map/ppermute | solution.py:402
  20.4 1.3 %collective-permute-start.5 = (bf16[2,512,256]{2,1,0:T(8,128)(2,1)}, bf16[2,512,256]{2,1,0:T(8,128)(2,1)S(1)}, u32[]{:S(2)}, u32[]{:S(2)}) collective-permute-start(bf16[2,512,256]{2,1,0:T(8,128)(2,1)} %pad_add_fusion.own_ref), channel_id=1, source_target_pairs={{0,4},{1,5},{2,6},{3,7},{8,12},{9,13},{10,14},{11,15},{16,20},{17,... | collective-permute-start | bytes 1572872 | tf_op jit(solution)/shard_map/ppermute | solution.py:406
  21.7 0.0 collective-permute-done.2
  21.8 0.8 %copy-done.3 = bf16[2,512,256]{2,1,0:T(8,128)(2,1)} copy-done((bf16[2,512,256]{2,1,0:T(8,128)(2,1)}, bf16[2,512,256]{2,1,0:T(8,128)(2,1)S(1)}, u32[]{:S(2)}) %copy-start.3) | copy-done | bytes 524312
  22.5 1.2 %add.19.far_ref = bf16[2,512,256]{2,1,0:T(8,128)(2,1)S(1)} add(bf16[2,512,256]{2,1,0:T(8,128)(2,1)} %collective-permute-done, bf16[2,512,256]{2,1,0:T(8,128)(2,1)S(1)} %collective-permute-done.2) | non-fusion elementwise | flops 262144 | bytes 1572864 | tf_op jit(solution)/shard_map/add | solution.py:431
  23.7 1.2 %collective-permute-start.6 = (bf16[2,512,256]{2,1,0:T(8,128)(2,1)S(1)}, bf16[2,512,256]{2,1,0:T(8,128)(2,1)S(1)}, u32[]{:S(2)}, u32[]{:S(2)}) collective-permute-start(bf16[2,512,256]{2,1,0:T(8,128)(2,1)S(1)} %add.19.far_ref), channel_id=1, source_target_pairs={{0,4},{4,0},{1,5},{5,1},{2,6},{6,2},{3,7},{7,3},{8,12},{12,8},{9,1... | collective-permute-start | bytes 1572872 | tf_op jit(solution)/shard_map/ppermute | solution.py:406
  25.6 0.1 pad_add_fusion.1.spot_ref
  25.7 0.7 collective-permute-start.3
  26.4 0.4 collective-permute-done.1.odd_ref
  26.8 4.7 %collective-permute-start.4 = (bf16[2,512,256]{2,1,0:T(8,128)(2,1)S(1)}, bf16[2,512,256]{2,1,0:T(8,128)(2,1)S(1)}, u32[]{:S(2)}, u32[]{:S(2)}) collective-permute-start(bf16[2,512,256]{2,1,0:T(8,128)(2,1)S(1)} %collective-permute-done.1.odd_ref), channel_id=1, source_target_pairs={{4,0},{5,1},{6,2},{7,3},{12,8},{13,9},{14,10},{15,11},{20,16},{21,... | collective-permute-start | bytes 1572872 | tf_op jit(solution)/shard_map/ppermute | solution.py:406
  31.5 3.4 %shard_map.77 = (f32[512,1024]{1,0:T(8,128)S(1)}, f32[8,512,128]{2,1,0:T(8,128)S(1)}, f32[8,512,128]{2,1,0:T(8,128)S(1)}, f32[512,128]{1,0:T(8,128)S(1)}) custom-call(s32[2]{0:T(128)S(1)} %pad_add_fusion.1.spot_ref, s32[1]{0:T(128)S(6)} %copy.11.hop_ref, s32[512]{0:T(512)S(1)} %copy-done.1, s32[4,128]{1,0:T(4,128)S(1)} %bitcast.13, ...), custom_call_target="tpu_custom_call" | custom-call | flops 2000000000 | bytes 1048576 | tf_op jit(solution)/shard_map/pallas_call | solution.py:365
  34.9 0.0 collective-permute-done.5.near_ref
  34.9 0.0 copy-start.2
  34.9 2.7 %shard_map.78 = (f32[512,1024]{1,0:T(8,128)S(1)}, f32[8,512,128]{2,1,0:T(8,128)S(1)}, f32[8,512,128]{2,1,0:T(8,128)S(1)}) custom-call(s32[2]{0:T(128)S(1)} %pad_add_fusion.1.spot_ref, s32[1]{0:T(128)S(6)} %copy.11.hop_ref, s32[512]{0:T(512)S(1)} %copy-done.1, bf16[512,1024]{1,0:T(8,128)(2,1)S(1)} %copy-done, ...), custom_call_target="tpu_custom_call" | custom-call | flops 1000000000 | bytes 1048576 | tf_op jit(solution)/shard_map/pallas_call | solution.py:365
  37.6 1.2 %shard_map.79 = (f32[512,1024]{1,0:T(8,128)S(1)}, f32[8,512,128]{2,1,0:T(8,128)S(1)}, f32[8,512,128]{2,1,0:T(8,128)S(1)}, f32[512,128]{1,0:T(8,128)S(1)}) custom-call(s32[2]{0:T(128)S(1)} %pad_add_fusion.1.spot_ref, s32[1]{0:T(128)S(6)} %copy.11.hop_ref, s32[512]{0:T(512)S(1)} %copy-done.1, bf16[512,1024]{1,0:T(8,128)(2,1)S(1)} %copy-done, ...), custom_call_target="tpu_custom_call" | custom-call | flops 1000000000 | bytes 1048576 | tf_op jit(solution)/shard_map/pallas_call | solution.py:365
  38.9 2.7 %shard_map.80 = (f32[512,1024]{1,0:T(8,128)S(1)}, f32[8,512,128]{2,1,0:T(8,128)S(1)}, f32[8,512,128]{2,1,0:T(8,128)S(1)}, bf16[512,1024]{1,0:T(8,128)(2,1)}, f32...) custom-call(s32[2]{0:T(128)S(1)} %pad_add_fusion.1.spot_ref, s32[1]{0:T(128)S(6)} %copy.11.hop_ref, s32[512]{0:T(512)S(1)} %copy-done.1, ...), custom_call_target="tpu_custom_call" | custom-call | flops 2000000000 | bytes 1048576 | tf_op jit(solution)/shard_map/pallas_call | solution.py:365
  41.6 0.0 collective-permute-done.4.side_ref
  41.6 1.4 %shard_map.81 = (bf16[512,1024]{1,0:T(8,128)(2,1)}, f32[256,128]{1,0:T(8,128)S(1)}) custom-call(s32[2]{0:T(128)S(1)} %pad_add_fusion.1.spot_ref, s32[1]{0:T(128)S(6)} %copy.11.hop_ref, s32[512]{0:T(512)S(1)} %copy-done.1, bf16[512,1024]{1,0:T(8,128)(2,1)S(1)} %copy-done, ...), custom_call_target="tpu_custom_call", output_to_operand_aliasing={{0}: (14, {})} | custom-call | flops 1000000000 | bytes 1048576 | tf_op jit(solution)/shard_map/pallas_call | solution.py:365
  43.0 32.6 %all_to_all.11 = f32[256,1,128]{2,1,0:T(1,128)S(1)} all-to-all(f32[256,1,128]{2,1,0:T(1,128)S(1)} %bitcast.12), channel_id=1, replica_groups=mesh['seq_0'=4,'seq_1'=8,'seq_2'=2,'head'=4] {'seq_0','seq_1','seq_2','h..., dimensions={0} | all-to-all | bytes 262144 | tf_op jit(solution)/shard_map/all_to_all | solution.py:471
  75.7 0.7 shard_map.82
  (8 shorter events, 0.0 us)
Async XLA Ops:
  0.6 30.9 %copy-start.1 = (s32[512]{0:T(512)S(1)}, s32[512]{0:T(512)}, u32[]{:S(2)}) copy-start(s32[512]{0:T(512)} %doc_ref.9) | copy-start | bytes 6148
  0.6 30.9 %copy-start = (bf16[512,1024]{1,0:T(8,128)(2,1)S(1)}, bf16[512,1024]{1,0:T(8,128)(2,1)}, u32[]{:S(2)}) copy-start(bf16[512,1024]{1,0:T(8,128)(2,1)} %q_ref.9) | copy-start | bytes 3145732
  2.6 13.8 %collective-permute-start = (bf16[2,512,256]{2,1,0:T(8,128)(2,1)}, bf16[2,512,256]{2,1,0:T(8,128)(2,1)}, u32[]{:S(2)}, u32[]{:S(2)}) collective-permute-start(bf16[2,512,256]{2,1,0:T(8,128)(2,1)} %pad_add_fusion.own_ref), channel_id=1, source_target_pairs={{4,12},{12,20},{20,28},{28,36},{36,44},{44,52},{52,60},{60,68},{68... | collective-permute-start | bytes 1572872 | tf_op jit(solution)/shard_map/ppermute | solution.py:402
  7.7 14.0 %collective-permute-start.2 = (bf16[2,512,256]{2,1,0:T(8,128)(2,1)}, bf16[2,512,256]{2,1,0:T(8,128)(2,1)S(1)}, u32[]{:S(2)}, u32[]{:S(2)}) collective-permute-start(bf16[2,512,256]{2,1,0:T(8,128)(2,1)} %pad_add_fusion.own_ref), channel_id=1, source_target_pairs={{0,8},{8,16},{16,24},{24,32},{32,40},{40,48},{48,56},{56,64},{64,7... | collective-permute-start | bytes 1572872 | tf_op jit(solution)/shard_map/ppermute | solution.py:402
  16.4 10.4 %collective-permute-start.1 = (bf16[2,512,256]{2,1,0:T(8,128)(2,1)}, bf16[2,512,256]{2,1,0:T(8,128)(2,1)S(1)}, u32[]{:S(2)}, u32[]{:S(2)}) collective-permute-start(bf16[2,512,256]{2,1,0:T(8,128)(2,1)} %collective-permute-done), channel_id=1, source_target_pairs={{4,12},{12,20},{20,28},{28,36},{36,44},{44,52},{52,60},{60,68},{68... | collective-permute-start | bytes 1572872 | tf_op jit(solution)/shard_map/ppermute | solution.py:402
  20.4 14.5 %collective-permute-start.5 = (bf16[2,512,256]{2,1,0:T(8,128)(2,1)}, bf16[2,512,256]{2,1,0:T(8,128)(2,1)S(1)}, u32[]{:S(2)}, u32[]{:S(2)}) collective-permute-start(bf16[2,512,256]{2,1,0:T(8,128)(2,1)} %pad_add_fusion.own_ref), channel_id=1, source_target_pairs={{0,4},{1,5},{2,6},{3,7},{8,12},{9,13},{10,14},{11,15},{16,20},{17,... | collective-permute-start | bytes 1572872 | tf_op jit(solution)/shard_map/ppermute | solution.py:406
  21.8 0.8 %copy-start.3 = (bf16[2,512,256]{2,1,0:T(8,128)(2,1)}, bf16[2,512,256]{2,1,0:T(8,128)(2,1)S(1)}, u32[]{:S(2)}) copy-start(bf16[2,512,256]{2,1,0:T(8,128)(2,1)S(1)} %collective-permute-done.2) | copy-start | bytes 1572868
  23.7 15.2 %collective-permute-start.6 = (bf16[2,512,256]{2,1,0:T(8,128)(2,1)S(1)}, bf16[2,512,256]{2,1,0:T(8,128)(2,1)S(1)}, u32[]{:S(2)}, u32[]{:S(2)}) collective-permute-start(bf16[2,512,256]{2,1,0:T(8,128)(2,1)S(1)} %add.19.far_ref), channel_id=1, source_target_pairs={{0,4},{4,0},{1,5},{5,1},{2,6},{6,2},{3,7},{7,3},{8,12},{12,8},{9,1... | collective-permute-start | bytes 1572872 | tf_op jit(solution)/shard_map/ppermute | solution.py:406
  25.7 15.9 %collective-permute-start.3 = (bf16[2,512,256]{2,1,0:T(8,128)(2,1)}, bf16[2,512,256]{2,1,0:T(8,128)(2,1)S(1)}, u32[]{:S(2)}, u32[]{:S(2)}) collective-permute-start(bf16[2,512,256]{2,1,0:T(8,128)(2,1)} %copy-done.3), channel_id=1, source_target_pairs={{0,8},{8,16},{16,24},{24,32},{32,40},{40,48},{48,56},{56,64},{64,7... | collective-permute-start | bytes 1572872 | tf_op jit(solution)/shard_map/ppermute | solution.py:402
  26.8 14.8 %collective-permute-start.4 = (bf16[2,512,256]{2,1,0:T(8,128)(2,1)S(1)}, bf16[2,512,256]{2,1,0:T(8,128)(2,1)S(1)}, u32[]{:S(2)}, u32[]{:S(2)}) collective-permute-start(bf16[2,512,256]{2,1,0:T(8,128)(2,1)S(1)} %collective-permute-done.1.odd_ref), channel_id=1, source_target_pairs={{4,0},{5,1},{6,2},{7,3},{12,8},{13,9},{14,10},{15,11},{20,16},{21,... | collective-permute-start | bytes 1572872 | tf_op jit(solution)/shard_map/ppermute | solution.py:406
  34.9 2.7 %copy-start.2 = (s32[512]{0:T(512)S(1)}, s32[512]{0:T(512)}, u32[]{:S(2)}) copy-start(s32[512]{0:T(512)} %param.11) | copy-start | bytes 6148

commit v12 on v10

--- a/solution.py
+++ b/solution.py
@@ -197,22 +197,17 @@
 
 
 def one_block(spot_ref, hop_ref, doc_ref, q_ref, block_ref, first_ref, source, state, offset):
-    def step(pair, carry):
-        rows = pair_rows(pair)
-        needed = reaches(spot_ref, hop_ref, doc_ref, pair * PAIR, offset)
-
-        @pl.when(needed)
-        def _():
-            attend_earlier(q_ref, block_ref, first_ref, same(rows), TILE, offset, source, state)
-
-        @pl.when(jnp.logical_not(needed))
-        def _():
-            for part in rows:
-                copy_tile(source, state, part, part)
-
-        return carry
-
-    lax.fori_loop(0, ROWS // PAIR, step, 0)
+    rows = [tile_rows(tile) for tile in range(TILES)]
+    needed = reaches(spot_ref, hop_ref, doc_ref, 0, offset)
+
+    @pl.when(needed)
+    def _():
+        attend_earlier(q_ref, block_ref, first_ref, same(rows), TILE, offset, source, state)
+
+    @pl.when(jnp.logical_not(needed))
+    def _():
+        for part in rows:
+            copy_tile(source, state, part, part)
 
 
 def near_kernel(

time: 76.6 us -> 76.3 us (level)
  blocking collectives: 32.7 us -> 30.9 us
  Pallas kernels: 11.8 us -> 13.3 us
    all_to_all x1, blocking collectives: 32.7 us -> 30.9 us  [on_device(): shares = lax.all_to_all(share, SEQ_HEAD, 0, 0, tiled=True)]
    pallas_call x5, Pallas kernels: 11.1 us -> 12.6 us  [call(): pl.pallas_call(kernel, out_shape=out_shapes, in_specs=[smem] * len(scalar...]
  transfers between devices with their start and end apart: 7 -> 7, of which waited for: 2 -> 2; matrix products, arithmetic and copies ran while one was open for 2% -> 2% of each run, Pallas kernels for 13% -> 15%
where the time goes in v12:
time: 76.3 us; the launch traced here: 76 us
  blocking collectives  30.9 us (40%)
  starting transfers between devices  17 us (22%)
  Pallas kernels  13.3 us (17%)
  waiting for transfers between devices  9.15 us (12%)
  other arithmetic  3.2 us (4%)
  between operations  1.62 us (2%)
  local copies, waits for them, and re-layouts  0.8 us (1%)
    all_to_all x1, blocking collectives, on_device(): shares = lax.all_to_all(share, SEQ_HEAD, 0, 0, tiled=True)  30.9 us
    pallas_call x5, Pallas kernels, call(): pl.pallas_call(kernel, out_shape=out_shapes, in_specs=[smem] * len(scalar...  12.6 us
    ppermute x4, starting transfers between devices, onward(): lax.ppermute(shard, SEQ, [(i, i + 2) for i in blocks if i % 2 in cores])  10.5 us
    ppermute x4, waiting for transfers between devices, onward(): lax.ppermute(shard, SEQ, [(i, i + 2) for i in blocks if i % 2 in cores])  9.14 us
    ppermute x3, starting transfers between devices, across(): return lax.ppermute(shard, 'seq_2', pairs)  6.47 us
    add x1, other arithmetic, packed(): jnp.pad(keys[None], ((0, 1), *pads))  1.95 us
  transfers between devices with their start and end apart: 7, of which 2 were waited for; matrix products, arithmetic and copies ran while one was open for 2% of the time, Pallas kernels for 15%

profile of v12, /device:TPU:1, one launch (start us, length us, event | category | flops | bytes accessed | tf_op | source)
XLA Modules:
  0.0 76.0 jit_solution(8770755783765866225)
XLA Ops:
  0.7 1.9 %pad_add_fusion.own_ref = bf16[2,512,256]{2,1,0:T(8,128)(2,1)} fusion(bf16[1,512,256]{2,1,0:T(8,128)(2,1)} %bitcast.15, bf16[1,512,256]{2,1,0:T(8,128)(2,1)} %bitcast.16), kind=kLoop, calls=%fused_computation | loop fusion | flops 262144 | bytes 1048576 | tf_op jit(solution)/shard_map/add | solution.py:367
  2.6 5.2 %collective-permute-start = (bf16[2,512,256]{2,1,0:T(8,128)(2,1)}, bf16[2,512,256]{2,1,0:T(8,128)(2,1)}, u32[]{:S(2)}, u32[]{:S(2)}) collective-permute-start(bf16[2,512,256]{2,1,0:T(8,128)(2,1)} %pad_add_fusion.own_ref), channel_id=1, source_target_pairs={{4,12},{12,20},{20,28},{28,36},{36,44},{44,52},{52,60},{60,68},{68... | collective-permute-start | bytes 1572872 | tf_op jit(solution)/shard_map/ppermute | solution.py:390
  7.8 0.7 collective-permute-start.2
  8.4 8.0 %collective-permute-done = bf16[2,512,256]{2,1,0:T(8,128)(2,1)} collective-permute-done((bf16[2,512,256]{2,1,0:T(8,128)(2,1)}, bf16[2,512,256]{2,1,0:T(8,128)(2,1)}, u32[]{:S(2)}, u32[]{:S(2)}) %collective-permute-start) | collective-permute-done | bytes 524320 | tf_op jit(solution)/shard_map/ppermute | solution.py:390
  16.4 4.0 %collective-permute-start.1 = (bf16[2,512,256]{2,1,0:T(8,128)(2,1)}, bf16[2,512,256]{2,1,0:T(8,128)(2,1)S(1)}, u32[]{:S(2)}, u32[]{:S(2)}) collective-permute-start(bf16[2,512,256]{2,1,0:T(8,128)(2,1)} %collective-permute-done), channel_id=1, source_target_pairs={{4,12},{12,20},{20,28},{28,36},{36,44},{44,52},{52,60},{60,68},{68... | collective-permute-start | bytes 1572872 | tf_op jit(solution)/shard_map/ppermute | solution.py:390
  20.4 1.3 %collective-permute-start.5 = (bf16[2,512,256]{2,1,0:T(8,128)(2,1)}, bf16[2,512,256]{2,1,0:T(8,128)(2,1)S(1)}, u32[]{:S(2)}, u32[]{:S(2)}) collective-permute-start(bf16[2,512,256]{2,1,0:T(8,128)(2,1)} %pad_add_fusion.own_ref), channel_id=1, source_target_pairs={{0,4},{1,5},{2,6},{3,7},{8,12},{9,13},{10,14},{11,15},{16,20},{17,... | collective-permute-start | bytes 1572872 | tf_op jit(solution)/shard_map/ppermute | solution.py:394
  21.7 0.0 collective-permute-done.2
  21.7 0.8 %copy-done.3 = bf16[2,512,256]{2,1,0:T(8,128)(2,1)} copy-done((bf16[2,512,256]{2,1,0:T(8,128)(2,1)}, bf16[2,512,256]{2,1,0:T(8,128)(2,1)S(1)}, u32[]{:S(2)}) %copy-start.3) | copy-done | bytes 524312
  22.5 1.2 %add.19.far_ref = bf16[2,512,256]{2,1,0:T(8,128)(2,1)S(1)} add(bf16[2,512,256]{2,1,0:T(8,128)(2,1)} %collective-permute-done, bf16[2,512,256]{2,1,0:T(8,128)(2,1)S(1)} %collective-permute-done.2) | non-fusion elementwise | flops 262144 | bytes 1572864 | tf_op jit(solution)/shard_map/add | solution.py:419
  23.7 1.2 %collective-permute-start.6 = (bf16[2,512,256]{2,1,0:T(8,128)(2,1)S(1)}, bf16[2,512,256]{2,1,0:T(8,128)(2,1)S(1)}, u32[]{:S(2)}, u32[]{:S(2)}) collective-permute-start(bf16[2,512,256]{2,1,0:T(8,128)(2,1)S(1)} %add.19.far_ref), channel_id=1, source_target_pairs={{0,4},{4,0},{1,5},{5,1},{2,6},{6,2},{3,7},{7,3},{8,12},{12,8},{9,1... | collective-permute-start | bytes 1572872 | tf_op jit(solution)/shard_map/ppermute | solution.py:394
  25.0 0.7 collective-permute-start.3
  25.6 1.2 %collective-permute-done.1.odd_ref = bf16[2,512,256]{2,1,0:T(8,128)(2,1)S(1)} collective-permute-done((bf16[2,512,256]{2,1,0:T(8,128)(2,1)}, bf16[2,512,256]{2,1,0:T(8,128)(2,1)S(1)}, u32[]{:S(2)}, u32[]{:S(2)}) %collective-permute-start.1) | collective-permute-done | bytes 524320 | tf_op jit(solution)/shard_map/ppermute | solution.py:390
  26.8 3.9 %collective-permute-start.4 = (bf16[2,512,256]{2,1,0:T(8,128)(2,1)S(1)}, bf16[2,512,256]{2,1,0:T(8,128)(2,1)S(1)}, u32[]{:S(2)}, u32[]{:S(2)}) collective-permute-start(bf16[2,512,256]{2,1,0:T(8,128)(2,1)S(1)} %collective-permute-done.1.odd_ref), channel_id=1, source_target_pairs={{4,0},{5,1},{6,2},{7,3},{12,8},{13,9},{14,10},{15,11},{20,16},{21,... | collective-permute-start | bytes 1572872 | tf_op jit(solution)/shard_map/ppermute | solution.py:394
  30.8 0.1 pad_add_fusion.1.spot_ref
  31.5 3.4 %shard_map.77 = (f32[512,1024]{1,0:T(8,128)S(1)}, f32[8,512,128]{2,1,0:T(8,128)S(1)}, f32[8,512,128]{2,1,0:T(8,128)S(1)}, f32[512,128]{1,0:T(8,128)S(1)}) custom-call(s32[2]{0:T(128)S(1)} %pad_add_fusion.1.spot_ref, s32[1]{0:T(128)S(6)} %copy.11.hop_ref, s32[512]{0:T(512)S(1)} %copy-done.1, s32[4,128]{1,0:T(4,128)S(1)} %bitcast.13, ...), custom_call_target="tpu_custom_call" | custom-call | flops 2000000000 | bytes 1048576 | tf_op jit(solution)/shard_map/pallas_call | solution.py:353
  34.9 0.0 collective-permute-done.5.near_ref
  34.9 0.0 copy-start.2
  34.9 4.2 %shard_map.78 = (f32[512,1024]{1,0:T(8,128)S(1)}, f32[8,512,128]{2,1,0:T(8,128)S(1)}, f32[8,512,128]{2,1,0:T(8,128)S(1)}) custom-call(s32[2]{0:T(128)S(1)} %pad_add_fusion.1.spot_ref, s32[1]{0:T(128)S(6)} %copy.11.hop_ref, s32[512]{0:T(512)S(1)} %copy-done.1, bf16[512,1024]{1,0:T(8,128)(2,1)S(1)} %copy-done, ...), custom_call_target="tpu_custom_call" | custom-call | flops 1000000000 | bytes 1048576 | tf_op jit(solution)/shard_map/pallas_call | solution.py:353
  39.1 1.3 %shard_map.79 = (f32[512,1024]{1,0:T(8,128)S(1)}, f32[8,512,128]{2,1,0:T(8,128)S(1)}, f32[8,512,128]{2,1,0:T(8,128)S(1)}, f32[512,128]{1,0:T(8,128)S(1)}) custom-call(s32[2]{0:T(128)S(1)} %pad_add_fusion.1.spot_ref, s32[1]{0:T(128)S(6)} %copy.11.hop_ref, s32[512]{0:T(512)S(1)} %copy-done.1, bf16[512,1024]{1,0:T(8,128)(2,1)S(1)} %copy-done, ...), custom_call_target="tpu_custom_call" | custom-call | flops 1000000000 | bytes 1048576 | tf_op jit(solution)/shard_map/pallas_call | solution.py:353
  40.4 2.8 %shard_map.80 = (f32[512,1024]{1,0:T(8,128)S(1)}, f32[8,512,128]{2,1,0:T(8,128)S(1)}, f32[8,512,128]{2,1,0:T(8,128)S(1)}, bf16[512,1024]{1,0:T(8,128)(2,1)}, f32[8,128]{1,0:T(8,128)S(1)}) custom-call(s32[2]{0:T(128)S(1)} %pad_add_fusion.1.spot_ref, s32[1]{0:T(128)S(6)} %copy.11.hop_ref, s32[512]{0:T(512)S(1)} %copy-done.1, bf16[512,1024]{1,0:T(8,128)(2,1)S(1)} %copy-done, ...), custom_call_target="tpu_custom_call" | custom-call | flops 1000000000 | bytes 1048576 | tf_op jit(solution)/shard_map/pallas_call | solution.py:353
  43.2 0.0 collective-permute-done.3.even_ref
  43.3 0.9 %shard_map.81 = (bf16[512,1024]{1,0:T(8,128)(2,1)}, f32[256,128]{1,0:T(8,128)S(1)}) custom-call(s32[2]{0:T(128)S(1)} %pad_add_fusion.1.spot_ref, s32[1]{0:T(128)S(6)} %copy.11.hop_ref, s32[512]{0:T(512)S(1)} %copy-done.1, bf16[512,1024]{1,0:T(8,128)(2,1)S(1)} %copy-done, ...), custom_call_target="tpu_custom_call", output_to_operand_aliasing={{0}: (13, {})} | custom-call | flops 1000000000 | bytes 1048576 | tf_op jit(solution)/shard_map/pallas_call | solution.py:353
  44.2 30.9 %all_to_all.11 = f32[256,1,128]{2,1,0:T(1,128)S(1)} all-to-all(f32[256,1,128]{2,1,0:T(1,128)S(1)} %bitcast.12), channel_id=1, replica_groups=mesh['seq_0'=4,'seq_1'=8,'seq_2'=2,'head'=4] {'seq_0','seq_1','seq_2','h..., dimensions={0} | all-to-all | bytes 262144 | tf_op jit(solution)/shard_map/all_to_all | solution.py:459
  75.1 0.7 shard_map.82
  (8 shorter events, 0.0 us)
Async XLA Ops:
  0.6 30.9 %copy-start.1 = (s32[512]{0:T(512)S(1)}, s32[512]{0:T(512)}, u32[]{:S(2)}) copy-start(s32[512]{0:T(512)} %doc_ref.9) | copy-start | bytes 6148
  0.6 30.9 %copy-start = (bf16[512,1024]{1,0:T(8,128)(2,1)S(1)}, bf16[512,1024]{1,0:T(8,128)(2,1)}, u32[]{:S(2)}) copy-start(bf16[512,1024]{1,0:T(8,128)(2,1)} %q_ref.9) | copy-start | bytes 3145732
  2.6 13.8 %collective-permute-start = (bf16[2,512,256]{2,1,0:T(8,128)(2,1)}, bf16[2,512,256]{2,1,0:T(8,128)(2,1)}, u32[]{:S(2)}, u32[]{:S(2)}) collective-permute-start(bf16[2,512,256]{2,1,0:T(8,128)(2,1)} %pad_add_fusion.own_ref), channel_id=1, source_target_pairs={{4,12},{12,20},{20,28},{28,36},{36,44},{44,52},{52,60},{60,68},{68... | collective-permute-start | bytes 1572872 | tf_op jit(solution)/shard_map/ppermute | solution.py:390
  7.8 14.0 %collective-permute-start.2 = (bf16[2,512,256]{2,1,0:T(8,128)(2,1)}, bf16[2,512,256]{2,1,0:T(8,128)(2,1)S(1)}, u32[]{:S(2)}, u32[]{:S(2)}) collective-permute-start(bf16[2,512,256]{2,1,0:T(8,128)(2,1)} %pad_add_fusion.own_ref), channel_id=1, source_target_pairs={{0,8},{8,16},{16,24},{24,32},{32,40},{40,48},{48,56},{56,64},{64,7... | collective-permute-start | bytes 1572872 | tf_op jit(solution)/shard_map/ppermute | solution.py:390
  16.4 10.4 %collective-permute-start.1 = (bf16[2,512,256]{2,1,0:T(8,128)(2,1)}, bf16[2,512,256]{2,1,0:T(8,128)(2,1)S(1)}, u32[]{:S(2)}, u32[]{:S(2)}) collective-permute-start(bf16[2,512,256]{2,1,0:T(8,128)(2,1)} %collective-permute-done), channel_id=1, source_target_pairs={{4,12},{12,20},{20,28},{28,36},{36,44},{44,52},{52,60},{60,68},{68... | collective-permute-start | bytes 1572872 | tf_op jit(solution)/shard_map/ppermute | solution.py:390
  20.4 14.5 %collective-permute-start.5 = (bf16[2,512,256]{2,1,0:T(8,128)(2,1)}, bf16[2,512,256]{2,1,0:T(8,128)(2,1)S(1)}, u32[]{:S(2)}, u32[]{:S(2)}) collective-permute-start(bf16[2,512,256]{2,1,0:T(8,128)(2,1)} %pad_add_fusion.own_ref), channel_id=1, source_target_pairs={{0,4},{1,5},{2,6},{3,7},{8,12},{9,13},{10,14},{11,15},{16,20},{17,... | collective-permute-start | bytes 1572872 | tf_op jit(solution)/shard_map/ppermute | solution.py:394
  21.7 0.8 %copy-start.3 = (bf16[2,512,256]{2,1,0:T(8,128)(2,1)}, bf16[2,512,256]{2,1,0:T(8,128)(2,1)S(1)}, u32[]{:S(2)}) copy-start(bf16[2,512,256]{2,1,0:T(8,128)(2,1)S(1)} %collective-permute-done.2) | copy-start | bytes 1572868
  23.7 16.7 %collective-permute-start.6 = (bf16[2,512,256]{2,1,0:T(8,128)(2,1)S(1)}, bf16[2,512,256]{2,1,0:T(8,128)(2,1)S(1)}, u32[]{:S(2)}, u32[]{:S(2)}) collective-permute-start(bf16[2,512,256]{2,1,0:T(8,128)(2,1)S(1)} %add.19.far_ref), channel_id=1, source_target_pairs={{0,4},{4,0},{1,5},{5,1},{2,6},{6,2},{3,7},{7,3},{8,12},{12,8},{9,1... | collective-permute-start | bytes 1572872 | tf_op jit(solution)/shard_map/ppermute | solution.py:394
  25.0 18.3 %collective-permute-start.3 = (bf16[2,512,256]{2,1,0:T(8,128)(2,1)}, bf16[2,512,256]{2,1,0:T(8,128)(2,1)S(1)}, u32[]{:S(2)}, u32[]{:S(2)}) collective-permute-start(bf16[2,512,256]{2,1,0:T(8,128)(2,1)} %copy-done.3), channel_id=1, source_target_pairs={{0,8},{8,16},{16,24},{24,32},{32,40},{40,48},{48,56},{56,64},{64,7... | collective-permute-start | bytes 1572872 | tf_op jit(solution)/shard_map/ppermute | solution.py:390
  26.8 16.4 %collective-permute-start.4 = (bf16[2,512,256]{2,1,0:T(8,128)(2,1)S(1)}, bf16[2,512,256]{2,1,0:T(8,128)(2,1)S(1)}, u32[]{:S(2)}, u32[]{:S(2)}) collective-permute-start(bf16[2,512,256]{2,1,0:T(8,128)(2,1)S(1)} %collective-permute-done.1.odd_ref), channel_id=1, source_target_pairs={{4,0},{5,1},{6,2},{7,3},{12,8},{13,9},{14,10},{15,11},{20,16},{21,... | collective-permute-start | bytes 1572872 | tf_op jit(solution)/shard_map/ppermute | solution.py:394
  34.9 4.2 %copy-start.2 = (s32[512]{0:T(512)S(1)}, s32[512]{0:T(512)}, u32[]{:S(2)}) copy-start(s32[512]{0:T(512)} %param.11) | copy-start | bytes 6148
